TPU v7x, 32 devices: a whole 2x2x4 slice. The times are simulated.
32 devices in a mesh: dp: 8 (over z, core), expert: 4 (over y, x).
Axes of the slice: x: 2, y: 2, z: 4, core: 2. Of those that a mesh axis runs over, the one named last changes fastest.
Arguments:
- tokens: bfloat16 [2048, 4, 1536], P('dp', 'expert'), may hold values from -6 to 6
- route_ids: int32 [4, 2048, 2], P('expert', 'dp'), may hold values from 0 to 7, all different within a row; in each aligned block of 256 rows (0 to 255, 256 to 511, ..., all dimensions but the last counted through in order) at most 96 rows name the same one
- router: bfloat16 [4, 1536, 8], P('expert'), may hold values from -0.15625 to 0.15625
- norm_gain: float32 [4, 1536], P('expert'), may hold values from 0.5 to 1.5
- w_in: bfloat16 [4, 8, 1536, 768], P('expert', 'dp'), may hold values from -0.15625 to 0.15625
- w_out: bfloat16 [4, 8, 768, 1536], P('expert', 'dp'), may hold values from -0.21875 to 0.21875
- cotangent: bfloat16 [2048, 4, 1536], P('dp', 'expert'), may hold values from -6 to 6
Outputs:
- normed_out: bfloat16 [2048, 4, 1536], P('dp', 'expert')
- grad_tokens: bfloat16 [2048, 4, 1536], P('dp', 'expert')
- grad_router: float32 [4, 1536, 8], P('expert')
- grad_gain: float32 [4, 1536], P('expert')
- grad_w_in: bfloat16 [4, 8, 1536, 768], P('expert', 'dp')
- grad_w_out: bfloat16 [4, 8, 768, 1536], P('expert', 'dp')
Inputs may be any that keep to these rules, and one draw needn't show every extreme that they name: `route_ids`: the two ids of a row differ. Among the rows of one device (one mixed token, 256 samples, two choices each) no expert is named more than 96 times.
All inputs are finite; a program needn't handle non-finite values.
Results may differ from a plain program's by a relative error of at most 0.015.
Values may be sent and summed in bfloat16 or wider, within the bound.
No kernel may reach another device: no remote copies, remote signals or barrier semaphores. Data moves between devices by JAX's collectives and lax.ppermute only.
A program may use at most 64 MiB of HBM per device.

v0:
```python
import jax
import jax.numpy as jnp
from jax import lax
from jax.sharding import PartitionSpec as P

gelu_coef = 0.7978845608028654
cubic_coef = 0.044715
norm_eps = 1e-05


def gelu_tanh(value):
    inner = gelu_coef * (value + cubic_coef * value * value * value)
    return 0.5 * value * (1.0 + jnp.tanh(inner))


def gelu_slope(value):
    inner = gelu_coef * (value + cubic_coef * value * value * value)
    tangent = jnp.tanh(inner)
    return 0.5 * (1.0 + tangent) + 0.5 * value * (1.0 - tangent * tangent) * gelu_coef * (
        1.0 + 3.0 * cubic_coef * value * value
    )


def send_back(result):
    return lax.all_to_all(result, "dp", split_axis=0, concat_axis=0, tiled=True)


def pick_rows(hot, rows):
    return lax.dot_general(hot, rows, (((0,), (0,)), ((), ())), preferred_element_type=jnp.float32)


def body(tokens, route_ids, router, norm_gain, w_in, w_out, cotangent):
    row_count = tokens.shape[0]
    model_width = tokens.shape[2]
    experts = lax.axis_size("dp")
    slot_depth = 3 * row_count // experts
    slot_rows = experts * slot_depth
    weight_in = w_in[0, 0]
    weight_out = w_out[0, 0]
    hidden = weight_in.shape[1]
    router_row = router[0]
    gain_row = norm_gain[0]
    own_rows = tokens.reshape(row_count, model_width)
    mixed_rows = lax.all_to_all(own_rows, "expert", split_axis=1, concat_axis=1, tiled=True)
    route_rows = route_ids.reshape(row_count, 2)
    labels = lax.broadcasted_iota(jnp.int32, (row_count, 2, experts), 2)
    chosen = (route_rows[:, :, None] == labels).astype(jnp.int32)
    flat_hot = chosen.reshape(row_count * 2, experts)
    before = jnp.cumsum(flat_hot, axis=0, dtype=jnp.int32) - flat_hot
    slot_place = jnp.sum(before * flat_hot, axis=1, dtype=jnp.int32).reshape(row_count, 2)
    target = route_rows * slot_depth + slot_place
    slot_index = lax.broadcasted_iota(jnp.int32, (slot_rows, row_count), 0)
    first_pick = target[None, :, 0] == slot_index
    second_pick = target[None, :, 1] == slot_index
    placer = jnp.logical_or(first_pick, second_pick).astype(jnp.bfloat16)
    first_hot = first_pick.astype(jnp.bfloat16)
    second_hot = second_pick.astype(jnp.bfloat16)
    chosen_f = chosen.astype(jnp.float32)
    logits = jnp.dot(mixed_rows, router_row, preferred_element_type=jnp.float32)
    picked = jnp.sum(logits[:, None, :] * chosen_f, axis=2)
    gate_value = jax.nn.sigmoid(picked)
    outgoing = jnp.dot(placer, mixed_rows, preferred_element_type=jnp.float32).astype(jnp.bfloat16)
    outgoing = outgoing.reshape(experts, slot_depth, model_width)

    def expert_rows(expert_input):
        pre_act = jnp.dot(expert_input, weight_in, preferred_element_type=jnp.float32)
        act_values = gelu_tanh(pre_act).astype(jnp.bfloat16)
        return (pre_act, act_values)

    received = lax.all_to_all(outgoing, "dp", split_axis=0, concat_axis=0, tiled=True)
    item_count = received.shape[1]
    expert_input = received.reshape(experts * item_count, model_width)
    pre_act, act_values = expert_rows(expert_input)
    result = jnp.dot(act_values, weight_out, preferred_element_type=jnp.float32).astype(
        jnp.bfloat16
    )
    mapped = send_back(result.reshape(experts, item_count, model_width))
    returned_rows = mapped.reshape(slot_rows, model_width)
    first_out = pick_rows(first_hot, returned_rows)
    second_out = pick_rows(second_hot, returned_rows)
    expert_sum = gate_value[:, 0:1] * first_out + gate_value[:, 1:2] * second_out
    residual = mixed_rows.astype(jnp.float32) + expert_sum
    row_mean = jnp.mean(residual, axis=1, keepdims=True)
    centered = residual - row_mean
    row_var = jnp.mean(centered * centered, axis=1, keepdims=True)
    inv_std = lax.rsqrt(row_var + norm_eps)
    normed = centered * inv_std
    normed_out = (normed * gain_row[None, :]).astype(jnp.bfloat16)
    cot_f = cotangent.reshape(row_count, model_width).astype(jnp.float32)
    grad_gain = jnp.sum(cot_f * normed, axis=0)
    grad_normed = cot_f * gain_row[None, :]
    grad_resid = inv_std * (
        grad_normed
        - jnp.mean(grad_normed, axis=1, keepdims=True)
        - normed * jnp.mean(grad_normed * normed, axis=1, keepdims=True)
    )
    grad_rounded = grad_resid.astype(jnp.bfloat16)
    first_grad = jnp.sum(grad_resid * first_out, axis=1)
    second_grad = jnp.sum(grad_resid * second_out, axis=1)
    grad_gate = jnp.stack([first_grad, second_grad], axis=1)
    grad_logit = grad_gate * gate_value * (1.0 - gate_value)
    route_grad = jnp.sum(grad_logit[:, :, None] * chosen_f, axis=1)
    selected = jnp.dot(placer, grad_rounded, preferred_element_type=jnp.float32)
    slot_gate = jnp.sum(
        jnp.where(first_pick, gate_value[None, :, 0], 0.0)
        + jnp.where(second_pick, gate_value[None, :, 1], 0.0),
        axis=1,
    )
    grad_send = (
        (slot_gate[:, None] * selected)
        .astype(jnp.bfloat16)
        .reshape(experts, slot_depth, model_width)
    )
    both_arrived = (
        lax.all_to_all(outgoing, "dp", split_axis=0, concat_axis=0, tiled=True),
        lax.all_to_all(grad_send, "dp", split_axis=0, concat_axis=0, tiled=True),
    )
    input_rows = both_arrived[0].reshape(slot_rows, model_width)
    grad_arrived = both_arrived[1]
    pre_rows, act_rows = expert_rows(input_rows)
    grad_out_rows = grad_arrived.reshape(slot_rows, model_width)
    grad_act = lax.dot_general(
        grad_out_rows, weight_out, (((1,), (1,)), ((), ())), preferred_element_type=jnp.float32
    )
    grad_pre = (grad_act * gelu_slope(pre_rows)).astype(jnp.bfloat16)
    grad_w_out = pick_rows(act_rows, grad_out_rows).astype(jnp.bfloat16)
    grad_w_in = pick_rows(input_rows, grad_pre).astype(jnp.bfloat16)
    grad_input = lax.dot_general(
        grad_pre, weight_in, (((1,), (1,)), ((), ())), preferred_element_type=jnp.float32
    ).astype(jnp.bfloat16)
    grad_back = lax.all_to_all(
        grad_input.reshape(experts, slot_depth, model_width),
        "dp",
        split_axis=0,
        concat_axis=0,
        tiled=True,
    )
    grad_back_rows = grad_back.reshape(slot_rows, model_width)
    first_input = pick_rows(first_hot, grad_back_rows)
    second_input = pick_rows(second_hot, grad_back_rows)
    router_f = router_row.astype(jnp.float32)
    grad_mixed = (
        grad_resid
        + first_input
        + second_input
        + jnp.dot(route_grad, router_f.T, precision=lax.Precision.HIGHEST)
    )
    router_part = jnp.dot(
        mixed_rows.astype(jnp.float32).T, route_grad, precision=lax.Precision.HIGHEST
    )
    grad_router, grad_gain_sum = (
        lax.psum(router_part.astype(jnp.bfloat16), "dp").astype(jnp.float32),
        lax.psum(grad_gain.astype(jnp.bfloat16), "dp").astype(jnp.float32),
    )
    grad_tokens = lax.all_to_all(
        grad_mixed.astype(jnp.bfloat16), "expert", split_axis=1, concat_axis=1, tiled=True
    )
    return (
        normed_out.reshape(row_count, 1, model_width),
        grad_tokens.reshape(row_count, 1, model_width),
        grad_router.reshape(1, model_width, experts),
        grad_gain_sum.reshape(1, model_width),
        grad_w_in.reshape(1, 1, model_width, hidden),
        grad_w_out.reshape(1, 1, hidden, model_width),
    )


def solution(mesh):
    return jax.shard_map(
        body,
        mesh=mesh,
        in_specs=(
            P("dp", "expert", None),
            P("expert", "dp", None),
            P("expert", None, None),
            P("expert", None),
            P("expert", "dp", None, None),
            P("expert", "dp", None, None),
            P("dp", "expert", None),
        ),
        out_specs=(
            P("dp", "expert", None),
            P("dp", "expert", None),
            P("expert", None, None),
            P("expert", None),
            P("expert", "dp", None, None),
            P("expert", "dp", None, None),
        ),
        check_vma=False,
    )
```

profile of v0, /device:TPU:0, one launch (start us, length us, event | category | flops | bytes accessed | tf_op | source)
XLA Modules:
  0.0 319.4 jit_solution(5962816775856016783)
XLA Ops:
  0.7 1.6 copy.43
  2.2 1.2 copy.44
  3.4 5.2 %all-to-all-start = ((bf16[256,4,384]{2,0,1:T(8,128)(2,1)}), bf16[256,4,384]{2,0,1:T(8,128)(2,1)S(1)}, u32[]{:S(2)}, u32[]{:S(2)}) async-start(bf16[256,4,384]{2,0,1:T(8,128)(2,1)} %copy.44), calls=%async_computation | async-start | bytes 1572864 | tf_op jit(solution)/shard_map/all_to_all | solution.py:44
  8.6 0.1 copy.46
  8.7 0.1 eq.51
  8.9 0.1 eq.48
  9.0 1.1 reduce-window.6
  10.2 0.2 slice_reduce_fusion.2
  10.4 0.1 fusion.45
  10.5 0.1 reshape.146
  10.7 0.2 slice_reduce_fusion.1
  10.9 8.5 %all-to-all-done = bf16[256,4,384]{2,0,1:T(8,128)(2,1)S(1)} async-done(((bf16[256,4,384]{2,0,1:T(8,128)(2,1)}), bf16[256,4,384]{2,0,1:T(8,128)(2,1)S(1)}, u32[]{:S(2)}, u32[]{:S(2)}) %all-to-all-start) | async-done | bytes 786464 | tf_op jit(solution)/shard_map/all_to_all | solution.py:44
  19.4 0.9 copy-done.3
  20.3 1.2 copy.54
  21.5 0.8 convolution_convert_fusion.4
  22.3 59.5 %all_to_all.42 = bf16[8,96,1536]{2,1,0:T(8,128)(2,1)S(1)} all-to-all(bf16[8,96,1536]{2,1,0:T(8,128)(2,1)S(1)} %bitcast.84), channel_id=1, replica_groups=mesh['dp'=8,'expert'=4] {'dp'}, dimensions={0} | all-to-all | bytes 4718592 | tf_op jit(solution)/shard_map/all_to_all | solution.py:70
  81.8 1.4 copy-done.4
  83.2 2.0 fusion.14
  85.2 3.6 %convolution_convert_fusion.3 = bf16[768,1536]{1,0:T(8,128)(2,1)} fusion(bf16[1,1,768,1536]{3,2,1,0:T(8,128)(2,1)S(1)} %copy-done, f32[768,768]{1,0:T(8,128)S(1)} %fusion.14), kind=kOutput, calls=%fused_computation.6 | convolution fusion | flops 1818427392 | bytes 7077888 | tf_op jit(solution)/shard_map/dot_general | solution.py:74
  88.7 4.5 %all-to-all-start.2 = ((bf16[8,96,1536]{2,1,0:T(8,128)(2,1)}), bf16[8,96,1536]{2,1,0:T(8,128)(2,1)}, u32[]{:S(2)}, u32[]{:S(2)}) async-start(bf16[8,96,1536]{2,1,0:T(8,128)(2,1)} %bitcast.96), calls=%async_computation.2 | async-start | bytes 4718592 | tf_op jit(solution)/shard_map/all_to_all | solution.py:25
  93.3 0.1 copy.47
  93.4 0.3 fusion.42
  93.7 0.2 add_reduce_fusion
  94.0 53.9 %all-to-all-done.2 = bf16[8,96,1536]{2,1,0:T(8,128)(2,1)} async-done(((bf16[8,96,1536]{2,1,0:T(8,128)(2,1)}), bf16[8,96,1536]{2,1,0:T(8,128)(2,1)}, u32[]{:S(2)}, u32[]{:S(2)}) %all-to-all-start.2) | async-done | bytes 2359328 | tf_op jit(solution)/shard_map/all_to_all | solution.py:25
  147.9 2.5 fusion.30
  150.4 2.8 fusion.49
  153.2 0.3 multiply_reduce_fusion.2
  153.5 0.7 fusion.23
  154.2 1.7 multiply_reduce_fusion.1
  155.9 0.8 multiply_convert_fusion
  156.7 57.2 %all_to_all.43 = bf16[8,96,1536]{2,1,0:T(8,128)(2,1)S(1)} all-to-all(bf16[8,96,1536]{2,1,0:T(8,128)(2,1)S(1)} %bitcast.83), channel_id=1, replica_groups=mesh['dp'=8,'expert'=4] {'dp'}, dimensions={0} | all-to-all | bytes 4718592 | tf_op jit(solution)/shard_map/all_to_all | solution.py:116
  213.9 2.9 fusion.9
  216.9 3.4 %convolution_convert_fusion.2 = bf16[768,1536]{1,0:T(8,128)(2,1)} fusion(bf16[768,768]{1,0:T(8,128)(2,1)S(1)} %fusion.9, bf16[1,1,1536,768]{3,2,1,0:T(8,128)(2,1)S(1)} %copy-done.11), kind=kOutput, calls=%fused_computation.5 | convolution fusion | flops 1813118976 | bytes 5898240 | tf_op jit(solution)/shard_map/dot_general | solution.py:128
  220.3 4.4 %all-to-all-start.4 = ((bf16[8,96,1536]{2,1,0:T(8,128)(2,1)}), bf16[8,96,1536]{2,1,0:T(8,128)(2,1)}, u32[]{:S(2)}, u32[]{:S(2)}) async-start(bf16[8,96,1536]{2,1,0:T(8,128)(2,1)} %bitcast.95), calls=%async_computation.4 | async-start | bytes 4718592 | tf_op jit(solution)/shard_map/all_to_all | solution.py:131
  224.7 0.4 fusion.16
  225.2 68.8 %all-reduce = (bf16[1,1536,8]{1,2,0:T(8,128)(2,1)S(1)}, bf16[1,1536]{1,0:T(2,128)(2,1)S(1)}) all-reduce(bf16[1,1536,8]{1,2,0:T(8,128)(2,1)S(1)} %fusion.16, bf16[1,1536]{1,0:T(2,128)(2,1)S(1)} %reshape.159), channel_id=1, replica_groups=mesh['dp'=8,'expert'=4] {'dp'}, use_global_device_ids=true, to_apply=%region_12.13 | all-reduce | flops 13824 | bytes 55296 | tf_op jit(solution)/shard_map/psum | solution.py:152
  293.9 0.6 reshape.160
  294.5 0.6 reshape.158
  295.2 2.9 convolution_add_fusion.2
  298.1 2.5 convolution_add_fusion.1
  300.6 0.9 fusion.2
  301.5 1.0 copy.56
  302.5 3.5 %all-to-all-start.5 = ((bf16[256,4,384]{2,0,1:T(8,128)(2,1)}), bf16[256,4,384]{2,0,1:T(8,128)(2,1)S(1)}, u32[]{:S(2)}, u32[]{:S(2)}) async-start(bf16[256,4,384]{2,0,1:T(8,128)(2,1)} %bitcast.87), calls=%async_computation.5 | async-start | bytes 1572864 | tf_op jit(solution)/shard_map/all_to_all | solution.py:155
  306.0 5.6 %fusion = bf16[1,1,1536,768]{3,2,1,0:T(8,128)(2,1)} fusion(bf16[768,1536]{1,0:T(8,128)(2,1)} %bitcast.92, bf16[768,768]{1,0:T(8,128)(2,1)} %copy-done.15), kind=kOutput, calls=%fused_computation.8 | convolution fusion | flops 1813118976 | bytes 5898240 | tf_op jit(solution)/shard_map/dot_general | solution.py:29
  311.6 3.6 %fusion.1 = bf16[1,1,768,1536]{3,2,1,0:T(8,128)(2,1)} fusion(bf16[768,1536]{1,0:T(8,128)(2,1)S(1)} %bitcast.94, f32[768,768]{1,0:T(8,128)S(1)} %copy-done.14), kind=kOutput, calls=%fused_computation.9 | convolution fusion | flops 1818427392 | bytes 7077888 | tf_op jit(solution)/shard_map/dot_general | solution.py:29
  315.1 0.8 all-to-all-done.5
  316.0 1.2 copy.51
  317.1 2.3 copy.52
  (45 shorter events, 0.3 us)
Async XLA Ops:
  0.6 84.5 %copy-start = (bf16[1,1,768,1536]{3,2,1,0:T(8,128)(2,1)S(1)}, bf16[1,1,768,1536]{3,2,1,0:T(8,128)(2,1)}, u32[]{:S(2)}) copy-start(bf16[1,1,768,1536]{3,2,1,0:T(8,128)(2,1)} %param.12) | copy-start | bytes 7077892
  0.6 7.9 %copy-start.9 = (s32[1,256,2]{1,2,0:T(2,128)S(1)}, s32[1,256,2]{1,2,0:T(2,128)}, u32[]{:S(2)}) copy-start(s32[1,256,2]{1,2,0:T(2,128)} %param.8) | copy-start | bytes 6148
  3.4 16.0 %all-to-all-start = ((bf16[256,4,384]{2,0,1:T(8,128)(2,1)}), bf16[256,4,384]{2,0,1:T(8,128)(2,1)S(1)}, u32[]{:S(2)}, u32[]{:S(2)}) async-start(bf16[256,4,384]{2,0,1:T(8,128)(2,1)} %copy.44), calls=%async_computation | async-start | bytes 1572864 | tf_op jit(solution)/shard_map/all_to_all | solution.py:44
  19.4 0.9 copy-start.3
  22.3 60.9 %copy-start.10 = (bf16[1,1,1536,768]{3,2,1,0:T(8,128)(2,1)S(1)}, bf16[1,1,1536,768]{3,2,1,0:T(8,128)(2,1)}, u32[]{:S(2)}) copy-start(bf16[1,1,1536,768]{3,2,1,0:T(8,128)(2,1)} %param.11) | copy-start | bytes 7077892
  81.8 1.4 copy-start.4
  85.2 3.6 %copy-start.12 = (f32[768,768]{1,0:T(8,128)}, f32[768,768]{1,0:T(8,128)S(1)}, u32[]{:S(2)}) copy-start(f32[768,768]{1,0:T(8,128)S(1)} %fusion.14) | copy-start | bytes 7077892
  88.7 4.6 %copy-start.8 = (f32[1,1536]{1,0:T(1,128)S(1)}, f32[1,1536]{1,0:T(1,128)}, u32[]{:S(2)}) copy-start(f32[1,1536]{1,0:T(1,128)} %param.10) | copy-start | bytes 18436
  88.7 4.6 %copy-start.7 = (bf16[1,1536,8]{1,2,0:T(8,128)(2,1)S(1)}, bf16[1,1536,8]{1,2,0:T(8,128)(2,1)}, u32[]{:S(2)}) copy-start(bf16[1,1536,8]{1,2,0:T(8,128)(2,1)} %param.9) | copy-start | bytes 73732
  88.7 59.2 %all-to-all-start.2 = ((bf16[8,96,1536]{2,1,0:T(8,128)(2,1)}), bf16[8,96,1536]{2,1,0:T(8,128)(2,1)}, u32[]{:S(2)}, u32[]{:S(2)}) async-start(bf16[8,96,1536]{2,1,0:T(8,128)(2,1)} %bitcast.96), calls=%async_computation.2 | async-start | bytes 4718592 | tf_op jit(solution)/shard_map/all_to_all | solution.py:25
  150.4 3.1 copy-start.2
  155.9 58.0 %copy-start.1 = (f32[256,1536]{1,0:T(8,128)}, f32[256,1536]{1,0:T(8,128)S(1)}, u32[]{:S(2)}) copy-start(f32[256,1536]{1,0:T(8,128)S(1)} %get-tuple-element.27) | copy-start | bytes 4718596
  156.7 57.2 %copy-start.13 = (f32[768,768]{1,0:T(8,128)S(1)}, f32[768,768]{1,0:T(8,128)}, u32[]{:S(2)}) copy-start(f32[768,768]{1,0:T(8,128)} %copy-done.12) | copy-start | bytes 7077892
  213.9 2.9 copy-start.5
  213.9 2.9 copy-start.11
  216.9 3.4 %copy-start.15 = (bf16[768,768]{1,0:T(8,128)(2,1)}, bf16[768,768]{1,0:T(8,128)(2,1)S(1)}, u32[]{:S(2)}) copy-start(bf16[768,768]{1,0:T(8,128)(2,1)S(1)} %fusion.9) | copy-start | bytes 3538948
  220.3 74.9 %all-to-all-start.4 = ((bf16[8,96,1536]{2,1,0:T(8,128)(2,1)}), bf16[8,96,1536]{2,1,0:T(8,128)(2,1)}, u32[]{:S(2)}, u32[]{:S(2)}) async-start(bf16[8,96,1536]{2,1,0:T(8,128)(2,1)} %bitcast.95), calls=%async_computation.4 | async-start | bytes 4718592 | tf_op jit(solution)/shard_map/all_to_all | solution.py:131
  302.5 13.5 %all-to-all-start.5 = ((bf16[256,4,384]{2,0,1:T(8,128)(2,1)}), bf16[256,4,384]{2,0,1:T(8,128)(2,1)S(1)}, u32[]{:S(2)}, u32[]{:S(2)}) async-start(bf16[256,4,384]{2,0,1:T(8,128)(2,1)} %bitcast.87), calls=%async_computation.5 | async-start | bytes 1572864 | tf_op jit(solution)/shard_map/all_to_all | solution.py:155
  306.0 5.6 %copy-start.6 = (bf16[8,96,1536]{2,1,0:T(8,128)(2,1)S(1)}, bf16[8,96,1536]{2,1,0:T(8,128)(2,1)}, u32[]{:S(2)}) copy-start(bf16[8,96,1536]{2,1,0:T(8,128)(2,1)} %copy-done.5) | copy-start | bytes 7077892
  306.0 5.6 %copy-start.14 = (f32[768,768]{1,0:T(8,128)S(1)}, f32[768,768]{1,0:T(8,128)}, u32[]{:S(2)}) copy-start(f32[768,768]{1,0:T(8,128)} %copy-done.12) | copy-start | bytes 7077892
where the time goes:
time: 320 us; the launch traced here: 319 us
  blocking collectives  186 us (58%)
  waiting for transfers between devices  63.2 us (20%)
  matrix products  34.8 us (11%)
  starting transfers between devices  17.6 us (6%)
  local copies, waits for them, and re-layouts  11.7 us (4%)
  other arithmetic  5.54 us (2%)
    psum x1, blocking collectives, body(): lax.psum(router_part.astype(jnp.bfloat16), 'dp').astype(jnp.float32)  68.8 us
    all_to_all x1, blocking collectives, body(): lax.all_to_all(outgoing, 'dp', split_axis=0, concat_axis=0, tiled=True)  59.5 us
    all_to_all x1, blocking collectives, body(): lax.all_to_all(grad_send, 'dp', split_axis=0, concat_axis=0, tiled=True)  57.2 us
    all_to_all x1, waiting for transfers between devices, send_back(): return lax.all_to_all(result, 'dp', split_axis=0, concat_axis=0, tiled=True)  53.9 us
    dot_general x6, matrix products, pick_rows(): lax.dot_general(hot, rows, (((0,), (0,)), ((), ())), preferred_element_ty...  19.8 us
    all_to_all x1, waiting for transfers between devices, body(): lax.all_to_all(own_rows, 'expert', split_axis=1, concat_axis=1, tiled=True)  8.51 us
  transfers between devices with their start and end apart: 4, of which 3 were waited for; matrix products, arithmetic and copies ran while one was open for 4% of the time, Pallas kernels for 0%

commit v1 on v0

v1 whole, which is shorter than its diff:
```python
import jax
import jax.numpy as jnp
from jax import lax
from jax.sharding import PartitionSpec as P

gelu_coef = 0.7978845608028654
cubic_coef = 0.044715
norm_eps = 1e-05
CHUNKS = 2


def gelu_tanh(value):
    inner = gelu_coef * (value + cubic_coef * value * value * value)
    return 0.5 * value * (1.0 + jnp.tanh(inner))


def gelu_slope(value):
    inner = gelu_coef * (value + cubic_coef * value * value * value)
    tangent = jnp.tanh(inner)
    return 0.5 * (1.0 + tangent) + 0.5 * value * (1.0 - tangent * tangent) * gelu_coef * (
        1.0 + 3.0 * cubic_coef * value * value
    )


def exchange(blocks):
    return lax.all_to_all(blocks, "dp", split_axis=0, concat_axis=0, tiled=True)


def dot(a, b, dims):
    return lax.dot_general(a, b, (dims, ((), ())), preferred_element_type=jnp.float32)


def body(tokens, route_ids, router, norm_gain, w_in, w_out, cotangent):
    row_count = tokens.shape[0]
    model_width = tokens.shape[2]
    experts = lax.axis_size("dp")
    slot_depth = 3 * row_count // experts
    part = slot_depth // CHUNKS
    part_rows = experts * part
    weight_in = w_in[0, 0]
    weight_out = w_out[0, 0]
    hidden = weight_in.shape[1]
    router_row = router[0]
    gain_row = norm_gain[0]
    me = lax.axis_index("dp")
    own_rows = tokens.reshape(row_count, model_width)
    mixed_rows = lax.all_to_all(own_rows, "expert", split_axis=1, concat_axis=1, tiled=True)
    route_rows = route_ids.reshape(row_count, 2)
    labels = lax.broadcasted_iota(jnp.int32, (row_count, 2, experts), 2)
    chosen = (route_rows[:, :, None] == labels).astype(jnp.int32)
    flat_hot = chosen.reshape(row_count * 2, experts)
    before = jnp.cumsum(flat_hot, axis=0, dtype=jnp.int32) - flat_hot
    slot_place = jnp.sum(before * flat_hot, axis=1, dtype=jnp.int32).reshape(row_count, 2)
    chunk_of = slot_place // part
    target = route_rows * part + slot_place - chunk_of * part
    slot_index = lax.broadcasted_iota(jnp.int32, (part_rows, row_count), 0)
    placers = []
    for c in range(CHUNKS):
        here = jnp.where(chunk_of == c, target, -1)
        placers.append(
            jnp.logical_or(here[None, :, 0] == slot_index, here[None, :, 1] == slot_index).astype(
                jnp.bfloat16
            )
        )
    my_column = lax.broadcasted_iota(jnp.int32, (1, experts), 1) == me

    def spread(placer, rows):
        picked = dot(placer, rows, ((1,), (0,))).astype(jnp.bfloat16)
        return picked.reshape(experts, part, model_width)

    arrived = [exchange(spread(p, mixed_rows)).reshape(part_rows, model_width) for p in placers]
    saved = []
    expert_sum = mixed_rows.astype(jnp.float32)
    for c in range(CHUNKS):
        rows = arrived[c]
        logits = dot(rows, router_row, ((1,), (0,)))
        gate = jax.nn.sigmoid(jnp.sum(jnp.where(my_column, logits, 0.0), axis=1, keepdims=True))
        pre_act = dot(rows, weight_in, ((1,), (0,)))
        act = gelu_tanh(pre_act).astype(jnp.bfloat16)
        out = dot(act, weight_out, ((1,), (0,)))
        result = out.astype(jnp.bfloat16)
        gated = (gate * out).astype(jnp.bfloat16)
        saved.append((rows, gate, pre_act, act, result))
        returned = exchange(gated.reshape(experts, part, model_width))
        expert_sum = expert_sum + dot(
            placers[c], returned.reshape(part_rows, model_width), ((0,), (0,))
        )
    residual = expert_sum
    row_mean = jnp.mean(residual, axis=1, keepdims=True)
    centered = residual - row_mean
    row_var = jnp.mean(centered * centered, axis=1, keepdims=True)
    inv_std = lax.rsqrt(row_var + norm_eps)
    normed = centered * inv_std
    normed_out = (normed * gain_row[None, :]).astype(jnp.bfloat16)
    cot_f = cotangent.reshape(row_count, model_width).astype(jnp.float32)
    grad_gain = jnp.sum(cot_f * normed, axis=0)
    grad_normed = cot_f * gain_row[None, :]
    grad_resid = inv_std * (
        grad_normed
        - jnp.mean(grad_normed, axis=1, keepdims=True)
        - normed * jnp.mean(grad_normed * normed, axis=1, keepdims=True)
    )
    grad_rounded = grad_resid.astype(jnp.bfloat16)

    grad_arrived = [exchange(spread(p, grad_rounded)).reshape(part_rows, model_width) for p in placers]
    router_mine = jnp.sum(jnp.where(my_column, router_row.astype(jnp.float32), 0.0), axis=1)
    grad_mixed = grad_resid
    pre_grads, out_grads, logit_grads = [], [], []
    for c in range(CHUNKS):
        rows, gate, pre_act, act, result = saved[c]
        grads = grad_arrived[c].astype(jnp.float32)
        grad_out = (gate * grads).astype(jnp.bfloat16)
        grad_gate = jnp.sum(grads * result.astype(jnp.float32), axis=1, keepdims=True)
        grad_logit = grad_gate * gate * (1.0 - gate)
        grad_act = dot(grad_out, weight_out, ((1,), (1,)))
        grad_pre = (grad_act * gelu_slope(pre_act)).astype(jnp.bfloat16)
        grad_input = dot(grad_pre, weight_in, ((1,), (1,))) + grad_logit * router_mine[None, :]
        back = exchange(grad_input.astype(jnp.bfloat16).reshape(experts, part, model_width))
        grad_mixed = grad_mixed + dot(placers[c], back.reshape(part_rows, model_width), ((0,), (0,)))
        pre_grads.append(grad_pre)
        out_grads.append(grad_out)
        logit_grads.append(grad_logit)
    all_rows = jnp.concatenate([s[0] for s in saved])
    all_act = jnp.concatenate([s[3] for s in saved])
    all_logit = jnp.concatenate(logit_grads)
    router_part = jnp.sum(all_rows.astype(jnp.float32) * all_logit, axis=0)
    lanes = 128
    small = jnp.stack([router_part, grad_gain]).reshape(1, 2 * model_width // lanes, lanes)
    small = exchange(jnp.broadcast_to(small, (experts,) + small.shape[1:]))
    small = small.reshape(experts, 2, model_width)
    grad_router = small[:, 0].T
    grad_gain_sum = jnp.sum(small[:, 1], axis=0)
    grad_w_out = dot(all_act, jnp.concatenate(out_grads), ((0,), (0,))).astype(jnp.bfloat16)
    grad_w_in = dot(all_rows, jnp.concatenate(pre_grads), ((0,), (0,))).astype(jnp.bfloat16)
    grad_tokens = lax.all_to_all(
        grad_mixed.astype(jnp.bfloat16), "expert", split_axis=1, concat_axis=1, tiled=True
    )
    return (
        normed_out.reshape(row_count, 1, model_width),
        grad_tokens.reshape(row_count, 1, model_width),
        grad_router.reshape(1, model_width, experts),
        grad_gain_sum.reshape(1, model_width),
        grad_w_in.reshape(1, 1, model_width, hidden),
        grad_w_out.reshape(1, 1, hidden, model_width),
    )


def solution(mesh):
    return jax.shard_map(
        body,
        mesh=mesh,
        in_specs=(
            P("dp", "expert", None),
            P("expert", "dp", None),
            P("expert", None, None),
            P("expert", None),
            P("expert", "dp", None, None),
            P("expert", "dp", None, None),
            P("dp", "expert", None),
        ),
        out_specs=(
            P("dp", "expert", None),
            P("dp", "expert", None),
            P("expert", None, None),
            P("expert", None),
            P("expert", "dp", None, None),
            P("expert", "dp", None, None),
        ),
        check_vma=False,
    )
```

time: 320 us -> 332 us (1.038)
  blocking collectives: 186 us -> 0 us
  waiting for transfers between devices: 63.2 us -> 192 us
  starting transfers between devices: 17.6 us -> 46.2 us
  matrix products: 34.8 us -> 53.2 us
  local copies, waits for them, and re-layouts: 11.7 us -> 23.4 us
  other arithmetic: 5.54 us -> 14.8 us
    all_to_all x2 -> x9, waiting for transfers between devices: 53.9 us -> 183 us  [exchange(): return lax.all_to_all(blocks, 'dp', split_axis=0, concat_axis=0, tiled=True)]
    all_to_all x2 -> x0, blocking collectives: 117 us -> none  [the longest x1 59.5 us: body(): lax.all_to_all(outgoing, 'dp', split_axis=0, concat_axis=0, tiled=True)]
    psum x1 -> x0, blocking collectives: 68.8 us -> none  [body(): lax.psum(router_part.astype(jnp.bfloat16), 'dp').astype(jnp.float32)]
    all_to_all x2 -> x9, starting transfers between devices: 8.89 us -> 37.3 us  [exchange(): return lax.all_to_all(blocks, 'dp', split_axis=0, concat_axis=0, tiled=True)]
    dot_general x15 -> x20, matrix products: 34.8 us -> 53.2 us  [dot(): lax.dot_general(a, b, (dims, ((), ())), preferred_element_type=jnp.float32)]
    unnamed x35 -> x80, local copies, waits for them, and re-layouts: 6.31 us -> 12.9 us
    convert_element_type x0 -> x4, other arithmetic: none -> 6.59 us  [body(): grad_out = (gate * grads).astype(jnp.bfloat16)]
  transfers between devices with their start and end apart: 4 -> 11, of which waited for: 3 -> 10; matrix products, arithmetic and copies ran while one was open for 4% -> 20% of each run, Pallas kernels for 0% -> 0%
where the time goes in v1:
time: 332 us; the launch traced here: 331 us
  waiting for transfers between devices  192 us (58%)
  matrix products  53.2 us (16%)
  starting transfers between devices  46.2 us (14%)
  local copies, waits for them, and re-layouts  23.4 us (7%)
  other arithmetic  14.8 us (4%)
    all_to_all x9, waiting for transfers between devices, exchange(): return lax.all_to_all(blocks, 'dp', split_axis=0, concat_axis=0, tiled=True)  183 us
    dot_general x20, matrix products, dot(): lax.dot_general(a, b, (dims, ((), ())), preferred_element_type=jnp.float32)  53.2 us
    all_to_all x9, starting transfers between devices, exchange(): return lax.all_to_all(blocks, 'dp', split_axis=0, concat_axis=0, tiled=True)  37.3 us
    unnamed x80, local copies, waits for them, and re-layouts  12.9 us
    all_to_all x1, waiting for transfers between devices, body(): lax.all_to_all(own_rows, 'expert', split_axis=1, concat_axis=1, tiled=True)  8.38 us
  transfers between devices with their start and end apart: 11, of which 10 were waited for; matrix products, arithmetic and copies ran while one was open for 20% of the time, Pallas kernels for 0%

profile of v1, /device:TPU:0, one launch (start us, length us, event | category | flops | bytes accessed | tf_op | source)
XLA Modules:
  0.0 330.6 jit_solution(13498083069401665649)
XLA Ops:
  0.6 1.6 copy.24
  3.4 5.2 %all-to-all-start = ((bf16[256,4,384]{2,0,1:T(8,128)(2,1)}), bf16[256,4,384]{2,0,1:T(8,128)(2,1)S(1)}, u32[]{:S(2)}, u32[]{:S(2)}) async-start(bf16[256,4,384]{2,0,1:T(8,128)(2,1)} %copy.25), calls=%async_computation | async-start | bytes 1572864 | tf_op jit(solution)/shard_map/all_to_all | solution.py:47
  11.0 8.4 %all-to-all-done = bf16[256,4,384]{2,0,1:T(8,128)(2,1)S(1)} async-done(((bf16[256,4,384]{2,0,1:T(8,128)(2,1)}), bf16[256,4,384]{2,0,1:T(8,128)(2,1)S(1)}, u32[]{:S(2)}, u32[]{:S(2)}) %all-to-all-start) | async-done | bytes 786464 | tf_op jit(solution)/shard_map/all_to_all | solution.py:47
  21.5 1.5 convolution_convert_fusion.5
  23.0 4.9 %all-to-all-start.1 = ((bf16[8,48,1536]{2,1,0:T(8,128)(2,1)}), bf16[8,48,1536]{2,1,0:T(8,128)(2,1)}, u32[]{:S(2)}, u32[]{:S(2)}) async-start(bf16[8,48,1536]{2,1,0:T(8,128)(2,1)} %bitcast.135), calls=%async_computation.1 | async-start | bytes 2359296 | tf_op jit(solution)/shard_map/all_to_all | solution.py:26
  28.1 1.5 convolution_convert_fusion.4
  29.6 27.8 %all-to-all-done.1 = bf16[8,48,1536]{2,1,0:T(8,128)(2,1)} async-done(((bf16[8,48,1536]{2,1,0:T(8,128)(2,1)}), bf16[8,48,1536]{2,1,0:T(8,128)(2,1)}, u32[]{:S(2)}, u32[]{:S(2)}) %all-to-all-start.1) | async-done | bytes 1179680 | tf_op jit(solution)/shard_map/all_to_all | solution.py:26
  57.4 4.4 %all-to-all-start.3 = ((bf16[8,48,1536]{2,1,0:T(8,128)(2,1)}), bf16[8,48,1536]{2,1,0:T(8,128)(2,1)}, u32[]{:S(2)}, u32[]{:S(2)}) async-start(bf16[8,48,1536]{2,1,0:T(8,128)(2,1)} %bitcast.134), calls=%async_computation.3 | async-start | bytes 2359296 | tf_op jit(solution)/shard_map/all_to_all | solution.py:26
  61.8 1.7 fusion.63
  63.6 4.2 %multiply_convert_fusion.4 = (bf16[384,768]{1,0:T(8,128)(2,1)S(1)}, f32[384,768]{1,0:T(8,128)}) fusion(bf16[384,1536]{1,0:T(8,128)(2,1)} %bitcast.5, bf16[1,1,1536,768]{3,2,1,0:T(8,128)(2,1)} %param.11), kind=kOutput, calls=%fused_computation.87 | convolution fusion | flops 908623872 | bytes 5308416 | tf_op jit(solution)/shard_map/dot_general | solution.py:30
  68.6 2.5 multiply_convert_fusion.1
  71.1 20.0 %all-to-all-done.3 = bf16[8,48,1536]{2,1,0:T(8,128)(2,1)} async-done(((bf16[8,48,1536]{2,1,0:T(8,128)(2,1)}), bf16[8,48,1536]{2,1,0:T(8,128)(2,1)}, u32[]{:S(2)}, u32[]{:S(2)}) %all-to-all-start.3) | async-done | bytes 1179680 | tf_op jit(solution)/shard_map/all_to_all | solution.py:26
  91.2 4.3 %all-to-all-start.2 = ((bf16[8,48,1536]{2,1,0:T(8,128)(2,1)}), bf16[8,48,1536]{2,1,0:T(8,128)(2,1)}, u32[]{:S(2)}, u32[]{:S(2)}) async-start(bf16[8,48,1536]{2,1,0:T(8,128)(2,1)} %bitcast.143), calls=%async_computation.2 | async-start | bytes 2359296 | tf_op jit(solution)/shard_map/all_to_all | solution.py:26
  95.4 1.7 fusion.64
  97.2 4.2 %multiply_convert_fusion.3 = (bf16[384,768]{1,0:T(8,128)(2,1)S(1)}, f32[384,768]{1,0:T(8,128)}) fusion(bf16[384,1536]{1,0:T(8,128)(2,1)} %bitcast.12, bf16[1,1,1536,768]{3,2,1,0:T(8,128)(2,1)} %param.11), kind=kOutput, calls=%fused_computation.86 | convolution fusion | flops 908623872 | bytes 5308416 | tf_op jit(solution)/shard_map/dot_general | solution.py:30
  102.2 2.5 multiply_convert_fusion
  104.7 20.0 %all-to-all-done.2 = bf16[8,48,1536]{2,1,0:T(8,128)(2,1)} async-done(((bf16[8,48,1536]{2,1,0:T(8,128)(2,1)}), bf16[8,48,1536]{2,1,0:T(8,128)(2,1)}, u32[]{:S(2)}, u32[]{:S(2)}) %all-to-all-start.2) | async-done | bytes 1179680 | tf_op jit(solution)/shard_map/all_to_all | solution.py:26
  124.8 4.4 %all-to-all-start.4 = ((bf16[8,48,1536]{2,1,0:T(8,128)(2,1)}), bf16[8,48,1536]{2,1,0:T(8,128)(2,1)}, u32[]{:S(2)}, u32[]{:S(2)}) async-start(bf16[8,48,1536]{2,1,0:T(8,128)(2,1)} %bitcast.144), calls=%async_computation.4 | async-start | bytes 2359296 | tf_op jit(solution)/shard_map/all_to_all | solution.py:26
  129.2 3.0 convolution_add_fusion.5
  132.3 26.3 %all-to-all-done.4 = bf16[8,48,1536]{2,1,0:T(8,128)(2,1)} async-done(((bf16[8,48,1536]{2,1,0:T(8,128)(2,1)}), bf16[8,48,1536]{2,1,0:T(8,128)(2,1)}, u32[]{:S(2)}, u32[]{:S(2)}) %all-to-all-start.4) | async-done | bytes 1179680 | tf_op jit(solution)/shard_map/all_to_all | solution.py:26
  158.6 2.5 fusion.87
  162.9 1.5 fusion.32
  164.4 1.6 convolution_convert_fusion.3
  165.9 3.6 %all-to-all-start.5 = ((bf16[8,48,1536]{2,1,0:T(8,128)(2,1)}), bf16[8,48,1536]{2,1,0:T(8,128)(2,1)S(1)}, u32[]{:S(2)}, u32[]{:S(2)}) async-start(bf16[8,48,1536]{2,1,0:T(8,128)(2,1)} %bitcast.136), calls=%async_computation.5 | async-start | bytes 2359296 | tf_op jit(solution)/shard_map/all_to_all | solution.py:26
  169.5 2.9 convolution_convert_fusion.2
  172.4 26.4 %all-to-all-done.5 = bf16[8,48,1536]{2,1,0:T(8,128)(2,1)S(1)} async-done(((bf16[8,48,1536]{2,1,0:T(8,128)(2,1)}), bf16[8,48,1536]{2,1,0:T(8,128)(2,1)S(1)}, u32[]{:S(2)}, u32[]{:S(2)}) %all-to-all-start.5) | async-done | bytes 1179680 | tf_op jit(solution)/shard_map/all_to_all | solution.py:26
  199.9 3.7 %all-to-all-start.7 = ((bf16[8,48,1536]{2,1,0:T(8,128)(2,1)}), bf16[8,48,1536]{2,1,0:T(8,128)(2,1)S(1)}, u32[]{:S(2)}, u32[]{:S(2)}) async-start(bf16[8,48,1536]{2,1,0:T(8,128)(2,1)} %bitcast.133), calls=%async_computation.7 | async-start | bytes 2359296 | tf_op jit(solution)/shard_map/all_to_all | solution.py:26
  203.7 1.4 select_reduce_fusion
  205.8 3.3 fusion.13
  210.4 1.4 fusion.44
  212.7 2.1 fusion.2
  214.8 17.9 %all-to-all-done.7 = bf16[8,48,1536]{2,1,0:T(8,128)(2,1)S(1)} async-done(((bf16[8,48,1536]{2,1,0:T(8,128)(2,1)}), bf16[8,48,1536]{2,1,0:T(8,128)(2,1)S(1)}, u32[]{:S(2)}, u32[]{:S(2)}) %all-to-all-start.7) | async-done | bytes 1179680 | tf_op jit(solution)/shard_map/all_to_all | solution.py:26
  232.8 4.4 %all-to-all-start.6 = ((bf16[8,48,1536]{2,1,0:T(8,128)(2,1)}), bf16[8,48,1536]{2,1,0:T(8,128)(2,1)}, u32[]{:S(2)}, u32[]{:S(2)}) async-start(bf16[8,48,1536]{2,1,0:T(8,128)(2,1)} %bitcast.142), calls=%async_computation.6 | async-start | bytes 2359296 | tf_op jit(solution)/shard_map/all_to_all | solution.py:26
  237.9 2.8 fusion.10
  242.0 1.5 fusion.41
  244.4 2.1 fusion.3
  246.5 20.1 %all-to-all-done.6 = bf16[8,48,1536]{2,1,0:T(8,128)(2,1)} async-done(((bf16[8,48,1536]{2,1,0:T(8,128)(2,1)}), bf16[8,48,1536]{2,1,0:T(8,128)(2,1)}, u32[]{:S(2)}, u32[]{:S(2)}) %all-to-all-start.6) | async-done | bytes 1179680 | tf_op jit(solution)/shard_map/all_to_all | solution.py:26
  266.6 3.7 %all-to-all-start.8 = ((bf16[8,48,1536]{2,1,0:T(8,128)(2,1)}), bf16[8,48,1536]{2,1,0:T(8,128)(2,1)S(1)}, u32[]{:S(2)}, u32[]{:S(2)}) async-start(bf16[8,48,1536]{2,1,0:T(8,128)(2,1)} %bitcast.141), calls=%async_computation.8 | async-start | bytes 2359296 | tf_op jit(solution)/shard_map/all_to_all | solution.py:26
  271.0 2.2 multiply_reduce_fusion
  274.5 3.5 %convolution_add_fusion.3 = f32[256,1536]{1,0:T(8,128)} fusion(f32[256,1536]{1,0:T(8,128)} %copy-done.1, bf16[384,1536]{1,0:T(8,128)(2,1)} %bitcast.21, s32[256]{0:T(256)} %copy-done.9, s32[256]{0:T(256)} %copy-done.8), kind=kOutput, calls=%fused_computation.11 | convolution fusion | flops 302678016 | bytes 4327424 | tf_op jit(solution)/shard_map/dot_general | solution.py:30
  278.1 21.5 %all-to-all-done.8 = bf16[8,48,1536]{2,1,0:T(8,128)(2,1)S(1)} async-done(((bf16[8,48,1536]{2,1,0:T(8,128)(2,1)}), bf16[8,48,1536]{2,1,0:T(8,128)(2,1)S(1)}, u32[]{:S(2)}, u32[]{:S(2)}) %all-to-all-start.8) | async-done | bytes 1179680 | tf_op jit(solution)/shard_map/all_to_all | solution.py:26
  300.2 4.0 %all-to-all-start.10 = ((f32[8,24,128]{2,1,0:T(8,128)}), f32[8,24,128]{2,1,0:T(8,128)}, u32[]{:S(2)}, u32[]{:S(2)}) async-start(f32[8,24,128]{2,1,0:T(8,128)} %broadcast_in_dim.53), calls=%async_computation.10 | async-start | bytes 196608 | tf_op jit(solution)/shard_map/all_to_all | solution.py:26
  304.2 2.0 fusion.4
  307.2 3.3 %all-to-all-done.10 = f32[8,24,128]{2,1,0:T(8,128)} async-done(((f32[8,24,128]{2,1,0:T(8,128)}), f32[8,24,128]{2,1,0:T(8,128)}, u32[]{:S(2)}, u32[]{:S(2)}) %all-to-all-start.10) | async-done | bytes 98336 | tf_op jit(solution)/shard_map/all_to_all | solution.py:26
  310.5 3.7 %all-to-all-start.9 = ((bf16[256,4,384]{2,0,1:T(8,128)(2,1)}), bf16[256,4,384]{2,0,1:T(8,128)(2,1)S(1)}, u32[]{:S(2)}, u32[]{:S(2)}) async-start(bf16[256,4,384]{2,0,1:T(8,128)(2,1)} %bitcast.127), calls=%async_computation.9 | async-start | bytes 1572864 | tf_op jit(solution)/shard_map/all_to_all | solution.py:135
  314.3 5.5 %fusion.1 = bf16[1,1,768,1536]{3,2,1,0:T(8,128)(2,1)} fusion(bf16[384,1536]{1,0:T(8,128)(2,1)} %get-tuple-element.23, bf16[384,1536]{1,0:T(8,128)(2,1)} %get-tuple-element.21, bf16[384,768]{1,0:T(8,128)(2,1)} %copy-done.31, bf16[384,768]{1,0:T(8,128)(2,1)} %copy-done.30), kind=kOutput, calls=%fused_computation.6 | convolution fusion | flops 1820196864 | bytes 5898240 | tf_op jit(solution)/shard_map/dot_general | solution.py:30
  319.8 5.1 %fusion = bf16[1,1,1536,768]{3,2,1,0:T(8,128)(2,1)} fusion(bf16[384,1536]{1,0:T(8,128)(2,1)} %bitcast.12, bf16[384,1536]{1,0:T(8,128)(2,1)} %bitcast.5, bf16[384,768]{1,0:T(8,128)(2,1)S(1)} %copy-done.37, bf16[384,768]{1,0:T(8,128)(2,1)S(1)} %copy-done.35), kind=kOutput, calls=%fused_computation.5 | convolution fusion | flops 1820196864 | bytes 5898240 | tf_op jit(solution)/shard_map/dot_general | solution.py:30
  328.3 2.3 copy.32
  (121 shorter events, 23.3 us)
Async XLA Ops:
  0.6 68.0 %copy-start = (bf16[1,1,768,1536]{3,2,1,0:T(8,128)(2,1)S(1)}, bf16[1,1,768,1536]{3,2,1,0:T(8,128)(2,1)}, u32[]{:S(2)}) copy-start(bf16[1,1,768,1536]{3,2,1,0:T(8,128)(2,1)} %param.12) | copy-start | bytes 7077892
  2.2 6.4 %copy-start.27 = (s32[1,256,2]{1,2,0:T(2,128)S(1)}, s32[1,256,2]{1,2,0:T(2,128)}, u32[]{:S(2)}) copy-start(s32[1,256,2]{1,2,0:T(2,128)} %param.8) | copy-start | bytes 6148
  3.4 16.0 %all-to-all-start = ((bf16[256,4,384]{2,0,1:T(8,128)(2,1)}), bf16[256,4,384]{2,0,1:T(8,128)(2,1)S(1)}, u32[]{:S(2)}, u32[]{:S(2)}) async-start(bf16[256,4,384]{2,0,1:T(8,128)(2,1)} %copy.25), calls=%async_computation | async-start | bytes 1572864 | tf_op jit(solution)/shard_map/all_to_all | solution.py:47
  11.0 153.4 %copy-start.8 = (s32[256]{0:T(256)}, s32[256]{0:T(256)S(1)}, u32[]{:S(2)}) copy-start(s32[256]{0:T(256)S(1)} %get-tuple-element.17) | copy-start | bytes 3076
  11.0 153.4 %copy-start.9 = (s32[256]{0:T(256)}, s32[256]{0:T(256)S(1)}, u32[]{:S(2)}) copy-start(s32[256]{0:T(256)S(1)} %get-tuple-element.18) | copy-start | bytes 3076
  19.4 0.9 copy-start.4
  23.0 34.4 %all-to-all-start.1 = ((bf16[8,48,1536]{2,1,0:T(8,128)(2,1)}), bf16[8,48,1536]{2,1,0:T(8,128)(2,1)}, u32[]{:S(2)}, u32[]{:S(2)}) async-start(bf16[8,48,1536]{2,1,0:T(8,128)(2,1)} %bitcast.135), calls=%async_computation.1 | async-start | bytes 2359296 | tf_op jit(solution)/shard_map/all_to_all | solution.py:26
  28.1 141.4 %copy-start.7 = (s32[256]{0:T(256)}, s32[256]{0:T(256)S(1)}, u32[]{:S(2)}) copy-start(s32[256]{0:T(256)S(1)} %get-tuple-element.16) | copy-start | bytes 3076
  57.4 4.4 %copy-start.6 = (bf16[1,1536,8]{1,2,0:T(8,128)(2,1)S(1)}, bf16[1,1536,8]{1,2,0:T(8,128)(2,1)}, u32[]{:S(2)}) copy-start(bf16[1,1536,8]{1,2,0:T(8,128)(2,1)} %param.9) | copy-start | bytes 73732
  57.4 33.8 %all-to-all-start.3 = ((bf16[8,48,1536]{2,1,0:T(8,128)(2,1)}), bf16[8,48,1536]{2,1,0:T(8,128)(2,1)}, u32[]{:S(2)}, u32[]{:S(2)}) async-start(bf16[8,48,1536]{2,1,0:T(8,128)(2,1)} %bitcast.134), calls=%async_computation.3 | async-start | bytes 2359296 | tf_op jit(solution)/shard_map/all_to_all | solution.py:26
  61.8 33.6 %copy-start.26 = (pred[8]{0:T(512)(128)(4,1)}, pred[8]{0:T(512)(128)(4,1)S(1)}, u32[]{:S(2)}) copy-start(pred[8]{0:T(512)(128)(4,1)S(1)} %iota_compare_fusion.6) | copy-start | bytes 28
  63.5 4.2 %copy-start.14 = (f32[384]{0:T(512)}, f32[384]{0:T(512)S(1)}, u32[]{:S(2)}) copy-start(f32[384]{0:T(512)S(1)} %fusion.63) | copy-start | bytes 4612
  63.6 4.2 %copy-start.16 = (f32[384]{0:T(512)}, f32[384]{0:T(512)S(1)}, u32[]{:S(2)}) copy-start(f32[384]{0:T(512)S(1)} %add_divide_fusion.1) | copy-start | bytes 4612
  91.2 33.6 %all-to-all-start.2 = ((bf16[8,48,1536]{2,1,0:T(8,128)(2,1)}), bf16[8,48,1536]{2,1,0:T(8,128)(2,1)}, u32[]{:S(2)}, u32[]{:S(2)}) async-start(bf16[8,48,1536]{2,1,0:T(8,128)(2,1)} %bitcast.143), calls=%async_computation.2 | async-start | bytes 2359296 | tf_op jit(solution)/shard_map/all_to_all | solution.py:26
  97.2 4.2 %copy-start.10 = (f32[384]{0:T(512)}, f32[384]{0:T(512)S(1)}, u32[]{:S(2)}) copy-start(f32[384]{0:T(512)S(1)} %fusion.64) | copy-start | bytes 4612
  97.2 4.2 %copy-start.12 = (f32[384]{0:T(512)}, f32[384]{0:T(512)S(1)}, u32[]{:S(2)}) copy-start(f32[384]{0:T(512)S(1)} %add_divide_fusion) | copy-start | bytes 4612
  101.4 0.8 copy-start.31
  124.8 4.4 %copy-start.25 = (f32[1,1536]{1,0:T(1,128)S(1)}, f32[1,1536]{1,0:T(1,128)}, u32[]{:S(2)}) copy-start(f32[1,1536]{1,0:T(1,128)} %param.10) | copy-start | bytes 18436
  124.8 33.8 %all-to-all-start.4 = ((bf16[8,48,1536]{2,1,0:T(8,128)(2,1)}), bf16[8,48,1536]{2,1,0:T(8,128)(2,1)}, u32[]{:S(2)}, u32[]{:S(2)}) async-start(bf16[8,48,1536]{2,1,0:T(8,128)(2,1)} %bitcast.144), calls=%async_computation.4 | async-start | bytes 2359296 | tf_op jit(solution)/shard_map/all_to_all | solution.py:26
  161.0 1.1 copy-start.5
  164.4 1.6 copy-start.1
  165.9 32.9 %all-to-all-start.5 = ((bf16[8,48,1536]{2,1,0:T(8,128)(2,1)}), bf16[8,48,1536]{2,1,0:T(8,128)(2,1)S(1)}, u32[]{:S(2)}, u32[]{:S(2)}) async-start(bf16[8,48,1536]{2,1,0:T(8,128)(2,1)} %bitcast.136), calls=%async_computation.5 | async-start | bytes 2359296 | tf_op jit(solution)/shard_map/all_to_all | solution.py:26
  198.8 1.1 copy-start.2
  198.8 6.3 %copy-start.17 = (f32[384]{0:T(512)S(1)}, f32[384]{0:T(512)}, u32[]{:S(2)}) copy-start(f32[384]{0:T(512)} %copy-done.16) | copy-start | bytes 4612
  199.9 32.9 %all-to-all-start.7 = ((bf16[8,48,1536]{2,1,0:T(8,128)(2,1)}), bf16[8,48,1536]{2,1,0:T(8,128)(2,1)S(1)}, u32[]{:S(2)}, u32[]{:S(2)}) async-start(bf16[8,48,1536]{2,1,0:T(8,128)(2,1)} %bitcast.133), calls=%async_computation.7 | async-start | bytes 2359296 | tf_op jit(solution)/shard_map/all_to_all | solution.py:26
  205.8 3.3 copy-start.15
  205.8 3.3 copy-start.3
  205.8 3.3 copy-start.18
  209.1 2.7 copy-start.20
  209.1 1.3 copy-start.33
  210.3 2.4 copy-start.23
  210.3 2.4 copy-start.28
  211.8 0.9 copy-start.34
  232.8 4.4 %copy-start.13 = (f32[384]{0:T(512)S(1)}, f32[384]{0:T(512)}, u32[]{:S(2)}) copy-start(f32[384]{0:T(512)} %copy-done.12) | copy-start | bytes 4612
  232.8 33.8 %all-to-all-start.6 = ((bf16[8,48,1536]{2,1,0:T(8,128)(2,1)}), bf16[8,48,1536]{2,1,0:T(8,128)(2,1)}, u32[]{:S(2)}, u32[]{:S(2)}) async-start(bf16[8,48,1536]{2,1,0:T(8,128)(2,1)} %bitcast.142), calls=%async_computation.6 | async-start | bytes 2359296 | tf_op jit(solution)/shard_map/all_to_all | solution.py:26
  237.9 2.8 copy-start.11
  237.9 2.8 copy-start.19
  240.7 2.8 copy-start.22
  240.7 1.3 copy-start.32
  242.0 2.4 copy-start.24
  242.0 2.4 copy-start.29
  243.5 0.9 copy-start.36
  266.6 4.4 %copy-start.21 = (f32[384]{0:T(512)S(1)}, f32[384]{0:T(512)}, u32[]{:S(2)}) copy-start(f32[384]{0:T(512)} %copy-done.20) | copy-start | bytes 4612
  266.6 33.0 %all-to-all-start.8 = ((bf16[8,48,1536]{2,1,0:T(8,128)(2,1)}), bf16[8,48,1536]{2,1,0:T(8,128)(2,1)S(1)}, u32[]{:S(2)}, u32[]{:S(2)}) async-start(bf16[8,48,1536]{2,1,0:T(8,128)(2,1)} %bitcast.141), calls=%async_computation.8 | async-start | bytes 2359296 | tf_op jit(solution)/shard_map/all_to_all | solution.py:26
  300.2 10.3 %all-to-all-start.10 = ((f32[8,24,128]{2,1,0:T(8,128)}), f32[8,24,128]{2,1,0:T(8,128)}, u32[]{:S(2)}, u32[]{:S(2)}) async-start(f32[8,24,128]{2,1,0:T(8,128)} %broadcast_in_dim.53), calls=%async_computation.10 | async-start | bytes 196608 | tf_op jit(solution)/shard_map/all_to_all | solution.py:26
  310.5 16.6 %all-to-all-start.9 = ((bf16[256,4,384]{2,0,1:T(8,128)(2,1)}), bf16[256,4,384]{2,0,1:T(8,128)(2,1)S(1)}, u32[]{:S(2)}, u32[]{:S(2)}) async-start(bf16[256,4,384]{2,0,1:T(8,128)(2,1)} %bitcast.127), calls=%async_computation.9 | async-start | bytes 1572864 | tf_op jit(solution)/shard_map/all_to_all | solution.py:135
  314.2 5.5 %copy-start.35 = (bf16[384,768]{1,0:T(8,128)(2,1)S(1)}, bf16[384,768]{1,0:T(8,128)(2,1)}, u32[]{:S(2)}) copy-start(bf16[384,768]{1,0:T(8,128)(2,1)} %copy-done.34) | copy-start | bytes 1769476
  314.3 5.5 %copy-start.37 = (bf16[384,768]{1,0:T(8,128)(2,1)S(1)}, bf16[384,768]{1,0:T(8,128)(2,1)}, u32[]{:S(2)}) copy-start(bf16[384,768]{1,0:T(8,128)(2,1)} %copy-done.36) | copy-start | bytes 1769476
  (1 other events, 0.8 us)

commit v2 on v1

v2 whole, which is shorter than its diff:
```python
import jax
import jax.numpy as jnp
from jax import lax
from jax.sharding import PartitionSpec as P


gelu_coef = 0.7978845608028654
cubic_coef = 0.044715
norm_eps = 1e-05


def gelu_tanh(value):
    inner = gelu_coef * (value + cubic_coef * value * value * value)
    return 0.5 * value * (1.0 + jnp.tanh(inner))


def gelu_slope(value):
    inner = gelu_coef * (value + cubic_coef * value * value * value)
    tangent = jnp.tanh(inner)
    return 0.5 * (1.0 + tangent) + 0.5 * value * (1.0 - tangent * tangent) * gelu_coef * (
        1.0 + 3.0 * cubic_coef * value * value
    )


def dot(a, b, dims):
    return lax.dot_general(a, b, (dims, ((), ())), preferred_element_type=jnp.float32)


def xor_pairs(size, k):
    return [(i, i ^ k) for i in range(size)]


def swap_cores(rows):
    return lax.ppermute(rows, "dp", xor_pairs(lax.axis_size("dp"), 1))


def to_chip(rows, k):
    return lax.ppermute(rows, "dp", xor_pairs(lax.axis_size("dp"), 2 * k)) if k else rows


def exchange(blocks):
    return lax.all_to_all(blocks, "dp", split_axis=0, concat_axis=0, tiled=True)


def mix_heads(rows):
    count = lax.axis_size("expert")
    mine = lax.axis_index("expert")
    head = rows.shape[1] // count
    if head % 128 or count & (count - 1):
        return lax.all_to_all(rows, "expert", split_axis=1, concat_axis=1, tiled=True)
    pieces = []
    for k in range(count):
        piece = lax.dynamic_slice_in_dim(rows, (mine ^ k) * head, head, 1)
        pieces.append(lax.ppermute(piece, "expert", xor_pairs(count, k)) if k else piece)
    stacked = jnp.stack(pieces)
    return jnp.concatenate(
        [lax.dynamic_index_in_dim(stacked, mine ^ t, 0, False) for t in range(count)], axis=1
    )


def body(tokens, route_ids, router, norm_gain, w_in, w_out, cotangent):
    row_count = tokens.shape[0]
    model_width = tokens.shape[2]
    experts = lax.axis_size("dp")
    chips = experts // 2
    depth = 3 * row_count // experts
    weight_in = w_in[0, 0]
    weight_out = w_out[0, 0]
    hidden = weight_in.shape[1]
    router_row = router[0]
    gain_row = norm_gain[0]
    me = lax.axis_index("dp")
    far = list(range(chips // 2, chips))
    near = list(range(chips // 2))
    groups = [far[:1], near] + [[k] for k in far[1:]]

    route_rows = route_ids.reshape(row_count, 2)
    labels = lax.broadcasted_iota(jnp.int32, (row_count, 2, experts), 2)
    flat_hot = (route_rows[:, :, None] == labels).astype(jnp.int32).reshape(row_count * 2, experts)
    before = jnp.cumsum(flat_hot, axis=0, dtype=jnp.int32) - flat_hot
    slot_place = jnp.sum(before * flat_hot, axis=1, dtype=jnp.int32).reshape(row_count, 2)
    target = (route_rows ^ me) * depth + slot_place

    def placer_of(group):
        rows = []
        for k in group:
            slot = lax.broadcasted_iota(jnp.int32, (2 * depth, row_count), 0) + 2 * k * depth
            rows.append(jnp.logical_or(target[None, :, 0] == slot, target[None, :, 1] == slot))
        return jnp.concatenate(rows).astype(jnp.bfloat16) if len(rows) > 1 else rows[0].astype(jnp.bfloat16)

    placers = [placer_of(g) for g in groups]
    my_column = lax.broadcasted_iota(jnp.int32, (1, experts), 1) == me
    router_mine = jnp.sum(jnp.where(my_column, router_row.astype(jnp.float32), 0.0), axis=1)

    def dispatch(rows):
        arrived = []
        for group, placer in zip(groups, placers):
            slots = dot(placer, rows, ((1,), (0,))).astype(jnp.bfloat16)
            parts = [to_chip(slots[2 * depth * i : 2 * depth * (i + 1)], k) for i, k in enumerate(group)]
            mine = jnp.concatenate([p[:depth] for p in parts])
            others = jnp.concatenate([p[depth:] for p in parts])
            arrived.append(jnp.concatenate([mine, swap_cores(others)]))
        return arrived

    def give_back(group, rows):
        half = len(group) * depth
        others = swap_cores(rows[half:])
        parts = []
        for i, k in enumerate(group):
            pair = jnp.concatenate([rows[depth * i : depth * (i + 1)], others[depth * i : depth * (i + 1)]])
            parts.append(to_chip(pair, k))
        return jnp.concatenate(parts)

    def collect(parts):
        return sum(dot(p, r, ((0,), (0,))) for p, r in zip(placers, parts))

    mixed = mix_heads(tokens.reshape(row_count, model_width))
    kept, parts = [], []
    for group, rows in zip(groups, dispatch(mixed)):
        logits = lax.optimization_barrier(dot(rows, router_row, ((1,), (0,))))
        gate = jax.nn.sigmoid(jnp.sum(jnp.where(my_column, logits, 0.0), axis=1, keepdims=True))
        pre_act = dot(rows, weight_in, ((1,), (0,)))
        act = gelu_tanh(pre_act).astype(jnp.bfloat16)
        out = dot(act, weight_out, ((1,), (0,)))
        kept.append((rows, gate, pre_act, act, out.astype(jnp.bfloat16)))
        parts.append(give_back(group, (gate * out).astype(jnp.bfloat16)))
    residual = mixed.astype(jnp.float32) + collect(parts)
    row_mean = jnp.mean(residual, axis=1, keepdims=True)
    centered = residual - row_mean
    row_var = jnp.mean(centered * centered, axis=1, keepdims=True)
    inv_std = lax.rsqrt(row_var + norm_eps)
    normed = centered * inv_std
    normed_out = (normed * gain_row[None, :]).astype(jnp.bfloat16)
    cot_f = cotangent.reshape(row_count, model_width).astype(jnp.float32)
    grad_gain = jnp.sum(cot_f * normed, axis=0)
    grad_normed = cot_f * gain_row[None, :]
    grad_resid = inv_std * (
        grad_normed
        - jnp.mean(grad_normed, axis=1, keepdims=True)
        - normed * jnp.mean(grad_normed * normed, axis=1, keepdims=True)
    )

    slopes = lax.optimization_barrier([gelu_slope(s[2]) for s in kept])
    parts, pre_grads, out_grads, logit_grads = [], [], [], []
    arrived = dispatch(grad_resid.astype(jnp.bfloat16))
    for g, (group, grads, saved) in enumerate(zip(groups, arrived, kept)):
        rows, gate, pre_act, act, result = saved
        grads_f = grads.astype(jnp.float32)
        grad_out = (gate * grads_f).astype(jnp.bfloat16)
        grad_gate = jnp.sum(grads_f * result.astype(jnp.float32), axis=1, keepdims=True)
        grad_logit = grad_gate * gate * (1.0 - gate)
        grad_act = dot(grad_out, weight_out, ((1,), (1,)))
        grad_pre = (grad_act * slopes[g]).astype(jnp.bfloat16)
        grad_input = dot(grad_pre, weight_in, ((1,), (1,))) + grad_logit * router_mine[None, :]
        parts.append(give_back(group, grad_input.astype(jnp.bfloat16)))
        pre_grads.append(grad_pre)
        out_grads.append(grad_out)
        logit_grads.append(grad_logit)
    grad_mixed = grad_resid + collect(parts)
    grad_tokens = mix_heads(grad_mixed.astype(jnp.bfloat16))

    all_rows = jnp.concatenate([s[0] for s in kept])
    all_act = jnp.concatenate([s[3] for s in kept])
    router_part = jnp.sum(all_rows.astype(jnp.float32) * jnp.concatenate(logit_grads), axis=0)
    lanes = 128
    small = jnp.stack([router_part, grad_gain]).reshape(1, 2 * model_width // lanes, lanes)
    small = exchange(jnp.broadcast_to(small, (experts,) + small.shape[1:]))
    small = small.reshape(experts, 2, model_width)
    grad_w_out = dot(all_act, jnp.concatenate(out_grads), ((0,), (0,))).astype(jnp.bfloat16)
    grad_w_in = dot(all_rows, jnp.concatenate(pre_grads), ((0,), (0,))).astype(jnp.bfloat16)
    return (
        normed_out.reshape(row_count, 1, model_width),
        grad_tokens.reshape(row_count, 1, model_width),
        small[:, 0].T.reshape(1, model_width, experts),
        jnp.sum(small[:, 1], axis=0).reshape(1, model_width),
        grad_w_in.reshape(1, 1, model_width, hidden),
        grad_w_out.reshape(1, 1, hidden, model_width),
    )


def solution(mesh):
    return jax.shard_map(
        body,
        mesh=mesh,
        in_specs=(
            P("dp", "expert", None),
            P("expert", "dp", None),
            P("expert", None, None),
            P("expert", None),
            P("expert", "dp", None, None),
            P("expert", "dp", None, None),
            P("dp", "expert", None),
        ),
        out_specs=(
            P("dp", "expert", None),
            P("dp", "expert", None),
            P("expert", None, None),
            P("expert", None),
            P("expert", "dp", None, None),
            P("expert", "dp", None, None),
        ),
        check_vma=False,
    )
```

time: 332 us -> 303 us (0.913)
  the two profiles are of different devices: /device:TPU:0 before, /device:TPU:16 now
where the time goes in v2:
time: 303 us
  waiting for transfers between devices  205 us (68%)
  starting transfers between devices  32.7 us (11%)
  matrix products  28.8 us (10%)
  local copies, waits for them, and re-layouts  18.2 us (6%)
  other arithmetic  16.5 us (5%)
    ppermute x12, waiting for transfers between devices, to_chip(): lax.ppermute(rows, 'dp', xor_pairs(lax.axis_size('dp'), 2 * k))  189 us
    dot_general x29, matrix products, dot(): lax.dot_general(a, b, (dims, ((), ())), preferred_element_type=jnp.float32)  28.8 us
    ppermute x12, starting transfers between devices, to_chip(): lax.ppermute(rows, 'dp', xor_pairs(lax.axis_size('dp'), 2 * k))  19 us
    ppermute x6, waiting for transfers between devices, mix_heads(): lax.ppermute(piece, 'expert', xor_pairs(count, k))  13.9 us
    ppermute x6, starting transfers between devices, mix_heads(): lax.ppermute(piece, 'expert', xor_pairs(count, k))  7.04 us
  transfers between devices with their start and end apart: 31, of which 17 were waited for; matrix products, arithmetic and copies ran while one was open for 16% of the time, Pallas kernels for 0%

profile of v2, /device:TPU:16, one launch (start us, length us, event | category | flops | bytes accessed | tf_op | source)
XLA Modules:
  0.0 302.5 jit_solution(5412870402840543631)
XLA Ops:
  0.7 2.1 dynamic-slice_bitcast_fusion.12
  2.8 1.5 collective-permute-start
  4.3 1.5 collective-permute-start.1
  6.8 1.1 reduce-window.6
  8.5 2.3 collective-permute-done
  10.8 3.1 %collective-permute-done.1 = bf16[256,384]{1,0:T(8,128)(2,1)S(1)} collective-permute-done((bf16[256,384]{1,0:T(8,128)(2,1)S(1)}, bf16[256,384]{1,0:T(8,128)(2,1)S(1)}, u32[]{:S(2)}, u32[]{:S(2)}) %collective-permute-start.1) | collective-permute-done | bytes 196640 | tf_op jit(solution)/shard_map/ppermute | solution.py:54
  13.9 1.1 collective-permute-done.2
  15.0 1.0 pad_maximum_fusion.2
  17.6 23.6 %collective-permute-done.3 = bf16[192,1536]{1,0:T(8,128)(2,1)S(1)} collective-permute-done((bf16[192,1536]{1,0:T(8,128)(2,1)S(1)}, bf16[192,1536]{1,0:T(8,128)(2,1)S(1)}, u32[]{:S(2)}, u32[]{:S(2)}) %collective-permute-start.3) | collective-permute-done | bytes 589856 | tf_op jit(solution)/shard_map/ppermute | solution.py:38
  41.2 0.9 constant_dynamic-update-slice_fusion.6
  44.8 4.6 %collective-permute-start.7 = (bf16[192,1536]{1,0:T(8,128)(2,1)S(1)}, bf16[192,1536]{1,0:T(8,128)(2,1)S(1)}, u32[]{:S(2)}, u32[]{:S(2)}) collective-permute-start(bf16[192,1536]{1,0:T(8,128)(2,1)S(1)} %slice.188), channel_id=1, source_target_pairs={{0,8},{4,12},{8,0},{12,4},{16,24},{20,28},{24,16},{28,20},{1,9},{5... | collective-permute-start | bytes 1769480 | tf_op jit(solution)/shard_map/ppermute | solution.py:38
  49.5 13.9 %collective-permute-done.7 = bf16[192,1536]{1,0:T(8,128)(2,1)S(1)} collective-permute-done((bf16[192,1536]{1,0:T(8,128)(2,1)S(1)}, bf16[192,1536]{1,0:T(8,128)(2,1)S(1)}, u32[]{:S(2)}, u32[]{:S(2)}) %collective-permute-start.7) | collective-permute-done | bytes 589856 | tf_op jit(solution)/shard_map/ppermute | solution.py:38
  66.3 26.2 %collective-permute-done.11 = bf16[192,1536]{1,0:T(8,128)(2,1)S(1)} collective-permute-done((bf16[192,1536]{1,0:T(8,128)(2,1)S(1)}, bf16[192,1536]{1,0:T(8,128)(2,1)S(1)}, u32[]{:S(2)}, u32[]{:S(2)}) %collective-permute-start.11) | collective-permute-done | bytes 589856 | tf_op jit(solution)/shard_map/ppermute | solution.py:38
  93.2 1.6 fusion.71
  94.9 1.1 multiply_convert_fusion
  101.2 2.9 collective-permute-start.6
  104.1 16.5 %collective-permute-done.14 = bf16[192,1536]{1,0:T(8,128)(2,1)S(1)} collective-permute-done((bf16[192,1536]{1,0:T(8,128)(2,1)S(1)}, bf16[192,1536]{1,0:T(8,128)(2,1)S(1)}, u32[]{:S(2)}, u32[]{:S(2)}) %collective-permute-start.14) | collective-permute-done | bytes 589856 | tf_op jit(solution)/shard_map/ppermute | solution.py:38
  121.7 20.2 %collective-permute-done.6 = bf16[192,1536]{1,0:T(8,128)(2,1)S(1)} collective-permute-done((bf16[192,1536]{1,0:T(8,128)(2,1)S(1)}, bf16[192,1536]{1,0:T(8,128)(2,1)S(1)}, u32[]{:S(2)}, u32[]{:S(2)}) %collective-permute-start.6) | collective-permute-done | bytes 589856 | tf_op jit(solution)/shard_map/ppermute | solution.py:38
  144.5 1.5 fusion.42
  146.8 3.5 %collective-permute-start.15 = (bf16[192,1536]{1,0:T(8,128)(2,1)S(1)}, bf16[192,1536]{1,0:T(8,128)(2,1)S(1)}, u32[]{:S(2)}, u32[]{:S(2)}) collective-permute-start(bf16[192,1536]{1,0:T(8,128)(2,1)S(1)} %convolution_convert_fusion.5), channel_id=1, source_target_pairs={{0,16},{4,20},{8,24},{12,28},{16,0},{20,4},{24,8},{28,12},{1,17},{... | collective-permute-start | bytes 1769480 | tf_op jit(solution)/shard_map/ppermute | solution.py:38
  150.3 1.2 collective-permute-start.19
  152.2 1.5 collective-permute-start.23
  153.7 23.2 %collective-permute-done.15 = bf16[192,1536]{1,0:T(8,128)(2,1)S(1)} collective-permute-done((bf16[192,1536]{1,0:T(8,128)(2,1)S(1)}, bf16[192,1536]{1,0:T(8,128)(2,1)S(1)}, u32[]{:S(2)}, u32[]{:S(2)}) %collective-permute-start.15) | collective-permute-done | bytes 589856 | tf_op jit(solution)/shard_map/ppermute | solution.py:38
  177.0 12.6 %collective-permute-done.19 = bf16[192,1536]{1,0:T(8,128)(2,1)S(1)} collective-permute-done((bf16[192,1536]{1,0:T(8,128)(2,1)S(1)}, bf16[192,1536]{1,0:T(8,128)(2,1)S(1)}, u32[]{:S(2)}, u32[]{:S(2)}) %collective-permute-start.19) | collective-permute-done | bytes 589856 | tf_op jit(solution)/shard_map/ppermute | solution.py:38
  189.8 12.0 %collective-permute-done.23 = bf16[192,1536]{1,0:T(8,128)(2,1)S(1)} collective-permute-done((bf16[192,1536]{1,0:T(8,128)(2,1)S(1)}, bf16[192,1536]{1,0:T(8,128)(2,1)S(1)}, u32[]{:S(2)}, u32[]{:S(2)}) %collective-permute-start.23) | collective-permute-done | bytes 589856 | tf_op jit(solution)/shard_map/ppermute | solution.py:38
  202.3 1.2 collective-permute-done.24
  210.3 1.0 copy-done.5
  211.3 1.1 fusion.48
  212.5 1.1 fusion.2
  213.6 3.5 %fusion = bf16[1,1,1536,768]{3,2,1,0:T(8,128)(2,1)} fusion(bf16[768,1536]{1,0:T(8,128)(2,1)S(1)} %constant_dynamic-update-slice_fusion, bf16[192,768]{1,0:T(8,128)(2,1)S(1)} %fusion.57, bf16[384,768]{1,0:T(8,128)(2,1)S(1)} %fusion.48, bf16[192,768]{1,0:T(8,128)(2,1)S(1)} %fusion.60), kind=kOutput, calls=%fused_computation.4 | convolution fusion | flops 1816657920 | bytes 5898240 | tf_op jit(solution)/shard_map/dot_general | solution.py:26
  220.2 1.3 broadcast_in_dim.66
  221.5 1.4 broadcast_in_dim.67
  222.9 4.5 %all-to-all-start = ((f32[8,24,128]{2,1,0:T(8,128)}), f32[8,24,128]{2,1,0:T(8,128)}, u32[]{:S(2)}, u32[]{:S(2)}) async-start(f32[8,24,128]{2,1,0:T(8,128)} %broadcast_in_dim.67), calls=%async_computation | async-start | bytes 196608 | tf_op jit(solution)/shard_map/all_to_all | solution.py:42
  227.4 2.0 pad_maximum_fusion.12
  229.4 2.1 pad_maximum_fusion.16
  231.4 2.9 collective-permute-start.26
  234.3 1.8 fusion.135
  237.0 1.5 collective-permute-start.22
  238.5 3.4 %fusion.1 = bf16[1,1,768,1536]{3,2,1,0:T(8,128)(2,1)} fusion(bf16[192,1536]{1,0:T(8,128)(2,1)S(1)} %get-tuple-element.70, bf16[384,1536]{1,0:T(8,128)(2,1)S(1)} %copy-done.6, bf16[192,1536]{1,0:T(8,128)(2,1)S(1)} %get-tuple-element.60, bf16[192,768]{1,0:T(8,128)(2,1)S(1)} %copy-done.11, bf16[384,768]{1,0:T(8,128)(2,1)S(1)} %copy-done.28, ...), kind=kOutput, calls=%fused_computation.5 | convolution fusion | flops 1823735808 | bytes 5898240 | tf_op jit(solution)/shard_map/dot_general | solution.py:26
  242.0 1.0 reshape.235
  243.0 40.9 %collective-permute-done.26 = bf16[192,1536]{1,0:T(8,128)(2,1)} collective-permute-done((bf16[192,1536]{1,0:T(8,128)(2,1)}, bf16[192,1536]{1,0:T(8,128)(2,1)}, u32[]{:S(2)}, u32[]{:S(2)}) %collective-permute-start.26) | collective-permute-done | bytes 589856 | tf_op jit(solution)/shard_map/ppermute | solution.py:38
  283.9 1.5 fusion.128
  285.5 1.8 fusion.78
  287.3 1.6 fusion.7
  289.0 1.6 collective-permute-start.27
  291.1 1.4 collective-permute-start.29
  293.9 3.0 collective-permute-done.27
  296.8 4.5 %collective-permute-done.28 = bf16[256,384]{1,0:T(8,128)(2,1)S(1)} collective-permute-done((bf16[256,384]{1,0:T(8,128)(2,1)S(1)}, bf16[256,384]{1,0:T(8,128)(2,1)S(1)}, u32[]{:S(2)}, u32[]{:S(2)}) %collective-permute-start.28) | collective-permute-done | bytes 196640 | tf_op jit(solution)/shard_map/ppermute | solution.py:54
  (188 shorter events, 34.3 us)
Async XLA Ops:
  0.6 94.2 %copy-start = (bf16[1,1,768,1536]{3,2,1,0:T(8,128)(2,1)S(1)}, bf16[1,1,768,1536]{3,2,1,0:T(8,128)(2,1)}, u32[]{:S(2)}) copy-start(bf16[1,1,768,1536]{3,2,1,0:T(8,128)(2,1)} %param.12) | copy-start | bytes 7077892
  2.8 8.0 %collective-permute-start = (bf16[256,384]{1,0:T(8,128)(2,1)}, bf16[256,384]{1,0:T(8,128)(2,1)S(1)}, u32[]{:S(2)}, u32[]{:S(2)}) collective-permute-start(bf16[256,384]{1,0:T(8,128)(2,1)} %get-tuple-element.45), channel_id=1, source_target_pairs={{0,1},{1,0},{2,3},{3,2},{4,5},{5,4},{6,7},{7,6},{8,9},{9,8},{10,11... | collective-permute-start | bytes 589832 | tf_op jit(solution)/shard_map/ppermute | solution.py:54
  4.3 9.6 %collective-permute-start.1 = (bf16[256,384]{1,0:T(8,128)(2,1)S(1)}, bf16[256,384]{1,0:T(8,128)(2,1)S(1)}, u32[]{:S(2)}, u32[]{:S(2)}) collective-permute-start(bf16[256,384]{1,0:T(8,128)(2,1)S(1)} %get-tuple-element.47), channel_id=1, source_target_pairs={{0,2},{1,3},{2,0},{3,1},{4,6},{5,7},{6,4},{7,5},{8,10},{9,11},{10,... | collective-permute-start | bytes 589832 | tf_op jit(solution)/shard_map/ppermute | solution.py:54
  5.8 9.2 %collective-permute-start.2 = (bf16[256,384]{1,0:T(8,128)(2,1)S(1)}, bf16[256,384]{1,0:T(8,128)(2,1)}, u32[]{:S(2)}, u32[]{:S(2)}) collective-permute-start(bf16[256,384]{1,0:T(8,128)(2,1)S(1)} %get-tuple-element.46), channel_id=1, source_target_pairs={{0,3},{1,2},{2,1},{3,0},{4,7},{5,6},{6,5},{7,4},{8,11},{9,10},{10,... | collective-permute-start | bytes 589832 | tf_op jit(solution)/shard_map/ppermute | solution.py:54
  6.8 9.4 %copy-start.22 = (s32[192]{0:T(256)}, s32[192]{0:T(256)S(1)}, u32[]{:S(2)}) copy-start(s32[192]{0:T(256)S(1)} %iota_add_fusion.2) | copy-start | bytes 2308
  16.5 24.7 %collective-permute-start.3 = (bf16[192,1536]{1,0:T(8,128)(2,1)S(1)}, bf16[192,1536]{1,0:T(8,128)(2,1)S(1)}, u32[]{:S(2)}, u32[]{:S(2)}) collective-permute-start(bf16[192,1536]{1,0:T(8,128)(2,1)S(1)} %convolution_convert_fusion.7), channel_id=1, source_target_pairs={{0,16},{4,20},{8,24},{12,28},{16,0},{20,4},{24,8},{28,12},{1,17},{... | collective-permute-start | bytes 1769480 | tf_op jit(solution)/shard_map/ppermute | solution.py:38
  17.6 128.7 %copy-start.15 = (pred[192,256]{1,0:T(32,128)(4,1)}, pred[192,256]{1,0:T(32,128)(4,1)S(1)}, u32[]{:S(2)}) copy-start(pred[192,256]{1,0:T(32,128)(4,1)S(1)} %get-tuple-element.85) | copy-start | bytes 147460
  17.6 128.7 %copy-start.17 = (pred[192,256]{1,0:T(32,128)(4,1)}, pred[192,256]{1,0:T(32,128)(4,1)S(1)}, u32[]{:S(2)}) copy-start(pred[192,256]{1,0:T(32,128)(4,1)S(1)} %get-tuple-element.86) | copy-start | bytes 147460
  42.2 7.2 %collective-permute-start.4 = (bf16[96,1536]{1,0:T(8,128)(2,1)}, bf16[96,1536]{1,0:T(8,128)(2,1)S(1)}, u32[]{:S(2)}, u32[]{:S(2)}) collective-permute-start(bf16[96,1536]{1,0:T(8,128)(2,1)} %get-tuple-element.55), channel_id=1, source_target_pairs={{0,4},{4,0},{8,12},{12,8},{16,20},{20,16},{24,28},{28,24},{1,5},{5... | collective-permute-start | bytes 884744 | tf_op jit(solution)/shard_map/ppermute | solution.py:34
  44.8 18.6 %collective-permute-start.7 = (bf16[192,1536]{1,0:T(8,128)(2,1)S(1)}, bf16[192,1536]{1,0:T(8,128)(2,1)S(1)}, u32[]{:S(2)}, u32[]{:S(2)}) collective-permute-start(bf16[192,1536]{1,0:T(8,128)(2,1)S(1)} %slice.188), channel_id=1, source_target_pairs={{0,8},{4,12},{8,0},{12,4},{16,24},{20,28},{24,16},{28,20},{1,9},{5... | collective-permute-start | bytes 1769480 | tf_op jit(solution)/shard_map/ppermute | solution.py:38
  49.5 14.1 %copy-start.20 = (s32[192]{0:T(256)S(1)}, s32[192]{0:T(256)}, u32[]{:S(2)}) copy-start(s32[192]{0:T(256)} %iota_add_fusion) | copy-start | bytes 2308
  63.5 2.7 collective-permute-start.8
  64.0 28.4 %collective-permute-start.11 = (bf16[192,1536]{1,0:T(8,128)(2,1)S(1)}, bf16[192,1536]{1,0:T(8,128)(2,1)S(1)}, u32[]{:S(2)}, u32[]{:S(2)}) collective-permute-start(bf16[192,1536]{1,0:T(8,128)(2,1)S(1)} %convolution_convert_fusion.6), channel_id=1, source_target_pairs={{0,24},{4,28},{8,16},{12,20},{16,8},{20,12},{24,0},{28,4},{1,25},{... | collective-permute-start | bytes 1769480 | tf_op jit(solution)/shard_map/ppermute | solution.py:38
  66.2 32.5 %copy-start.8 = (bf16[192,768]{1,0:T(8,128)(2,1)}, bf16[192,768]{1,0:T(8,128)(2,1)S(1)}, u32[]{:S(2)}) copy-start(bf16[192,768]{1,0:T(8,128)(2,1)S(1)} %get-tuple-element.76) | copy-start | bytes 884740
  92.5 4.0 %collective-permute-start.12 = (bf16[96,1536]{1,0:T(8,128)(2,1)S(1)}, bf16[96,1536]{1,0:T(8,128)(2,1)S(1)}, u32[]{:S(2)}, u32[]{:S(2)}) collective-permute-start(bf16[96,1536]{1,0:T(8,128)(2,1)S(1)} %get-tuple-element.49), channel_id=1, source_target_pairs={{0,4},{4,0},{8,12},{12,8},{16,20},{20,16},{24,28},{28,24},{1,5},{5... | collective-permute-start | bytes 884744 | tf_op jit(solution)/shard_map/ppermute | solution.py:34
  96.0 4.6 %collective-permute-start.9 = (bf16[192,1536]{1,0:T(8,128)(2,1)S(1)}, bf16[192,1536]{1,0:T(8,128)(2,1)S(1)}, u32[]{:S(2)}, u32[]{:S(2)}) collective-permute-start(bf16[192,1536]{1,0:T(8,128)(2,1)S(1)} %slice.193), channel_id=1, source_target_pairs={{0,4},{4,0},{8,12},{12,8},{16,20},{20,16},{24,28},{28,24},{1,5},{5... | collective-permute-start | bytes 1769480 | tf_op jit(solution)/shard_map/ppermute | solution.py:34
  98.6 1.6 collective-permute-start.13
  99.4 1.7 collective-permute-start.5
  100.3 20.3 %collective-permute-start.14 = (bf16[192,1536]{1,0:T(8,128)(2,1)S(1)}, bf16[192,1536]{1,0:T(8,128)(2,1)S(1)}, u32[]{:S(2)}, u32[]{:S(2)}) collective-permute-start(bf16[192,1536]{1,0:T(8,128)(2,1)S(1)} %pad_maximum_fusion.10), channel_id=1, source_target_pairs={{0,24},{4,28},{8,16},{12,20},{16,8},{20,12},{24,0},{28,4},{1,25},{... | collective-permute-start | bytes 1769480 | tf_op jit(solution)/shard_map/ppermute | solution.py:38
  100.7 20.4 %collective-permute-start.10 = (bf16[192,1536]{1,0:T(8,128)(2,1)S(1)}, bf16[192,1536]{1,0:T(8,128)(2,1)S(1)}, u32[]{:S(2)}, u32[]{:S(2)}) collective-permute-start(bf16[192,1536]{1,0:T(8,128)(2,1)S(1)} %pad_maximum_fusion.8), channel_id=1, source_target_pairs={{0,8},{4,12},{8,0},{12,4},{16,24},{20,28},{24,16},{28,20},{1,9},{5... | collective-permute-start | bytes 1769480 | tf_op jit(solution)/shard_map/ppermute | solution.py:38
  101.2 40.7 %collective-permute-start.6 = (bf16[192,1536]{1,0:T(8,128)(2,1)S(1)}, bf16[192,1536]{1,0:T(8,128)(2,1)S(1)}, u32[]{:S(2)}, u32[]{:S(2)}) collective-permute-start(bf16[192,1536]{1,0:T(8,128)(2,1)S(1)} %pad_maximum_fusion.6), channel_id=1, source_target_pairs={{0,16},{4,20},{8,24},{12,28},{16,0},{20,4},{24,8},{28,12},{1,17},{... | collective-permute-start | bytes 1769480 | tf_op jit(solution)/shard_map/ppermute | solution.py:38
  121.1 20.8 %copy-start.23 = (s32[192]{0:T(256)S(1)}, s32[192]{0:T(256)}, u32[]{:S(2)}) copy-start(s32[192]{0:T(256)} %copy-done.22) | copy-start | bytes 2308
  146.8 30.1 %collective-permute-start.15 = (bf16[192,1536]{1,0:T(8,128)(2,1)S(1)}, bf16[192,1536]{1,0:T(8,128)(2,1)S(1)}, u32[]{:S(2)}, u32[]{:S(2)}) collective-permute-start(bf16[192,1536]{1,0:T(8,128)(2,1)S(1)} %convolution_convert_fusion.5), channel_id=1, source_target_pairs={{0,16},{4,20},{8,24},{12,28},{16,0},{20,4},{24,8},{28,12},{1,17},{... | collective-permute-start | bytes 1769480 | tf_op jit(solution)/shard_map/ppermute | solution.py:38
  150.3 39.3 %collective-permute-start.19 = (bf16[192,1536]{1,0:T(8,128)(2,1)S(1)}, bf16[192,1536]{1,0:T(8,128)(2,1)S(1)}, u32[]{:S(2)}, u32[]{:S(2)}) collective-permute-start(bf16[192,1536]{1,0:T(8,128)(2,1)S(1)} %slice.206), channel_id=1, source_target_pairs={{0,8},{4,12},{8,0},{12,4},{16,24},{20,28},{24,16},{28,20},{1,9},{5... | collective-permute-start | bytes 1769480 | tf_op jit(solution)/shard_map/ppermute | solution.py:38
  152.2 49.6 %collective-permute-start.23 = (bf16[192,1536]{1,0:T(8,128)(2,1)S(1)}, bf16[192,1536]{1,0:T(8,128)(2,1)S(1)}, u32[]{:S(2)}, u32[]{:S(2)}) collective-permute-start(bf16[192,1536]{1,0:T(8,128)(2,1)S(1)} %convolution_convert_fusion.4), channel_id=1, source_target_pairs={{0,24},{4,28},{8,16},{12,20},{16,8},{20,12},{24,0},{28,4},{1,25},{... | collective-permute-start | bytes 1769480 | tf_op jit(solution)/shard_map/ppermute | solution.py:38
  176.9 25.0 %collective-permute-start.16 = (bf16[96,1536]{1,0:T(8,128)(2,1)S(1)}, bf16[96,1536]{1,0:T(8,128)(2,1)S(1)}, u32[]{:S(2)}, u32[]{:S(2)}) collective-permute-start(bf16[96,1536]{1,0:T(8,128)(2,1)S(1)} %get-tuple-element.62), channel_id=1, source_target_pairs={{0,4},{4,0},{8,12},{12,8},{16,20},{20,16},{24,28},{28,24},{1,5},{5... | collective-permute-start | bytes 884744 | tf_op jit(solution)/shard_map/ppermute | solution.py:34
  189.7 20.1 %collective-permute-start.20 = (bf16[192,1536]{1,0:T(8,128)(2,1)S(1)}, bf16[192,1536]{1,0:T(8,128)(2,1)S(1)}, u32[]{:S(2)}, u32[]{:S(2)}) collective-permute-start(bf16[192,1536]{1,0:T(8,128)(2,1)S(1)} %pad_maximum_fusion.13), channel_id=1, source_target_pairs={{0,4},{4,0},{8,12},{12,8},{16,20},{20,16},{24,28},{28,24},{1,5},{5... | collective-permute-start | bytes 1769480 | tf_op jit(solution)/shard_map/ppermute | solution.py:34
  201.8 1.6 collective-permute-start.24
  206.6 20.8 %collective-permute-start.17 = (bf16[96,1536]{1,0:T(8,128)(2,1)}, bf16[96,1536]{1,0:T(8,128)(2,1)}, u32[]{:S(2)}, u32[]{:S(2)}) collective-permute-start(bf16[96,1536]{1,0:T(8,128)(2,1)} %get-tuple-element.58), channel_id=1, source_target_pairs={{0,4},{4,0},{8,12},{12,8},{16,20},{20,16},{24,28},{28,24},{1,5},{5... | collective-permute-start | bytes 884744 | tf_op jit(solution)/shard_map/ppermute | solution.py:34
  209.4 20.0 %collective-permute-start.25 = (bf16[96,1536]{1,0:T(8,128)(2,1)}, bf16[96,1536]{1,0:T(8,128)(2,1)}, u32[]{:S(2)}, u32[]{:S(2)}) collective-permute-start(bf16[96,1536]{1,0:T(8,128)(2,1)} %get-tuple-element.68), channel_id=1, source_target_pairs={{0,4},{4,0},{8,12},{12,8},{16,20},{20,16},{24,28},{28,24},{1,5},{5... | collective-permute-start | bytes 884744 | tf_op jit(solution)/shard_map/ppermute | solution.py:34
  219.5 14.9 %collective-permute-start.21 = (bf16[192,1536]{1,0:T(8,128)(2,1)}, bf16[192,1536]{1,0:T(8,128)(2,1)}, u32[]{:S(2)}, u32[]{:S(2)}) collective-permute-start(bf16[192,1536]{1,0:T(8,128)(2,1)} %slice.211), channel_id=1, source_target_pairs={{0,4},{4,0},{8,12},{12,8},{16,20},{20,16},{24,28},{28,24},{1,5},{5... | collective-permute-start | bytes 1769480 | tf_op jit(solution)/shard_map/ppermute | solution.py:34
  222.9 19.1 %all-to-all-start = ((f32[8,24,128]{2,1,0:T(8,128)}), f32[8,24,128]{2,1,0:T(8,128)}, u32[]{:S(2)}, u32[]{:S(2)}) async-start(f32[8,24,128]{2,1,0:T(8,128)} %broadcast_in_dim.67), calls=%async_computation | async-start | bytes 196608 | tf_op jit(solution)/shard_map/all_to_all | solution.py:42
  227.4 8.8 %copy-start.7 = (bf16[96,1536]{1,0:T(8,128)(2,1)S(1)}, bf16[96,1536]{1,0:T(8,128)(2,1)}, u32[]{:S(2)}) copy-start(bf16[96,1536]{1,0:T(8,128)(2,1)} %get-tuple-element.23) | copy-start | bytes 884740
  229.3 58.0 %collective-permute-start.18 = (bf16[192,1536]{1,0:T(8,128)(2,1)}, bf16[192,1536]{1,0:T(8,128)(2,1)}, u32[]{:S(2)}, u32[]{:S(2)}) collective-permute-start(bf16[192,1536]{1,0:T(8,128)(2,1)} %pad_maximum_fusion.12), channel_id=1, source_target_pairs={{0,16},{4,20},{8,24},{12,28},{16,0},{20,4},{24,8},{28,12},{1,17},{... | collective-permute-start | bytes 1769480 | tf_op jit(solution)/shard_map/ppermute | solution.py:38
  229.3 9.1 %copy-start.6 = (bf16[384,1536]{1,0:T(8,128)(2,1)S(1)}, bf16[384,1536]{1,0:T(8,128)(2,1)}, u32[]{:S(2)}) copy-start(bf16[384,1536]{1,0:T(8,128)(2,1)} %copy-done.5) | copy-start | bytes 3538948
  229.4 9.1 %copy-start.9 = (bf16[192,768]{1,0:T(8,128)(2,1)S(1)}, bf16[192,768]{1,0:T(8,128)(2,1)}, u32[]{:S(2)}) copy-start(bf16[192,768]{1,0:T(8,128)(2,1)} %copy-done.8) | copy-start | bytes 884740
  229.4 9.1 %copy-start.11 = (bf16[192,768]{1,0:T(8,128)(2,1)S(1)}, bf16[192,768]{1,0:T(8,128)(2,1)}, u32[]{:S(2)}) copy-start(bf16[192,768]{1,0:T(8,128)(2,1)} %copy-done.10) | copy-start | bytes 884740
  229.4 9.1 %copy-start.28 = (bf16[384,768]{1,0:T(8,128)(2,1)S(1)}, bf16[384,768]{1,0:T(8,128)(2,1)}, u32[]{:S(2)}) copy-start(bf16[384,768]{1,0:T(8,128)(2,1)} %copy-done.27) | copy-start | bytes 1769476
  231.4 52.4 %collective-permute-start.26 = (bf16[192,1536]{1,0:T(8,128)(2,1)}, bf16[192,1536]{1,0:T(8,128)(2,1)}, u32[]{:S(2)}, u32[]{:S(2)}) collective-permute-start(bf16[192,1536]{1,0:T(8,128)(2,1)} %pad_maximum_fusion.16), channel_id=1, source_target_pairs={{0,24},{4,28},{8,16},{12,20},{16,8},{20,12},{24,0},{28,4},{1,25},{... | collective-permute-start | bytes 1769480 | tf_op jit(solution)/shard_map/ppermute | solution.py:38
  237.0 46.8 %copy-start.21 = (s32[192]{0:T(256)S(1)}, s32[192]{0:T(256)}, u32[]{:S(2)}) copy-start(s32[192]{0:T(256)} %iota_add_fusion) | copy-start | bytes 2308
  237.0 48.4 %collective-permute-start.22 = (bf16[192,1536]{1,0:T(8,128)(2,1)}, bf16[192,1536]{1,0:T(8,128)(2,1)}, u32[]{:S(2)}, u32[]{:S(2)}) collective-permute-start(bf16[192,1536]{1,0:T(8,128)(2,1)} %pad_maximum_fusion.14), channel_id=1, source_target_pairs={{0,8},{4,12},{8,0},{12,4},{16,24},{20,28},{24,16},{28,20},{1,9},{5... | collective-permute-start | bytes 1769480 | tf_op jit(solution)/shard_map/ppermute | solution.py:38
  241.9 43.5 %copy-start.12 = (bf16[96,1536]{1,0:T(8,128)(2,1)S(1)}, bf16[96,1536]{1,0:T(8,128)(2,1)}, u32[]{:S(2)}) copy-start(bf16[96,1536]{1,0:T(8,128)(2,1)} %get-tuple-element.22) | copy-start | bytes 884740
  241.9 43.5 %copy-start.14 = (bf16[96,1536]{1,0:T(8,128)(2,1)S(1)}, bf16[96,1536]{1,0:T(8,128)(2,1)}, u32[]{:S(2)}) copy-start(bf16[96,1536]{1,0:T(8,128)(2,1)} %get-tuple-element.63) | copy-start | bytes 884740
  241.9 43.5 %copy-start.16 = (pred[192,256]{1,0:T(32,128)(4,1)S(1)}, pred[192,256]{1,0:T(32,128)(4,1)}, u32[]{:S(2)}) copy-start(pred[192,256]{1,0:T(32,128)(4,1)} %copy-done.15) | copy-start | bytes 147460
  241.9 43.5 %copy-start.18 = (pred[192,256]{1,0:T(32,128)(4,1)S(1)}, pred[192,256]{1,0:T(32,128)(4,1)}, u32[]{:S(2)}) copy-start(pred[192,256]{1,0:T(32,128)(4,1)} %copy-done.17) | copy-start | bytes 147460
  289.0 7.8 %collective-permute-start.27 = (bf16[256,384]{1,0:T(8,128)(2,1)S(1)}, bf16[256,384]{1,0:T(8,128)(2,1)S(1)}, u32[]{:S(2)}, u32[]{:S(2)}) collective-permute-start(bf16[256,384]{1,0:T(8,128)(2,1)S(1)} %get-tuple-element.39), channel_id=1, source_target_pairs={{0,1},{1,0},{2,3},{3,2},{4,5},{5,4},{6,7},{7,6},{8,9},{9,8},{10,11... | collective-permute-start | bytes 589832 | tf_op jit(solution)/shard_map/ppermute | solution.py:54
  290.6 10.8 %collective-permute-start.28 = (bf16[256,384]{1,0:T(8,128)(2,1)S(1)}, bf16[256,384]{1,0:T(8,128)(2,1)S(1)}, u32[]{:S(2)}, u32[]{:S(2)}) collective-permute-start(bf16[256,384]{1,0:T(8,128)(2,1)S(1)} %get-tuple-element.38), channel_id=1, source_target_pairs={{0,2},{1,3},{2,0},{3,1},{4,6},{5,7},{6,4},{7,5},{8,10},{9,11},{10,... | collective-permute-start | bytes 589832 | tf_op jit(solution)/shard_map/ppermute | solution.py:54
  291.1 10.2 %collective-permute-start.29 = (bf16[256,384]{1,0:T(8,128)(2,1)S(1)}, bf16[256,384]{1,0:T(8,128)(2,1)S(1)}, u32[]{:S(2)}, u32[]{:S(2)}) collective-permute-start(bf16[256,384]{1,0:T(8,128)(2,1)S(1)} %get-tuple-element.37), channel_id=1, source_target_pairs={{0,3},{1,2},{2,1},{3,0},{4,7},{5,6},{6,5},{7,4},{8,11},{9,10},{10,... | collective-permute-start | bytes 589832 | tf_op jit(solution)/shard_map/ppermute | solution.py:54
  (12 other events, 26.6 us)

commit v3 on v2

--- a/solution.py
+++ b/solution.py
@@ -24,6 +24,10 @@
 
 def dot(a, b, dims):
     return lax.dot_general(a, b, (dims, ((), ())), preferred_element_type=jnp.float32)
+
+
+def after(rows, *others):
+    return lax.optimization_barrier((rows,) + others)[0]
 
 
 def xor_pairs(size, k):
@@ -111,20 +115,26 @@
             parts.append(to_chip(pair, k))
         return jnp.concatenate(parts)
 
-    def collect(parts):
-        return sum(dot(p, r, ((0,), (0,))) for p, r in zip(placers, parts))
+    def collect(start, parts):
+        for place, rows in zip(placers[:-1], parts[:-1]):
+            start = start + dot(place, rows, ((0,), (0,)))
+        start = lax.optimization_barrier(start)
+        return start + dot(placers[-1], parts[-1], ((0,), (0,)))
 
     mixed = mix_heads(tokens.reshape(row_count, model_width))
     kept, parts = [], []
     for group, rows in zip(groups, dispatch(mixed)):
+        if parts:
+            rows = after(rows, gated)
         logits = lax.optimization_barrier(dot(rows, router_row, ((1,), (0,))))
         gate = jax.nn.sigmoid(jnp.sum(jnp.where(my_column, logits, 0.0), axis=1, keepdims=True))
         pre_act = dot(rows, weight_in, ((1,), (0,)))
         act = gelu_tanh(pre_act).astype(jnp.bfloat16)
         out = dot(act, weight_out, ((1,), (0,)))
-        kept.append((rows, gate, pre_act, act, out.astype(jnp.bfloat16)))
-        parts.append(give_back(group, (gate * out).astype(jnp.bfloat16)))
-    residual = mixed.astype(jnp.float32) + collect(parts)
+        kept.append((rows, gate, lax.optimization_barrier(pre_act), act, out.astype(jnp.bfloat16)))
+        gated = (gate * out).astype(jnp.bfloat16)
+        parts.append(give_back(group, gated))
+    residual = collect(mixed.astype(jnp.float32), parts)
     row_mean = jnp.mean(residual, axis=1, keepdims=True)
     centered = residual - row_mean
     row_var = jnp.mean(centered * centered, axis=1, keepdims=True)
@@ -140,10 +150,15 @@
         - normed * jnp.mean(grad_normed * normed, axis=1, keepdims=True)
     )
 
-    slopes = lax.optimization_barrier([gelu_slope(s[2]) for s in kept])
-    parts, pre_grads, out_grads, logit_grads = [], [], [], []
+    slopes = []
+    for saved in kept:
+        slopes.append(lax.optimization_barrier(gelu_slope(saved[2])))
+    router_parts = []
+    parts, pre_grads, out_grads = [], [], []
     arrived = dispatch(grad_resid.astype(jnp.bfloat16))
     for g, (group, grads, saved) in enumerate(zip(groups, arrived, kept)):
+        if parts:
+            grads = after(grads, back)
         rows, gate, pre_act, act, result = saved
         grads_f = grads.astype(jnp.float32)
         grad_out = (gate * grads_f).astype(jnp.bfloat16)
@@ -152,18 +167,19 @@
         grad_act = dot(grad_out, weight_out, ((1,), (1,)))
         grad_pre = (grad_act * slopes[g]).astype(jnp.bfloat16)
         grad_input = dot(grad_pre, weight_in, ((1,), (1,))) + grad_logit * router_mine[None, :]
-        parts.append(give_back(group, grad_input.astype(jnp.bfloat16)))
+        back = grad_input.astype(jnp.bfloat16)
+        parts.append(give_back(group, back))
+        part = jnp.sum(rows.astype(jnp.float32) * grad_logit, axis=0)
+        router_parts.append(lax.optimization_barrier(part))
         pre_grads.append(grad_pre)
         out_grads.append(grad_out)
-        logit_grads.append(grad_logit)
-    grad_mixed = grad_resid + collect(parts)
+    grad_mixed = collect(grad_resid, parts)
     grad_tokens = mix_heads(grad_mixed.astype(jnp.bfloat16))
 
     all_rows = jnp.concatenate([s[0] for s in kept])
     all_act = jnp.concatenate([s[3] for s in kept])
-    router_part = jnp.sum(all_rows.astype(jnp.float32) * jnp.concatenate(logit_grads), axis=0)
     lanes = 128
-    small = jnp.stack([router_part, grad_gain]).reshape(1, 2 * model_width // lanes, lanes)
+    small = jnp.stack([sum(router_parts), grad_gain]).reshape(1, 2 * model_width // lanes, lanes)
     small = exchange(jnp.broadcast_to(small, (experts,) + small.shape[1:]))
     small = small.reshape(experts, 2, model_width)
     grad_w_out = dot(all_act, jnp.concatenate(out_grads), ((0,), (0,))).astype(jnp.bfloat16)

time: 303 us -> 294 us (0.970)
  waiting for transfers between devices: 205 us -> 198 us
  local copies, waits for them, and re-layouts: 18.2 us -> 14.3 us
    ppermute x12, waiting for transfers between devices: 189 us -> 182 us  [to_chip(): lax.ppermute(rows, 'dp', xor_pairs(lax.axis_size('dp'), 2 * k))]
  transfers between devices with their start and end apart: 31 -> 31, of which waited for: 17 -> 14; matrix products, arithmetic and copies ran while one was open for 16% -> 16% of each run, Pallas kernels for 0% -> 0%
where the time goes in v3:
time: 294 us; the launch traced here: 293 us
  waiting for transfers between devices  198 us (67%)
  starting transfers between devices  35.1 us (12%)
  matrix products  28.1 us (10%)
  other arithmetic  15.8 us (5%)
  local copies, waits for them, and re-layouts  14.3 us (5%)
    ppermute x12, waiting for transfers between devices, to_chip(): lax.ppermute(rows, 'dp', xor_pairs(lax.axis_size('dp'), 2 * k))  182 us
    dot_general x29, matrix products, dot(): lax.dot_general(a, b, (dims, ((), ())), preferred_element_type=jnp.float32)  28.1 us
    ppermute x12, starting transfers between devices, to_chip(): lax.ppermute(rows, 'dp', xor_pairs(lax.axis_size('dp'), 2 * k))  18.1 us
    ppermute x6, waiting for transfers between devices, mix_heads(): lax.ppermute(piece, 'expert', xor_pairs(count, k))  13.6 us
    all_to_all x1, starting transfers between devices, exchange(): return lax.all_to_all(blocks, 'dp', split_axis=0, concat_axis=0, tiled=True)  7.27 us
    ppermute x6, starting transfers between devices, mix_heads(): lax.ppermute(piece, 'expert', xor_pairs(count, k))  7.04 us
  transfers between devices with their start and end apart: 31, of which 14 were waited for; matrix products, arithmetic and copies ran while one was open for 16% of the time, Pallas kernels for 0%

profile of v3, /device:TPU:16, one launch (start us, length us, event | category | flops | bytes accessed | tf_op | source)
XLA Modules:
  0.0 293.1 jit_solution(14052898752444993853)
XLA Ops:
  0.7 2.1 dynamic-slice_bitcast_fusion.12
  2.8 1.5 collective-permute-start
  4.3 1.5 collective-permute-start.1
  6.8 1.1 reduce-window.6
  8.9 1.9 collective-permute-done
  10.8 3.1 %collective-permute-done.1 = bf16[256,384]{1,0:T(8,128)(2,1)S(1)} collective-permute-done((bf16[256,384]{1,0:T(8,128)(2,1)S(1)}, bf16[256,384]{1,0:T(8,128)(2,1)S(1)}, u32[]{:S(2)}, u32[]{:S(2)}) %collective-permute-start.1) | collective-permute-done | bytes 196640 | tf_op jit(solution)/shard_map/ppermute | solution.py:58
  13.9 1.1 collective-permute-done.2
  15.0 1.0 pad_maximum_fusion.2
  17.4 3.6 %collective-permute-start.3 = (bf16[192,1536]{1,0:T(8,128)(2,1)S(1)}, bf16[192,1536]{1,0:T(8,128)(2,1)S(1)}, u32[]{:S(2)}, u32[]{:S(2)}) collective-permute-start(bf16[192,1536]{1,0:T(8,128)(2,1)S(1)} %convolution_convert_fusion.7), channel_id=1, source_target_pairs={{0,16},{4,20},{8,24},{12,28},{16,0},{20,4},{24,8},{28,12},{1,17},{... | collective-permute-start | bytes 1769480 | tf_op jit(solution)/shard_map/ppermute | solution.py:42
  21.6 36.4 %collective-permute-done.11 = bf16[192,1536]{1,0:T(8,128)(2,1)S(1)} collective-permute-done((bf16[192,1536]{1,0:T(8,128)(2,1)S(1)}, bf16[192,1536]{1,0:T(8,128)(2,1)S(1)}, u32[]{:S(2)}, u32[]{:S(2)}) %collective-permute-start.11) | collective-permute-done | bytes 589856 | tf_op jit(solution)/shard_map/ppermute | solution.py:42
  58.2 8.5 %collective-permute-done.3 = bf16[192,1536]{1,0:T(8,128)(2,1)S(1)} collective-permute-done((bf16[192,1536]{1,0:T(8,128)(2,1)S(1)}, bf16[192,1536]{1,0:T(8,128)(2,1)S(1)}, u32[]{:S(2)}, u32[]{:S(2)}) %collective-permute-start.3) | collective-permute-done | bytes 589856 | tf_op jit(solution)/shard_map/ppermute | solution.py:42
  67.5 0.9 collective-permute-done.4
  71.0 1.2 fusion.75
  72.8 1.1 multiply_convert_fusion
  76.2 3.4 %collective-permute-start.6 = (bf16[192,1536]{1,0:T(8,128)(2,1)S(1)}, bf16[192,1536]{1,0:T(8,128)(2,1)S(1)}, u32[]{:S(2)}, u32[]{:S(2)}) collective-permute-start(bf16[192,1536]{1,0:T(8,128)(2,1)S(1)} %pad_maximum_fusion.6), channel_id=1, source_target_pairs={{0,16},{4,20},{8,24},{12,28},{16,0},{20,4},{24,8},{28,12},{1,17},{... | collective-permute-start | bytes 1769480 | tf_op jit(solution)/shard_map/ppermute | solution.py:42
  79.8 1.6 collective-permute-start.14
  83.2 1.2 fusion.123
  84.4 59.5 %collective-permute-done.14 = bf16[192,1536]{1,0:T(8,128)(2,1)S(1)} collective-permute-done((bf16[192,1536]{1,0:T(8,128)(2,1)S(1)}, bf16[192,1536]{1,0:T(8,128)(2,1)S(1)}, u32[]{:S(2)}, u32[]{:S(2)}) %collective-permute-start.14) | collective-permute-done | bytes 589856 | tf_op jit(solution)/shard_map/ppermute | solution.py:42
  147.7 1.5 fusion.46
  150.2 1.6 collective-permute-start.23
  152.4 2.0 collective-permute-start.19
  154.4 24.8 %collective-permute-done.23 = bf16[192,1536]{1,0:T(8,128)(2,1)S(1)} collective-permute-done((bf16[192,1536]{1,0:T(8,128)(2,1)S(1)}, bf16[192,1536]{1,0:T(8,128)(2,1)S(1)}, u32[]{:S(2)}, u32[]{:S(2)}) %collective-permute-start.23) | collective-permute-done | bytes 589856 | tf_op jit(solution)/shard_map/ppermute | solution.py:42
  179.3 10.7 %collective-permute-done.15 = bf16[192,1536]{1,0:T(8,128)(2,1)S(1)} collective-permute-done((bf16[192,1536]{1,0:T(8,128)(2,1)S(1)}, bf16[192,1536]{1,0:T(8,128)(2,1)S(1)}, u32[]{:S(2)}, u32[]{:S(2)}) %collective-permute-start.15) | collective-permute-done | bytes 589856 | tf_op jit(solution)/shard_map/ppermute | solution.py:42
  190.7 0.9 collective-permute-done.16
  192.2 0.9 fusion.64
  193.2 0.9 fusion.5
  196.1 1.1 fusion.52
  197.3 1.1 fusion.2
  200.1 1.2 fusion.70
  202.5 1.3 broadcast_in_dim.66
  203.8 1.3 broadcast_in_dim.67
  205.2 7.3 %all-to-all-start = ((f32[8,24,128]{2,1,0:T(8,128)}), f32[8,24,128]{2,1,0:T(8,128)}, u32[]{:S(2)}, u32[]{:S(2)}) async-start(f32[8,24,128]{2,1,0:T(8,128)} %broadcast_in_dim.67), calls=%async_computation | async-start | bytes 196608 | tf_op jit(solution)/shard_map/all_to_all | solution.py:46
  212.4 2.3 fusion.61
  214.8 0.9 fusion.6
  216.5 3.5 %fusion = bf16[1,1,1536,768]{3,2,1,0:T(8,128)(2,1)} fusion(bf16[192,1536]{1,0:T(8,128)(2,1)S(1)} %copy-done.4, bf16[384,1536]{1,0:T(8,128)(2,1)S(1)} %pad_maximum_fusion, bf16[96,1536]{1,0:T(8,128)(2,1)S(1)} %copy-done.22, bf16[96,1536]{1,0:T(8,128)(2,1)S(1)} %copy-done.10, bf16[192,768]{1,0:T(8,128)(2,1)S(1)} %fusion.61, ...), kind=kOutput, calls=%fused_computation.3 | convolution fusion | flops 1826095104 | bytes 5898240 | tf_op jit(solution)/shard_map/dot_general | solution.py:26
  219.9 1.0 pad_maximum_fusion.12
  222.3 2.6 collective-permute-start.26
  226.5 1.4 collective-permute-start.22
  228.0 3.4 %fusion.1 = bf16[1,1,768,1536]{3,2,1,0:T(8,128)(2,1)} fusion(bf16[192,1536]{1,0:T(8,128)(2,1)S(1)} %copy-done.8, bf16[384,1536]{1,0:T(8,128)(2,1)S(1)} %copy-done.12, bf16[192,1536]{1,0:T(8,128)(2,1)S(1)} %copy-done.7, bf16[192,768]{1,0:T(8,128)(2,1)S(1)} %copy-done.20, bf16[384,768]{1,0:T(8,128)(2,1)S(1)} %copy-done.52, bf16[192,768]{1,0:T(8,128)(2,1)S(1)} %copy-done.18), kind=kOutput, calls=%fused_computation.4 | convolution fusion | flops 1823735808 | bytes 5898240 | tf_op jit(solution)/shard_map/dot_general | solution.py:26
  231.5 1.6 reshape.163
  233.1 42.2 %collective-permute-done.26 = bf16[192,1536]{1,0:T(8,128)(2,1)S(1)} collective-permute-done((bf16[192,1536]{1,0:T(8,128)(2,1)}, bf16[192,1536]{1,0:T(8,128)(2,1)S(1)}, u32[]{:S(2)}, u32[]{:S(2)}) %collective-permute-start.26) | collective-permute-done | bytes 589856 | tf_op jit(solution)/shard_map/ppermute | solution.py:42
  275.8 1.8 fusion.87
  277.7 1.6 fusion.3
  279.6 1.6 collective-permute-start.27
  281.7 1.4 collective-permute-start.29
  284.4 3.0 %collective-permute-done.27 = bf16[256,384]{1,0:T(8,128)(2,1)S(1)} collective-permute-done((bf16[256,384]{1,0:T(8,128)(2,1)S(1)}, bf16[256,384]{1,0:T(8,128)(2,1)S(1)}, u32[]{:S(2)}, u32[]{:S(2)}) %collective-permute-start.27) | collective-permute-done | bytes 196640 | tf_op jit(solution)/shard_map/ppermute | solution.py:58
  287.4 4.5 %collective-permute-done.28 = bf16[256,384]{1,0:T(8,128)(2,1)S(1)} collective-permute-done((bf16[256,384]{1,0:T(8,128)(2,1)S(1)}, bf16[256,384]{1,0:T(8,128)(2,1)S(1)}, u32[]{:S(2)}, u32[]{:S(2)}) %collective-permute-start.28) | collective-permute-done | bytes 196640 | tf_op jit(solution)/shard_map/ppermute | solution.py:58
  292.2 0.9 maximum_bitcast_fusion
  (244 shorter events, 29.9 us)
Async XLA Ops:
  0.6 68.9 %copy-start = (bf16[1,1,768,1536]{3,2,1,0:T(8,128)(2,1)S(1)}, bf16[1,1,768,1536]{3,2,1,0:T(8,128)(2,1)}, u32[]{:S(2)}) copy-start(bf16[1,1,768,1536]{3,2,1,0:T(8,128)(2,1)} %param.12) | copy-start | bytes 7077892
  0.7 8.0 %copy-start.27 = (bf16[1,1536,8]{1,2,0:T(8,128)(2,1)S(1)}, bf16[1,1536,8]{1,2,0:T(8,128)(2,1)}, u32[]{:S(2)}) copy-start(bf16[1,1536,8]{1,2,0:T(8,128)(2,1)} %param.9) | copy-start | bytes 73732
  2.8 8.0 %collective-permute-start = (bf16[256,384]{1,0:T(8,128)(2,1)}, bf16[256,384]{1,0:T(8,128)(2,1)S(1)}, u32[]{:S(2)}, u32[]{:S(2)}) collective-permute-start(bf16[256,384]{1,0:T(8,128)(2,1)} %get-tuple-element.44), channel_id=1, source_target_pairs={{0,1},{1,0},{2,3},{3,2},{4,5},{5,4},{6,7},{7,6},{8,9},{9,8},{10,11... | collective-permute-start | bytes 589832 | tf_op jit(solution)/shard_map/ppermute | solution.py:58
  4.3 9.6 %collective-permute-start.1 = (bf16[256,384]{1,0:T(8,128)(2,1)S(1)}, bf16[256,384]{1,0:T(8,128)(2,1)S(1)}, u32[]{:S(2)}, u32[]{:S(2)}) collective-permute-start(bf16[256,384]{1,0:T(8,128)(2,1)S(1)} %get-tuple-element.46), channel_id=1, source_target_pairs={{0,2},{1,3},{2,0},{3,1},{4,6},{5,7},{6,4},{7,5},{8,10},{9,11},{10,... | collective-permute-start | bytes 589832 | tf_op jit(solution)/shard_map/ppermute | solution.py:58
  5.9 9.2 %collective-permute-start.2 = (bf16[256,384]{1,0:T(8,128)(2,1)S(1)}, bf16[256,384]{1,0:T(8,128)(2,1)}, u32[]{:S(2)}, u32[]{:S(2)}) collective-permute-start(bf16[256,384]{1,0:T(8,128)(2,1)S(1)} %get-tuple-element.45), channel_id=1, source_target_pairs={{0,3},{1,2},{2,1},{3,0},{4,7},{5,6},{6,5},{7,4},{8,11},{9,10},{10,... | collective-permute-start | bytes 589832 | tf_op jit(solution)/shard_map/ppermute | solution.py:58
  6.8 9.4 %copy-start.33 = (s32[192]{0:T(256)}, s32[192]{0:T(256)S(1)}, u32[]{:S(2)}) copy-start(s32[192]{0:T(256)S(1)} %iota_add_fusion) | copy-start | bytes 2308
  6.8 10.3 %copy-start.36 = (s32[192]{0:T(256)}, s32[192]{0:T(256)S(1)}, u32[]{:S(2)}) copy-start(s32[192]{0:T(256)S(1)} %iota_add_fusion.2) | copy-start | bytes 2308
  8.6 60.0 %copy-start.40 = (pred[8]{0:T(512)(128)(4,1)}, pred[8]{0:T(512)(128)(4,1)S(1)}, u32[]{:S(2)}) copy-start(pred[8]{0:T(512)(128)(4,1)S(1)} %iota_compare_fusion.4) | copy-start | bytes 28
  8.8 188.5 %copy-start.42 = (f32[1536]{0:T(1024)}, f32[1536]{0:T(1024)S(1)}, u32[]{:S(2)}) copy-start(f32[1536]{0:T(1024)S(1)} %select_reduce_fusion) | copy-start | bytes 18436
  8.9 140.8 %copy-start.29 = (pred[192,256]{1,0:T(32,128)(4,1)}, pred[192,256]{1,0:T(32,128)(4,1)S(1)}, u32[]{:S(2)}) copy-start(pred[192,256]{1,0:T(32,128)(4,1)S(1)} %get-tuple-element.77) | copy-start | bytes 147460
  8.9 140.8 %copy-start.31 = (pred[192,256]{1,0:T(32,128)(4,1)}, pred[192,256]{1,0:T(32,128)(4,1)S(1)}, u32[]{:S(2)}) copy-start(pred[192,256]{1,0:T(32,128)(4,1)S(1)} %get-tuple-element.78) | copy-start | bytes 147460
  16.5 41.5 %collective-permute-start.11 = (bf16[192,1536]{1,0:T(8,128)(2,1)S(1)}, bf16[192,1536]{1,0:T(8,128)(2,1)S(1)}, u32[]{:S(2)}, u32[]{:S(2)}) collective-permute-start(bf16[192,1536]{1,0:T(8,128)(2,1)S(1)} %convolution_convert_fusion.6), channel_id=1, source_target_pairs={{0,24},{4,28},{8,16},{12,20},{16,8},{20,12},{24,0},{28,4},{1,25},{... | collective-permute-start | bytes 1769480 | tf_op jit(solution)/shard_map/ppermute | solution.py:42
  17.4 49.2 %collective-permute-start.3 = (bf16[192,1536]{1,0:T(8,128)(2,1)S(1)}, bf16[192,1536]{1,0:T(8,128)(2,1)S(1)}, u32[]{:S(2)}, u32[]{:S(2)}) collective-permute-start(bf16[192,1536]{1,0:T(8,128)(2,1)S(1)} %convolution_convert_fusion.7), channel_id=1, source_target_pairs={{0,16},{4,20},{8,24},{12,28},{16,0},{20,4},{24,8},{28,12},{1,17},{... | collective-permute-start | bytes 1769480 | tf_op jit(solution)/shard_map/ppermute | solution.py:42
  21.5 45.3 %collective-permute-start.7 = (bf16[192,1536]{1,0:T(8,128)(2,1)S(1)}, bf16[192,1536]{1,0:T(8,128)(2,1)S(1)}, u32[]{:S(2)}, u32[]{:S(2)}) collective-permute-start(bf16[192,1536]{1,0:T(8,128)(2,1)S(1)} %slice.188), channel_id=1, source_target_pairs={{0,8},{4,12},{8,0},{12,4},{16,24},{20,28},{24,16},{28,20},{1,9},{5... | collective-permute-start | bytes 1769480 | tf_op jit(solution)/shard_map/ppermute | solution.py:42
  58.1 12.7 %collective-permute-start.12 = (bf16[96,1536]{1,0:T(8,128)(2,1)S(1)}, bf16[96,1536]{1,0:T(8,128)(2,1)S(1)}, u32[]{:S(2)}, u32[]{:S(2)}) collective-permute-start(bf16[96,1536]{1,0:T(8,128)(2,1)S(1)} %get-tuple-element.66), channel_id=1, source_target_pairs={{0,4},{4,0},{8,12},{12,8},{16,20},{20,16},{24,28},{28,24},{1,5},{5... | collective-permute-start | bytes 884744 | tf_op jit(solution)/shard_map/ppermute | solution.py:38
  66.7 125.3 %copy-start.9 = (bf16[96,1536]{1,0:T(8,128)(2,1)}, bf16[96,1536]{1,0:T(8,128)(2,1)S(1)}, u32[]{:S(2)}) copy-start(bf16[96,1536]{1,0:T(8,128)(2,1)S(1)} %get-tuple-element.71) | copy-start | bytes 884740
  66.7 1.6 collective-permute-start.4
  66.9 4.0 %collective-permute-start.8 = (bf16[192,1536]{1,0:T(8,128)(2,1)S(1)}, bf16[192,1536]{1,0:T(8,128)(2,1)S(1)}, u32[]{:S(2)}, u32[]{:S(2)}) collective-permute-start(bf16[192,1536]{1,0:T(8,128)(2,1)S(1)} %pad_maximum_fusion.7), channel_id=1, source_target_pairs={{0,4},{4,0},{8,12},{12,8},{16,20},{20,16},{24,28},{28,24},{1,5},{5... | collective-permute-start | bytes 1769480 | tf_op jit(solution)/shard_map/ppermute | solution.py:38
  68.4 123.6 %copy-start.21 = (bf16[96,1536]{1,0:T(8,128)(2,1)}, bf16[96,1536]{1,0:T(8,128)(2,1)S(1)}, u32[]{:S(2)}) copy-start(bf16[96,1536]{1,0:T(8,128)(2,1)S(1)} %collective-permute-done.4) | copy-start | bytes 884740
  70.2 6.0 %collective-permute-start.5 = (bf16[96,1536]{1,0:T(8,128)(2,1)S(1)}, bf16[96,1536]{1,0:T(8,128)(2,1)S(1)}, u32[]{:S(2)}, u32[]{:S(2)}) collective-permute-start(bf16[96,1536]{1,0:T(8,128)(2,1)S(1)} %get-tuple-element.68), channel_id=1, source_target_pairs={{0,4},{4,0},{8,12},{12,8},{16,20},{20,16},{24,28},{28,24},{1,5},{5... | collective-permute-start | bytes 884744 | tf_op jit(solution)/shard_map/ppermute | solution.py:38
  70.9 130.4 %copy-start.3 = (bf16[192,1536]{1,0:T(8,128)(2,1)}, bf16[192,1536]{1,0:T(8,128)(2,1)S(1)}, u32[]{:S(2)}) copy-start(bf16[192,1536]{1,0:T(8,128)(2,1)S(1)} %pad_maximum_fusion.9) | copy-start | bytes 1769476
  75.8 4.0 %collective-permute-start.13 = (bf16[96,1536]{1,0:T(8,128)(2,1)S(1)}, bf16[96,1536]{1,0:T(8,128)(2,1)S(1)}, u32[]{:S(2)}, u32[]{:S(2)}) collective-permute-start(bf16[96,1536]{1,0:T(8,128)(2,1)S(1)} %get-tuple-element.64), channel_id=1, source_target_pairs={{0,4},{4,0},{8,12},{12,8},{16,20},{20,16},{24,28},{28,24},{1,5},{5... | collective-permute-start | bytes 884744 | tf_op jit(solution)/shard_map/ppermute | solution.py:38
  76.2 68.8 %collective-permute-start.6 = (bf16[192,1536]{1,0:T(8,128)(2,1)S(1)}, bf16[192,1536]{1,0:T(8,128)(2,1)S(1)}, u32[]{:S(2)}, u32[]{:S(2)}) collective-permute-start(bf16[192,1536]{1,0:T(8,128)(2,1)S(1)} %pad_maximum_fusion.6), channel_id=1, source_target_pairs={{0,16},{4,20},{8,24},{12,28},{16,0},{20,4},{24,8},{28,12},{1,17},{... | collective-permute-start | bytes 1769480 | tf_op jit(solution)/shard_map/ppermute | solution.py:42
  79.7 2.0 collective-permute-start.9
  79.8 64.1 %collective-permute-start.14 = (bf16[192,1536]{1,0:T(8,128)(2,1)S(1)}, bf16[192,1536]{1,0:T(8,128)(2,1)S(1)}, u32[]{:S(2)}, u32[]{:S(2)}) collective-permute-start(bf16[192,1536]{1,0:T(8,128)(2,1)S(1)} %pad_maximum_fusion.10), channel_id=1, source_target_pairs={{0,24},{4,28},{8,16},{12,20},{16,8},{20,12},{24,0},{28,4},{1,25},{... | collective-permute-start | bytes 1769480 | tf_op jit(solution)/shard_map/ppermute | solution.py:42
  81.8 62.1 %copy-start.34 = (s32[192]{0:T(256)S(1)}, s32[192]{0:T(256)}, u32[]{:S(2)}) copy-start(s32[192]{0:T(256)} %copy-done.33) | copy-start | bytes 2308
  81.8 62.6 %collective-permute-start.10 = (bf16[192,1536]{1,0:T(8,128)(2,1)S(1)}, bf16[192,1536]{1,0:T(8,128)(2,1)S(1)}, u32[]{:S(2)}, u32[]{:S(2)}) collective-permute-start(bf16[192,1536]{1,0:T(8,128)(2,1)S(1)} %pad_maximum_fusion.8), channel_id=1, source_target_pairs={{0,8},{4,12},{8,0},{12,4},{16,24},{20,28},{24,16},{28,20},{1,9},{5... | collective-permute-start | bytes 1769480 | tf_op jit(solution)/shard_map/ppermute | solution.py:42
  150.2 28.9 %collective-permute-start.23 = (bf16[192,1536]{1,0:T(8,128)(2,1)S(1)}, bf16[192,1536]{1,0:T(8,128)(2,1)S(1)}, u32[]{:S(2)}, u32[]{:S(2)}) collective-permute-start(bf16[192,1536]{1,0:T(8,128)(2,1)S(1)} %convolution_convert_fusion.4), channel_id=1, source_target_pairs={{0,24},{4,28},{8,16},{12,20},{16,8},{20,12},{24,0},{28,4},{1,25},{... | collective-permute-start | bytes 1769480 | tf_op jit(solution)/shard_map/ppermute | solution.py:42
  152.2 37.7 %collective-permute-start.15 = (bf16[192,1536]{1,0:T(8,128)(2,1)S(1)}, bf16[192,1536]{1,0:T(8,128)(2,1)S(1)}, u32[]{:S(2)}, u32[]{:S(2)}) collective-permute-start(bf16[192,1536]{1,0:T(8,128)(2,1)S(1)} %convolution_convert_fusion.5), channel_id=1, source_target_pairs={{0,16},{4,20},{8,24},{12,28},{16,0},{20,4},{24,8},{28,12},{1,17},{... | collective-permute-start | bytes 1769480 | tf_op jit(solution)/shard_map/ppermute | solution.py:42
  152.4 37.6 %collective-permute-start.19 = (bf16[192,1536]{1,0:T(8,128)(2,1)S(1)}, bf16[192,1536]{1,0:T(8,128)(2,1)S(1)}, u32[]{:S(2)}, u32[]{:S(2)}) collective-permute-start(bf16[192,1536]{1,0:T(8,128)(2,1)S(1)} %slice.206), channel_id=1, source_target_pairs={{0,8},{4,12},{8,0},{12,4},{16,24},{20,28},{24,16},{28,20},{1,9},{5... | collective-permute-start | bytes 1769480 | tf_op jit(solution)/shard_map/ppermute | solution.py:42
  179.2 15.9 %collective-permute-start.24 = (bf16[96,1536]{1,0:T(8,128)(2,1)S(1)}, bf16[96,1536]{1,0:T(8,128)(2,1)S(1)}, u32[]{:S(2)}, u32[]{:S(2)}) collective-permute-start(bf16[96,1536]{1,0:T(8,128)(2,1)S(1)} %get-tuple-element.52), channel_id=1, source_target_pairs={{0,4},{4,0},{8,12},{12,8},{16,20},{20,16},{24,28},{28,24},{1,5},{5... | collective-permute-start | bytes 884744 | tf_op jit(solution)/shard_map/ppermute | solution.py:38
  190.0 1.6 collective-permute-start.16
  190.2 5.0 %collective-permute-start.20 = (bf16[192,1536]{1,0:T(8,128)(2,1)S(1)}, bf16[192,1536]{1,0:T(8,128)(2,1)S(1)}, u32[]{:S(2)}, u32[]{:S(2)}) collective-permute-start(bf16[192,1536]{1,0:T(8,128)(2,1)S(1)} %pad_maximum_fusion.13), channel_id=1, source_target_pairs={{0,4},{4,0},{8,12},{12,8},{16,20},{20,16},{24,28},{28,24},{1,5},{5... | collective-permute-start | bytes 1769480 | tf_op jit(solution)/shard_map/ppermute | solution.py:38
  194.9 25.0 %collective-permute-start.17 = (bf16[96,1536]{1,0:T(8,128)(2,1)}, bf16[96,1536]{1,0:T(8,128)(2,1)}, u32[]{:S(2)}, u32[]{:S(2)}) collective-permute-start(bf16[96,1536]{1,0:T(8,128)(2,1)} %get-tuple-element.54), channel_id=1, source_target_pairs={{0,4},{4,0},{8,12},{12,8},{16,20},{20,16},{24,28},{28,24},{1,5},{5... | collective-permute-start | bytes 884744 | tf_op jit(solution)/shard_map/ppermute | solution.py:38
  205.2 26.3 %all-to-all-start = ((f32[8,24,128]{2,1,0:T(8,128)}), f32[8,24,128]{2,1,0:T(8,128)}, u32[]{:S(2)}, u32[]{:S(2)}) async-start(f32[8,24,128]{2,1,0:T(8,128)} %broadcast_in_dim.67), calls=%async_computation | async-start | bytes 196608 | tf_op jit(solution)/shard_map/all_to_all | solution.py:46
  215.8 5.6 %collective-permute-start.25 = (bf16[96,1536]{1,0:T(8,128)(2,1)S(1)}, bf16[96,1536]{1,0:T(8,128)(2,1)S(1)}, u32[]{:S(2)}, u32[]{:S(2)}) collective-permute-start(bf16[96,1536]{1,0:T(8,128)(2,1)S(1)} %get-tuple-element.48), channel_id=1, source_target_pairs={{0,4},{4,0},{8,12},{12,8},{16,20},{20,16},{24,28},{28,24},{1,5},{5... | collective-permute-start | bytes 884744 | tf_op jit(solution)/shard_map/ppermute | solution.py:38
  216.0 8.9 %collective-permute-start.21 = (bf16[192,1536]{1,0:T(8,128)(2,1)S(1)}, bf16[192,1536]{1,0:T(8,128)(2,1)S(1)}, u32[]{:S(2)}, u32[]{:S(2)}) collective-permute-start(bf16[192,1536]{1,0:T(8,128)(2,1)S(1)} %copy-done.15), channel_id=1, source_target_pairs={{0,4},{4,0},{8,12},{12,8},{16,20},{20,16},{24,28},{28,24},{1,5},{5... | collective-permute-start | bytes 1769480 | tf_op jit(solution)/shard_map/ppermute | solution.py:38
  221.0 56.6 %collective-permute-start.18 = (bf16[192,1536]{1,0:T(8,128)(2,1)S(1)}, bf16[192,1536]{1,0:T(8,128)(2,1)}, u32[]{:S(2)}, u32[]{:S(2)}) collective-permute-start(bf16[192,1536]{1,0:T(8,128)(2,1)S(1)} %pad_maximum_fusion.12), channel_id=1, source_target_pairs={{0,16},{4,20},{8,24},{12,28},{16,0},{20,4},{24,8},{28,12},{1,17},{... | collective-permute-start | bytes 1769480 | tf_op jit(solution)/shard_map/ppermute | solution.py:42
  222.3 52.9 %collective-permute-start.26 = (bf16[192,1536]{1,0:T(8,128)(2,1)}, bf16[192,1536]{1,0:T(8,128)(2,1)S(1)}, u32[]{:S(2)}, u32[]{:S(2)}) collective-permute-start(bf16[192,1536]{1,0:T(8,128)(2,1)} %pad_maximum_fusion.16), channel_id=1, source_target_pairs={{0,24},{4,28},{8,16},{12,20},{16,8},{20,12},{24,0},{28,4},{1,25},{... | collective-permute-start | bytes 1769480 | tf_op jit(solution)/shard_map/ppermute | solution.py:42
  226.5 48.7 %copy-start.35 = (s32[192]{0:T(256)S(1)}, s32[192]{0:T(256)}, u32[]{:S(2)}) copy-start(s32[192]{0:T(256)} %copy-done.33) | copy-start | bytes 2308
  226.5 49.2 %collective-permute-start.22 = (bf16[192,1536]{1,0:T(8,128)(2,1)}, bf16[192,1536]{1,0:T(8,128)(2,1)}, u32[]{:S(2)}, u32[]{:S(2)}) collective-permute-start(bf16[192,1536]{1,0:T(8,128)(2,1)} %pad_maximum_fusion.14), channel_id=1, source_target_pairs={{0,8},{4,12},{8,0},{12,4},{16,24},{20,28},{24,16},{28,20},{1,9},{5... | collective-permute-start | bytes 1769480 | tf_op jit(solution)/shard_map/ppermute | solution.py:42
  233.0 42.7 %copy-start.23 = (bf16[96,1536]{1,0:T(8,128)(2,1)S(1)}, bf16[96,1536]{1,0:T(8,128)(2,1)}, u32[]{:S(2)}) copy-start(bf16[96,1536]{1,0:T(8,128)(2,1)} %get-tuple-element.21) | copy-start | bytes 884740
  233.0 42.7 %copy-start.24 = (bf16[96,1536]{1,0:T(8,128)(2,1)S(1)}, bf16[96,1536]{1,0:T(8,128)(2,1)}, u32[]{:S(2)}) copy-start(bf16[96,1536]{1,0:T(8,128)(2,1)} %get-tuple-element.55) | copy-start | bytes 884740
  233.0 42.7 %copy-start.30 = (pred[192,256]{1,0:T(32,128)(4,1)S(1)}, pred[192,256]{1,0:T(32,128)(4,1)}, u32[]{:S(2)}) copy-start(pred[192,256]{1,0:T(32,128)(4,1)} %copy-done.29) | copy-start | bytes 147460
  233.0 42.7 %copy-start.32 = (pred[192,256]{1,0:T(32,128)(4,1)S(1)}, pred[192,256]{1,0:T(32,128)(4,1)}, u32[]{:S(2)}) copy-start(pred[192,256]{1,0:T(32,128)(4,1)} %copy-done.31) | copy-start | bytes 147460
  279.6 7.8 %collective-permute-start.27 = (bf16[256,384]{1,0:T(8,128)(2,1)S(1)}, bf16[256,384]{1,0:T(8,128)(2,1)S(1)}, u32[]{:S(2)}, u32[]{:S(2)}) collective-permute-start(bf16[256,384]{1,0:T(8,128)(2,1)S(1)} %get-tuple-element.38), channel_id=1, source_target_pairs={{0,1},{1,0},{2,3},{3,2},{4,5},{5,4},{6,7},{7,6},{8,9},{9,8},{10,11... | collective-permute-start | bytes 589832 | tf_op jit(solution)/shard_map/ppermute | solution.py:58
  281.2 10.8 %collective-permute-start.28 = (bf16[256,384]{1,0:T(8,128)(2,1)S(1)}, bf16[256,384]{1,0:T(8,128)(2,1)S(1)}, u32[]{:S(2)}, u32[]{:S(2)}) collective-permute-start(bf16[256,384]{1,0:T(8,128)(2,1)S(1)} %get-tuple-element.37), channel_id=1, source_target_pairs={{0,2},{1,3},{2,0},{3,1},{4,6},{5,7},{6,4},{7,5},{8,10},{9,11},{10,... | collective-permute-start | bytes 589832 | tf_op jit(solution)/shard_map/ppermute | solution.py:58
  281.7 10.2 %collective-permute-start.29 = (bf16[256,384]{1,0:T(8,128)(2,1)S(1)}, bf16[256,384]{1,0:T(8,128)(2,1)S(1)}, u32[]{:S(2)}, u32[]{:S(2)}) collective-permute-start(bf16[256,384]{1,0:T(8,128)(2,1)S(1)} %get-tuple-element.36), channel_id=1, source_target_pairs={{0,3},{1,2},{2,1},{3,0},{4,7},{5,6},{6,5},{7,4},{8,11},{9,10},{10,... | collective-permute-start | bytes 589832 | tf_op jit(solution)/shard_map/ppermute | solution.py:58
  (36 other events, 104.9 us)

commit v4 on v3

--- a/solution.py
+++ b/solution.py
@@ -46,20 +46,47 @@
     return lax.all_to_all(blocks, "dp", split_axis=0, concat_axis=0, tiled=True)
 
 
-def mix_heads(rows):
+def can_split(width):
+    count = lax.axis_size("expert")
+    return (width // count) % 128 == 0 and count & (count - 1) == 0
+
+
+def blocks_of(rows, width):
+    count = lax.axis_size("expert")
+    head = width // count
+    mine = lax.axis_index("expert")
+    return [lax.dynamic_slice_in_dim(rows, (mine ^ k) * head, head, 1) for k in range(count)]
+
+
+def in_order(pieces):
     count = lax.axis_size("expert")
     mine = lax.axis_index("expert")
-    head = rows.shape[1] // count
-    if head % 128 or count & (count - 1):
+    blocks = []
+    for t in range(count):
+        block = pieces[0]
+        for k in range(1, count):
+            block = jnp.where(mine ^ t == k, pieces[k], block)
+        blocks.append(block)
+    return jnp.concatenate(blocks, axis=1)
+
+
+def cut(rows, width):
+    head = width // lax.axis_size("expert")
+    return [rows[:, i : i + head] for i in range(0, rows.shape[1], head)]
+
+
+def swap_heads(pieces):
+    moved = []
+    for k, piece in enumerate(pieces):
+        pairs = xor_pairs(lax.axis_size("expert"), k)
+        moved.append(lax.ppermute(piece, "expert", pairs) if k else piece)
+    return moved
+
+
+def mix_heads(rows):
+    if not can_split(rows.shape[1]):
         return lax.all_to_all(rows, "expert", split_axis=1, concat_axis=1, tiled=True)
-    pieces = []
-    for k in range(count):
-        piece = lax.dynamic_slice_in_dim(rows, (mine ^ k) * head, head, 1)
-        pieces.append(lax.ppermute(piece, "expert", xor_pairs(count, k)) if k else piece)
-    stacked = jnp.stack(pieces)
-    return jnp.concatenate(
-        [lax.dynamic_index_in_dim(stacked, mine ^ t, 0, False) for t in range(count)], axis=1
-    )
+    return in_order(swap_heads(blocks_of(rows, rows.shape[1])))
 
 
 def body(tokens, route_ids, router, norm_gain, w_in, w_out, cotangent):
@@ -96,10 +123,21 @@
     my_column = lax.broadcasted_iota(jnp.int32, (1, experts), 1) == me
     router_mine = jnp.sum(jnp.where(my_column, router_row.astype(jnp.float32), 0.0), axis=1)
 
-    def dispatch(rows):
+    def slots_of(placer, rows):
+        return dot(placer, rows, ((1,), (0,))).astype(jnp.bfloat16)
+
+    def dispatch(rows, pieces=None):
         arrived = []
-        for group, placer in zip(groups, placers):
-            slots = dot(placer, rows, ((1,), (0,))).astype(jnp.bfloat16)
+        if pieces is not None:
+            early = to_chip(slots_of(placers[0], pieces[0]), groups[0][0])
+            rest = jnp.concatenate(pieces[1:], axis=1)
+        for i, (group, placer) in enumerate(zip(groups, placers)):
+            if pieces is not None and i == 0:
+                late = to_chip(slots_of(placer, rest), group[0])
+                whole = in_order([early] + cut(late, model_width))
+                arrived.append(jnp.concatenate([whole[:depth], swap_cores(whole[depth:])]))
+                continue
+            slots = slots_of(placer, rows)
             parts = [to_chip(slots[2 * depth * i : 2 * depth * (i + 1)], k) for i, k in enumerate(group)]
             mine = jnp.concatenate([p[:depth] for p in parts])
             others = jnp.concatenate([p[depth:] for p in parts])
@@ -115,15 +153,26 @@
             parts.append(to_chip(pair, k))
         return jnp.concatenate(parts)
 
-    def collect(start, parts):
+    def partial_sum(start, parts):
         for place, rows in zip(placers[:-1], parts[:-1]):
             start = start + dot(place, rows, ((0,), (0,)))
-        start = lax.optimization_barrier(start)
+        return lax.optimization_barrier(start)
+
+    def collect(start, parts):
+        start = partial_sum(start, parts)
         return start + dot(placers[-1], parts[-1], ((0,), (0,)))
 
-    mixed = mix_heads(tokens.reshape(row_count, model_width))
+    own_rows = tokens.reshape(row_count, model_width)
+    split = can_split(model_width)
+    if split:
+        pieces = swap_heads(blocks_of(own_rows, model_width))
+        mixed = in_order(pieces)
+    else:
+        pieces, mixed = None, mix_heads(own_rows)
+    cot_f = cotangent.reshape(row_count, model_width).astype(jnp.float32)
+    mean_grad = lax.optimization_barrier(jnp.mean(cot_f * gain_row[None, :], axis=1, keepdims=True))
     kept, parts = [], []
-    for group, rows in zip(groups, dispatch(mixed)):
+    for group, rows in zip(groups, dispatch(mixed, pieces)):
         if parts:
             rows = after(rows, gated)
         logits = lax.optimization_barrier(dot(rows, router_row, ((1,), (0,))))
@@ -141,12 +190,11 @@
     inv_std = lax.rsqrt(row_var + norm_eps)
     normed = centered * inv_std
     normed_out = (normed * gain_row[None, :]).astype(jnp.bfloat16)
-    cot_f = cotangent.reshape(row_count, model_width).astype(jnp.float32)
     grad_gain = jnp.sum(cot_f * normed, axis=0)
     grad_normed = cot_f * gain_row[None, :]
     grad_resid = inv_std * (
         grad_normed
-        - jnp.mean(grad_normed, axis=1, keepdims=True)
+        - mean_grad
         - normed * jnp.mean(grad_normed * normed, axis=1, keepdims=True)
     )
 
@@ -168,13 +216,25 @@
         grad_pre = (grad_act * slopes[g]).astype(jnp.bfloat16)
         grad_input = dot(grad_pre, weight_in, ((1,), (1,))) + grad_logit * router_mine[None, :]
         back = grad_input.astype(jnp.bfloat16)
-        parts.append(give_back(group, back))
+        if split and g == len(groups) - 1:
+            pair = jnp.concatenate([back[:depth], swap_cores(back[depth:])])
+            own_block, *others = blocks_of(pair, model_width)
+            parts.append(to_chip(jnp.concatenate(others, axis=1), group[0]))
+            last_block = to_chip(own_block, group[0])
+        else:
+            parts.append(give_back(group, back))
         part = jnp.sum(rows.astype(jnp.float32) * grad_logit, axis=0)
         router_parts.append(lax.optimization_barrier(part))
         pre_grads.append(grad_pre)
         out_grads.append(grad_out)
-    grad_mixed = collect(grad_resid, parts)
-    grad_tokens = mix_heads(grad_mixed.astype(jnp.bfloat16))
+    if split:
+        start, *others = blocks_of(partial_sum(grad_resid, parts), model_width)
+        main = jnp.concatenate(others, axis=1) + dot(placers[-1], parts[-1], ((0,), (0,)))
+        main = main.astype(jnp.bfloat16)
+        start = (start + dot(placers[-1], last_block, ((0,), (0,)))).astype(jnp.bfloat16)
+        grad_tokens = in_order(swap_heads([start] + cut(main, model_width)))
+    else:
+        grad_tokens = mix_heads(collect(grad_resid, parts).astype(jnp.bfloat16))
 
     all_rows = jnp.concatenate([s[0] for s in kept])
     all_act = jnp.concatenate([s[3] for s in kept])

time: 294 us -> 279 us (0.949)
  the two profiles are of different devices: /device:TPU:16 before, /device:TPU:0 now
where the time goes in v4:
time: 279 us; the launch traced here: 276 us
  waiting for transfers between devices  164 us (59%)
  starting transfers between devices  49.2 us (18%)
  matrix products  30.4 us (11%)
  local copies, waits for them, and re-layouts  15.7 us (6%)
  other arithmetic  14.7 us (5%)
    ppermute x14, waiting for transfers between devices, to_chip(): lax.ppermute(rows, 'dp', xor_pairs(lax.axis_size('dp'), 2 * k))  147 us
    ppermute x14, starting transfers between devices, to_chip(): lax.ppermute(rows, 'dp', xor_pairs(lax.axis_size('dp'), 2 * k))  35.3 us
    dot_general x31, matrix products, dot(): lax.dot_general(a, b, (dims, ((), ())), preferred_element_type=jnp.float32)  30.4 us
    ppermute x6, waiting for transfers between devices, swap_heads(): moved.append(lax.ppermute(piece, 'expert', pairs) if k else piece)  15.3 us
    ppermute x6, starting transfers between devices, swap_heads(): moved.append(lax.ppermute(piece, 'expert', pairs) if k else piece)  7.04 us
  transfers between devices with their start and end apart: 33, of which 17 were waited for; matrix products, arithmetic and copies ran while one was open for 17% of the time, Pallas kernels for 0%

profile of v4, /device:TPU:0, one launch (start us, length us, event | category | flops | bytes accessed | tf_op | source)
XLA Modules:
  0.0 276.4 jit_solution(2635634462494413473)
XLA Ops:
  0.7 1.0 copy.19
  2.0 1.1 reduce-window.6
  4.4 1.8 convolution_convert_fusion.8
  6.3 4.1 %collective-permute-start.4 = (bf16[192,384]{1,0:T(8,128)(2,1)}, bf16[192,384]{1,0:T(8,128)(2,1)S(1)}, u32[]{:S(2)}, u32[]{:S(2)}) collective-permute-start(bf16[192,384]{1,0:T(8,128)(2,1)} %convolution_convert_fusion.8), channel_id=1, source_target_pairs={{0,16},{4,20},{8,24},{12,28},{16,0},{20,4},{24,8},{28,12},{1,17},{... | collective-permute-start | bytes 442376 | tf_op jit(solution)/shard_map/ppermute | solution.py:42
  11.1 2.4 collective-permute-start
  14.9 5.2 %collective-permute-done = bf16[256,384]{1,0:T(8,128)(2,1)} collective-permute-done((bf16[256,384]{1,0:T(8,128)(2,1)}, bf16[256,384]{1,0:T(8,128)(2,1)}, u32[]{:S(2)}, u32[]{:S(2)}) %collective-permute-start) | collective-permute-done | bytes 196640 | tf_op jit(solution)/shard_map/ppermute | solution.py:82
  20.1 2.8 %collective-permute-done.1 = bf16[256,384]{1,0:T(8,128)(2,1)} collective-permute-done((bf16[256,384]{1,0:T(8,128)(2,1)}, bf16[256,384]{1,0:T(8,128)(2,1)}, u32[]{:S(2)}, u32[]{:S(2)}) %collective-permute-start.1) | collective-permute-done | bytes 196640 | tf_op jit(solution)/shard_map/ppermute | solution.py:82
  23.0 1.5 convolution_convert_fusion.7
  24.9 1.4 fusion.133
  26.8 1.6 collective-permute-start.8
  28.8 2.6 collective-permute-start.12
  31.4 16.6 %collective-permute-done.3 = bf16[192,1152]{1,0:T(8,128)(2,1)S(1)} collective-permute-done((bf16[192,1152]{1,0:T(8,128)(2,1)S(1)}, bf16[192,1152]{1,0:T(8,128)(2,1)S(1)}, u32[]{:S(2)}, u32[]{:S(2)}) %collective-permute-start.3) | collective-permute-done | bytes 442400 | tf_op jit(solution)/shard_map/ppermute | solution.py:42
  48.3 1.8 collective-permute-done.8
  50.3 13.6 %collective-permute-done.12 = bf16[192,1536]{1,0:T(8,128)(2,1)S(1)} collective-permute-done((bf16[192,1536]{1,0:T(8,128)(2,1)S(1)}, bf16[192,1536]{1,0:T(8,128)(2,1)S(1)}, u32[]{:S(2)}, u32[]{:S(2)}) %collective-permute-start.12) | collective-permute-done | bytes 589856 | tf_op jit(solution)/shard_map/ppermute | solution.py:42
  67.7 8.7 %collective-permute-start.7 = (bf16[192,1536]{1,0:T(8,128)(2,1)S(1)}, bf16[192,1536]{1,0:T(8,128)(2,1)S(1)}, u32[]{:S(2)}, u32[]{:S(2)}) collective-permute-start(bf16[192,1536]{1,0:T(8,128)(2,1)S(1)} %pad_maximum_fusion.5), channel_id=1, source_target_pairs={{0,16},{4,20},{8,24},{12,28},{16,0},{20,4},{24,8},{28,12},{1,17},{... | collective-permute-start | bytes 1769480 | tf_op jit(solution)/shard_map/ppermute | solution.py:42
  76.9 1.3 fusion.75
  78.3 1.1 multiply_convert_fusion
  83.2 2.7 collective-permute-start.15
  86.5 29.4 %collective-permute-done.7 = bf16[192,1536]{1,0:T(8,128)(2,1)S(1)} collective-permute-done((bf16[192,1536]{1,0:T(8,128)(2,1)S(1)}, bf16[192,1536]{1,0:T(8,128)(2,1)S(1)}, u32[]{:S(2)}, u32[]{:S(2)}) %collective-permute-start.7) | collective-permute-done | bytes 589856 | tf_op jit(solution)/shard_map/ppermute | solution.py:42
  116.9 7.3 %collective-permute-done.11 = bf16[192,1536]{1,0:T(8,128)(2,1)S(1)} collective-permute-done((bf16[192,1536]{1,0:T(8,128)(2,1)S(1)}, bf16[192,1536]{1,0:T(8,128)(2,1)S(1)}, u32[]{:S(2)}, u32[]{:S(2)}) %collective-permute-start.11) | collective-permute-done | bytes 589856 | tf_op jit(solution)/shard_map/ppermute | solution.py:42
  127.0 1.6 fusion.46
  129.5 2.7 collective-permute-start.24
  132.6 4.0 %collective-permute-start.16 = (bf16[192,1536]{1,0:T(8,128)(2,1)S(1)}, bf16[192,1536]{1,0:T(8,128)(2,1)S(1)}, u32[]{:S(2)}, u32[]{:S(2)}) collective-permute-start(bf16[192,1536]{1,0:T(8,128)(2,1)S(1)} %convolution_convert_fusion.5), channel_id=1, source_target_pairs={{0,16},{4,20},{8,24},{12,28},{16,0},{20,4},{24,8},{28,12},{1,17},{... | collective-permute-start | bytes 1769480 | tf_op jit(solution)/shard_map/ppermute | solution.py:42
  137.0 10.7 %collective-permute-done.24 = bf16[192,1536]{1,0:T(8,128)(2,1)S(1)} collective-permute-done((bf16[192,1536]{1,0:T(8,128)(2,1)S(1)}, bf16[192,1536]{1,0:T(8,128)(2,1)S(1)}, u32[]{:S(2)}, u32[]{:S(2)}) %collective-permute-start.24) | collective-permute-done | bytes 589856 | tf_op jit(solution)/shard_map/ppermute | solution.py:42
  147.8 35.9 %collective-permute-done.16 = bf16[192,1536]{1,0:T(8,128)(2,1)S(1)} collective-permute-done((bf16[192,1536]{1,0:T(8,128)(2,1)S(1)}, bf16[192,1536]{1,0:T(8,128)(2,1)S(1)}, u32[]{:S(2)}, u32[]{:S(2)}) %collective-permute-start.16) | collective-permute-done | bytes 589856 | tf_op jit(solution)/shard_map/ppermute | solution.py:42
  187.7 0.9 fusion.175
  189.7 1.1 fusion.52
  190.8 1.1 fusion.2
  195.5 0.9 fusion.6
  198.4 1.3 broadcast_in_dim.66
  199.8 1.4 broadcast_in_dim.67
  201.1 4.2 %all-to-all-start = ((f32[8,24,128]{2,1,0:T(8,128)}), f32[8,24,128]{2,1,0:T(8,128)}, u32[]{:S(2)}, u32[]{:S(2)}) async-start(f32[8,24,128]{2,1,0:T(8,128)} %broadcast_in_dim.67), calls=%async_computation | async-start | bytes 196608 | tf_op jit(solution)/shard_map/all_to_all | solution.py:46
  205.4 5.2 %fusion = bf16[1,1,1536,768]{3,2,1,0:T(8,128)(2,1)} fusion(bf16[192,1536]{1,0:T(8,128)(2,1)} %copy-done.3, bf16[384,1536]{1,0:T(8,128)(2,1)S(1)} %pad_maximum_fusion, bf16[96,1536]{1,0:T(8,128)(2,1)} %copy-done.21, bf16[96,1536]{1,0:T(8,128)(2,1)} %copy-done.9, bf16[192,768]{1,0:T(8,128)(2,1)} %copy-done.24, bf16[384,768]{1,0:T(8,128)(2,1)} %copy-done.41, ...), kind=kOutput, calls=%fused_computation.3 | convolution fusion | flops 1826095104 | bytes 5898240 | tf_op jit(solution)/shard_map/dot_general | solution.py:26
  210.6 3.4 %fusion.1 = bf16[1,1,768,1536]{3,2,1,0:T(8,128)(2,1)} fusion(bf16[192,1536]{1,0:T(8,128)(2,1)S(1)} %copy-done.8, bf16[384,1536]{1,0:T(8,128)(2,1)S(1)} %copy-done.11, bf16[192,1536]{1,0:T(8,128)(2,1)S(1)} %copy-done.6, bf16[192,768]{1,0:T(8,128)(2,1)S(1)} %copy-done.20, bf16[384,768]{1,0:T(8,128)(2,1)S(1)} %copy-done.43, bf16[192,768]{1,0:T(8,128)(2,1)S(1)} %copy-done.18), kind=kOutput, calls=%fused_computation.4 | convolution fusion | flops 1823735808 | bytes 5898240 | tf_op jit(solution)/shard_map/dot_general | solution.py:26
  214.1 1.0 pad_maximum_fusion.11
  215.1 2.7 collective-permute-start.19
  217.8 1.6 reshape.168
  219.4 1.1 fusion.176
  220.6 1.5 collective-permute-start.23
  223.4 1.1 fusion.142
  224.9 3.5 %collective-permute-start.31 = (bf16[192,384]{1,0:T(8,128)(2,1)S(1)}, bf16[192,384]{1,0:T(8,128)(2,1)S(1)}, u32[]{:S(2)}, u32[]{:S(2)}) collective-permute-start(bf16[192,384]{1,0:T(8,128)(2,1)S(1)} %get-tuple-element.45), channel_id=1, source_target_pairs={{0,24},{4,28},{8,16},{12,20},{16,8},{20,12},{24,0},{28,4},{1,25},{... | collective-permute-start | bytes 442376 | tf_op jit(solution)/shard_map/ppermute | solution.py:42
  228.4 31.5 %collective-permute-done.23 = bf16[192,1536]{1,0:T(8,128)(2,1)S(1)} collective-permute-done((bf16[192,1536]{1,0:T(8,128)(2,1)S(1)}, bf16[192,1536]{1,0:T(8,128)(2,1)S(1)}, u32[]{:S(2)}, u32[]{:S(2)}) %collective-permute-start.23) | collective-permute-done | bytes 589856 | tf_op jit(solution)/shard_map/ppermute | solution.py:42
  261.4 1.6 fusion.3
  264.2 1.1 collective-permute-start.28
  265.3 2.0 collective-permute-start.29
  268.1 4.8 %collective-permute-done.28 = bf16[256,384]{1,0:T(8,128)(2,1)S(1)} collective-permute-done((bf16[256,384]{1,0:T(8,128)(2,1)S(1)}, bf16[256,384]{1,0:T(8,128)(2,1)S(1)}, u32[]{:S(2)}, u32[]{:S(2)}) %collective-permute-start.28) | collective-permute-done | bytes 196640 | tf_op jit(solution)/shard_map/ppermute | solution.py:82
  272.9 2.2 collective-permute-done.29
  275.5 0.9 maximum_bitcast_fusion
  (234 shorter events, 35.4 us)
Async XLA Ops:
  0.6 64.5 %copy-start = (bf16[1,1,768,1536]{3,2,1,0:T(8,128)(2,1)S(1)}, bf16[1,1,768,1536]{3,2,1,0:T(8,128)(2,1)}, u32[]{:S(2)}) copy-start(bf16[1,1,768,1536]{3,2,1,0:T(8,128)(2,1)} %param.12) | copy-start | bytes 7077892
  0.7 14.0 %copy-start.25 = (bf16[1,1536,8]{1,2,0:T(8,128)(2,1)S(1)}, bf16[1,1536,8]{1,2,0:T(8,128)(2,1)}, u32[]{:S(2)}) copy-start(bf16[1,1536,8]{1,2,0:T(8,128)(2,1)} %param.9) | copy-start | bytes 73732
  2.0 22.5 %copy-start.34 = (s32[192]{0:T(256)}, s32[192]{0:T(256)S(1)}, u32[]{:S(2)}) copy-start(s32[192]{0:T(256)S(1)} %iota_add_fusion.2) | copy-start | bytes 2308
  6.3 25.1 %collective-permute-start.4 = (bf16[192,384]{1,0:T(8,128)(2,1)}, bf16[192,384]{1,0:T(8,128)(2,1)S(1)}, u32[]{:S(2)}, u32[]{:S(2)}) collective-permute-start(bf16[192,384]{1,0:T(8,128)(2,1)} %convolution_convert_fusion.8), channel_id=1, source_target_pairs={{0,16},{4,20},{8,24},{12,28},{16,0},{20,4},{24,8},{28,12},{1,17},{... | collective-permute-start | bytes 442376 | tf_op jit(solution)/shard_map/ppermute | solution.py:42
  11.1 9.0 %collective-permute-start = (bf16[256,384]{1,0:T(8,128)(2,1)}, bf16[256,384]{1,0:T(8,128)(2,1)}, u32[]{:S(2)}, u32[]{:S(2)}) collective-permute-start(bf16[256,384]{1,0:T(8,128)(2,1)} %get-tuple-element.44), channel_id=1, source_target_pairs={{0,3},{1,2},{2,1},{3,0},{4,7},{5,6},{6,5},{7,4},{8,11},{9,10},{10,... | collective-permute-start | bytes 589832 | tf_op jit(solution)/shard_map/ppermute | solution.py:82
  13.6 9.3 %collective-permute-start.1 = (bf16[256,384]{1,0:T(8,128)(2,1)}, bf16[256,384]{1,0:T(8,128)(2,1)}, u32[]{:S(2)}, u32[]{:S(2)}) collective-permute-start(bf16[256,384]{1,0:T(8,128)(2,1)} %get-tuple-element.43), channel_id=1, source_target_pairs={{0,2},{1,3},{2,0},{3,1},{4,6},{5,7},{6,4},{7,5},{8,10},{9,11},{10,... | collective-permute-start | bytes 589832 | tf_op jit(solution)/shard_map/ppermute | solution.py:82
  14.1 8.9 %collective-permute-start.2 = (bf16[256,384]{1,0:T(8,128)(2,1)S(1)}, bf16[256,384]{1,0:T(8,128)(2,1)}, u32[]{:S(2)}, u32[]{:S(2)}) collective-permute-start(bf16[256,384]{1,0:T(8,128)(2,1)S(1)} %get-tuple-element.42), channel_id=1, source_target_pairs={{0,1},{1,0},{2,3},{3,2},{4,5},{5,4},{6,7},{7,6},{8,9},{9,8},{10,11... | collective-permute-start | bytes 589832 | tf_op jit(solution)/shard_map/ppermute | solution.py:82
  14.6 49.6 %copy-start.37 = (pred[8]{0:T(512)(128)(4,1)}, pred[8]{0:T(512)(128)(4,1)S(1)}, u32[]{:S(2)}) copy-start(pred[8]{0:T(512)(128)(4,1)S(1)} %iota_compare_fusion.4) | copy-start | bytes 28
  14.9 114.1 %copy-start.27 = (pred[192,256]{1,0:T(32,128)(4,1)}, pred[192,256]{1,0:T(32,128)(4,1)S(1)}, u32[]{:S(2)}) copy-start(pred[192,256]{1,0:T(32,128)(4,1)S(1)} %get-tuple-element.85) | copy-start | bytes 147460
  14.9 114.1 %copy-start.29 = (pred[192,256]{1,0:T(32,128)(4,1)}, pred[192,256]{1,0:T(32,128)(4,1)S(1)}, u32[]{:S(2)}) copy-start(pred[192,256]{1,0:T(32,128)(4,1)S(1)} %get-tuple-element.86) | copy-start | bytes 147460
  24.5 23.5 %collective-permute-start.3 = (bf16[192,1152]{1,0:T(8,128)(2,1)S(1)}, bf16[192,1152]{1,0:T(8,128)(2,1)S(1)}, u32[]{:S(2)}, u32[]{:S(2)}) collective-permute-start(bf16[192,1152]{1,0:T(8,128)(2,1)S(1)} %convolution_convert_fusion.7), channel_id=1, source_target_pairs={{0,16},{4,20},{8,24},{12,28},{16,0},{20,4},{24,8},{28,12},{1,17},{... | collective-permute-start | bytes 1327112 | tf_op jit(solution)/shard_map/ppermute | solution.py:42
  26.8 23.3 %collective-permute-start.8 = (bf16[192,1536]{1,0:T(8,128)(2,1)S(1)}, bf16[192,1536]{1,0:T(8,128)(2,1)S(1)}, u32[]{:S(2)}, u32[]{:S(2)}) collective-permute-start(bf16[192,1536]{1,0:T(8,128)(2,1)S(1)} %slice.215), channel_id=1, source_target_pairs={{0,8},{4,12},{8,0},{12,4},{16,24},{20,28},{24,16},{28,20},{1,9},{5... | collective-permute-start | bytes 1769480 | tf_op jit(solution)/shard_map/ppermute | solution.py:42
  28.8 35.1 %collective-permute-start.12 = (bf16[192,1536]{1,0:T(8,128)(2,1)S(1)}, bf16[192,1536]{1,0:T(8,128)(2,1)S(1)}, u32[]{:S(2)}, u32[]{:S(2)}) collective-permute-start(bf16[192,1536]{1,0:T(8,128)(2,1)S(1)} %convolution_convert_fusion.6), channel_id=1, source_target_pairs={{0,24},{4,28},{8,16},{12,20},{16,8},{20,12},{24,0},{28,4},{1,25},{... | collective-permute-start | bytes 1769480 | tf_op jit(solution)/shard_map/ppermute | solution.py:42
  48.3 140.5 %copy-start.9 = (bf16[96,1536]{1,0:T(8,128)(2,1)}, bf16[96,1536]{1,0:T(8,128)(2,1)S(1)}, u32[]{:S(2)}) copy-start(bf16[96,1536]{1,0:T(8,128)(2,1)S(1)} %get-tuple-element.78) | copy-start | bytes 884740
  48.3 15.7 %collective-permute-start.5 = (bf16[96,1536]{1,0:T(8,128)(2,1)S(1)}, bf16[96,1536]{1,0:T(8,128)(2,1)S(1)}, u32[]{:S(2)}, u32[]{:S(2)}) collective-permute-start(bf16[96,1536]{1,0:T(8,128)(2,1)S(1)} %get-tuple-element.79), channel_id=1, source_target_pairs={{0,4},{4,0},{8,12},{12,8},{16,20},{20,16},{24,28},{28,24},{1,5},{5... | collective-permute-start | bytes 884744 | tf_op jit(solution)/shard_map/ppermute | solution.py:38
  50.2 14.2 %copy-start.40 = (bf16[1,1,1536,768]{3,2,1,0:T(8,128)(2,1)S(1)}, bf16[1,1,1536,768]{3,2,1,0:T(8,128)(2,1)}, u32[]{:S(2)}) copy-start(bf16[1,1,1536,768]{3,2,1,0:T(8,128)(2,1)} %param.11) | copy-start | bytes 7077892
  50.2 26.2 %collective-permute-start.9 = (bf16[192,1536]{1,0:T(8,128)(2,1)S(1)}, bf16[192,1536]{1,0:T(8,128)(2,1)S(1)}, u32[]{:S(2)}, u32[]{:S(2)}) collective-permute-start(bf16[192,1536]{1,0:T(8,128)(2,1)S(1)} %pad_maximum_fusion.6), channel_id=1, source_target_pairs={{0,4},{4,0},{8,12},{12,8},{16,20},{20,16},{24,28},{28,24},{1,5},{5... | collective-permute-start | bytes 1769480 | tf_op jit(solution)/shard_map/ppermute | solution.py:38
  63.9 2.9 %collective-permute-start.13 = (bf16[96,1536]{1,0:T(8,128)(2,1)S(1)}, bf16[96,1536]{1,0:T(8,128)(2,1)S(1)}, u32[]{:S(2)}, u32[]{:S(2)}) collective-permute-start(bf16[96,1536]{1,0:T(8,128)(2,1)S(1)} %get-tuple-element.71), channel_id=1, source_target_pairs={{0,4},{4,0},{8,12},{12,8},{16,20},{20,16},{24,28},{28,24},{1,5},{5... | collective-permute-start | bytes 884744 | tf_op jit(solution)/shard_map/ppermute | solution.py:38
  64.0 124.7 %copy-start.21 = (bf16[96,1536]{1,0:T(8,128)(2,1)}, bf16[96,1536]{1,0:T(8,128)(2,1)S(1)}, u32[]{:S(2)}) copy-start(bf16[96,1536]{1,0:T(8,128)(2,1)S(1)} %collective-permute-done.5) | copy-start | bytes 884740
  65.9 1.8 collective-permute-start.6
  66.9 127.5 %copy-start.3 = (bf16[192,1536]{1,0:T(8,128)(2,1)}, bf16[192,1536]{1,0:T(8,128)(2,1)S(1)}, u32[]{:S(2)}) copy-start(bf16[192,1536]{1,0:T(8,128)(2,1)S(1)} %pad_maximum_fusion.8) | copy-start | bytes 1769476
  67.7 48.2 %collective-permute-start.7 = (bf16[192,1536]{1,0:T(8,128)(2,1)S(1)}, bf16[192,1536]{1,0:T(8,128)(2,1)S(1)}, u32[]{:S(2)}, u32[]{:S(2)}) collective-permute-start(bf16[192,1536]{1,0:T(8,128)(2,1)S(1)} %pad_maximum_fusion.5), channel_id=1, source_target_pairs={{0,16},{4,20},{8,24},{12,28},{16,0},{20,4},{24,8},{28,12},{1,17},{... | collective-permute-start | bytes 1769480 | tf_op jit(solution)/shard_map/ppermute | solution.py:42
  80.5 5.4 %collective-permute-start.10 = (bf16[192,1536]{1,0:T(8,128)(2,1)S(1)}, bf16[192,1536]{1,0:T(8,128)(2,1)S(1)}, u32[]{:S(2)}, u32[]{:S(2)}) collective-permute-start(bf16[192,1536]{1,0:T(8,128)(2,1)S(1)} %slice.220), channel_id=1, source_target_pairs={{0,4},{4,0},{8,12},{12,8},{16,20},{20,16},{24,28},{28,24},{1,5},{5... | collective-permute-start | bytes 1769480 | tf_op jit(solution)/shard_map/ppermute | solution.py:38
  81.5 1.7 collective-permute-start.14
  83.2 32.7 %copy-start.35 = (s32[192]{0:T(256)S(1)}, s32[192]{0:T(256)}, u32[]{:S(2)}) copy-start(s32[192]{0:T(256)} %copy-done.34) | copy-start | bytes 2308
  83.2 33.2 %collective-permute-start.15 = (bf16[192,1536]{1,0:T(8,128)(2,1)S(1)}, bf16[192,1536]{1,0:T(8,128)(2,1)S(1)}, u32[]{:S(2)}, u32[]{:S(2)}) collective-permute-start(bf16[192,1536]{1,0:T(8,128)(2,1)S(1)} %pad_maximum_fusion.9), channel_id=1, source_target_pairs={{0,24},{4,28},{8,16},{12,20},{16,8},{20,12},{24,0},{28,4},{1,25},{... | collective-permute-start | bytes 1769480 | tf_op jit(solution)/shard_map/ppermute | solution.py:42
  86.0 30.4 %copy-start.32 = (s32[192]{0:T(256)S(1)}, s32[192]{0:T(256)}, u32[]{:S(2)}) copy-start(s32[192]{0:T(256)} %copy-done.31) | copy-start | bytes 2308
  86.1 38.2 %collective-permute-start.11 = (bf16[192,1536]{1,0:T(8,128)(2,1)S(1)}, bf16[192,1536]{1,0:T(8,128)(2,1)S(1)}, u32[]{:S(2)}, u32[]{:S(2)}) collective-permute-start(bf16[192,1536]{1,0:T(8,128)(2,1)S(1)} %pad_maximum_fusion.7), channel_id=1, source_target_pairs={{0,8},{4,12},{8,0},{12,4},{16,24},{20,28},{24,16},{28,20},{1,9},{5... | collective-permute-start | bytes 1769480 | tf_op jit(solution)/shard_map/ppermute | solution.py:42
  129.5 18.2 %collective-permute-start.24 = (bf16[192,1536]{1,0:T(8,128)(2,1)S(1)}, bf16[192,1536]{1,0:T(8,128)(2,1)S(1)}, u32[]{:S(2)}, u32[]{:S(2)}) collective-permute-start(bf16[192,1536]{1,0:T(8,128)(2,1)S(1)} %convolution_convert_fusion.4), channel_id=1, source_target_pairs={{0,24},{4,28},{8,16},{12,20},{16,8},{20,12},{24,0},{28,4},{1,25},{... | collective-permute-start | bytes 1769480 | tf_op jit(solution)/shard_map/ppermute | solution.py:42
  132.6 51.2 %collective-permute-start.16 = (bf16[192,1536]{1,0:T(8,128)(2,1)S(1)}, bf16[192,1536]{1,0:T(8,128)(2,1)S(1)}, u32[]{:S(2)}, u32[]{:S(2)}) collective-permute-start(bf16[192,1536]{1,0:T(8,128)(2,1)S(1)} %convolution_convert_fusion.5), channel_id=1, source_target_pairs={{0,16},{4,20},{8,24},{12,28},{16,0},{20,4},{24,8},{28,12},{1,17},{... | collective-permute-start | bytes 1769480 | tf_op jit(solution)/shard_map/ppermute | solution.py:42
  136.6 47.3 %collective-permute-start.20 = (bf16[192,1536]{1,0:T(8,128)(2,1)S(1)}, bf16[192,1536]{1,0:T(8,128)(2,1)S(1)}, u32[]{:S(2)}, u32[]{:S(2)}) collective-permute-start(bf16[192,1536]{1,0:T(8,128)(2,1)S(1)} %slice.233), channel_id=1, source_target_pairs={{0,8},{4,12},{8,0},{12,4},{16,24},{20,28},{24,16},{28,20},{1,9},{5... | collective-permute-start | bytes 1769480 | tf_op jit(solution)/shard_map/ppermute | solution.py:42
  147.8 41.2 %collective-permute-start.25 = (bf16[96,1536]{1,0:T(8,128)(2,1)S(1)}, bf16[96,1536]{1,0:T(8,128)(2,1)S(1)}, u32[]{:S(2)}, u32[]{:S(2)}) collective-permute-start(bf16[96,1536]{1,0:T(8,128)(2,1)S(1)} %get-tuple-element.67), channel_id=1, source_target_pairs={{0,4},{4,0},{8,12},{12,8},{16,20},{20,16},{24,28},{28,24},{1,5},{5... | collective-permute-start | bytes 884744 | tf_op jit(solution)/shard_map/ppermute | solution.py:38
  183.8 1.6 collective-permute-start.17
  184.0 5.0 %collective-permute-start.21 = (bf16[192,1536]{1,0:T(8,128)(2,1)S(1)}, bf16[192,1536]{1,0:T(8,128)(2,1)S(1)}, u32[]{:S(2)}, u32[]{:S(2)}) collective-permute-start(bf16[192,1536]{1,0:T(8,128)(2,1)S(1)} %pad_maximum_fusion.12), channel_id=1, source_target_pairs={{0,4},{4,0},{8,12},{12,8},{16,20},{20,16},{24,28},{28,24},{1,5},{5... | collective-permute-start | bytes 1769480 | tf_op jit(solution)/shard_map/ppermute | solution.py:38
  188.6 25.4 %collective-permute-start.18 = (bf16[96,1536]{1,0:T(8,128)(2,1)}, bf16[96,1536]{1,0:T(8,128)(2,1)}, u32[]{:S(2)}, u32[]{:S(2)}) collective-permute-start(bf16[96,1536]{1,0:T(8,128)(2,1)} %get-tuple-element.53), channel_id=1, source_target_pairs={{0,4},{4,0},{8,12},{12,8},{16,20},{20,16},{24,28},{28,24},{1,5},{5... | collective-permute-start | bytes 884744 | tf_op jit(solution)/shard_map/ppermute | solution.py:38
  197.3 26.1 %collective-permute-start.26 = (bf16[96,1536]{1,0:T(8,128)(2,1)}, bf16[96,1536]{1,0:T(8,128)(2,1)}, u32[]{:S(2)}, u32[]{:S(2)}) collective-permute-start(bf16[96,1536]{1,0:T(8,128)(2,1)} %get-tuple-element.56), channel_id=1, source_target_pairs={{0,4},{4,0},{8,12},{12,8},{16,20},{20,16},{24,28},{28,24},{1,5},{5... | collective-permute-start | bytes 884744 | tf_op jit(solution)/shard_map/ppermute | solution.py:38
  197.7 21.7 %collective-permute-start.22 = (bf16[192,1536]{1,0:T(8,128)(2,1)}, bf16[192,1536]{1,0:T(8,128)(2,1)}, u32[]{:S(2)}, u32[]{:S(2)}) collective-permute-start(bf16[192,1536]{1,0:T(8,128)(2,1)} %slice.238), channel_id=1, source_target_pairs={{0,4},{4,0},{8,12},{12,8},{16,20},{20,16},{24,28},{28,24},{1,5},{5... | collective-permute-start | bytes 1769480 | tf_op jit(solution)/shard_map/ppermute | solution.py:38
  201.1 16.7 %all-to-all-start = ((f32[8,24,128]{2,1,0:T(8,128)}), f32[8,24,128]{2,1,0:T(8,128)}, u32[]{:S(2)}, u32[]{:S(2)}) async-start(f32[8,24,128]{2,1,0:T(8,128)} %broadcast_in_dim.67), calls=%async_computation | async-start | bytes 196608 | tf_op jit(solution)/shard_map/all_to_all | solution.py:46
  215.1 45.5 %collective-permute-start.19 = (bf16[192,1536]{1,0:T(8,128)(2,1)S(1)}, bf16[192,1536]{1,0:T(8,128)(2,1)}, u32[]{:S(2)}, u32[]{:S(2)}) collective-permute-start(bf16[192,1536]{1,0:T(8,128)(2,1)S(1)} %pad_maximum_fusion.11), channel_id=1, source_target_pairs={{0,16},{4,20},{8,24},{12,28},{16,0},{20,4},{24,8},{28,12},{1,17},{... | collective-permute-start | bytes 1769480 | tf_op jit(solution)/shard_map/ppermute | solution.py:42
  220.5 39.5 %copy-start.22 = (bf16[96,1536]{1,0:T(8,128)(2,1)S(1)}, bf16[96,1536]{1,0:T(8,128)(2,1)}, u32[]{:S(2)}) copy-start(bf16[96,1536]{1,0:T(8,128)(2,1)} %get-tuple-element.28) | copy-start | bytes 884740
  220.5 39.4 %copy-start.28 = (pred[192,256]{1,0:T(32,128)(4,1)S(1)}, pred[192,256]{1,0:T(32,128)(4,1)}, u32[]{:S(2)}) copy-start(pred[192,256]{1,0:T(32,128)(4,1)} %copy-done.27) | copy-start | bytes 147460
  220.5 39.4 %copy-start.30 = (pred[192,256]{1,0:T(32,128)(4,1)S(1)}, pred[192,256]{1,0:T(32,128)(4,1)}, u32[]{:S(2)}) copy-start(pred[192,256]{1,0:T(32,128)(4,1)} %copy-done.29) | copy-start | bytes 147460
  220.6 39.4 %collective-permute-start.23 = (bf16[192,1536]{1,0:T(8,128)(2,1)S(1)}, bf16[192,1536]{1,0:T(8,128)(2,1)S(1)}, u32[]{:S(2)}, u32[]{:S(2)}) collective-permute-start(bf16[192,1536]{1,0:T(8,128)(2,1)S(1)} %pad_maximum_fusion.13), channel_id=1, source_target_pairs={{0,8},{4,12},{8,0},{12,4},{16,24},{20,28},{24,16},{28,20},{1,9},{5... | collective-permute-start | bytes 1769480 | tf_op jit(solution)/shard_map/ppermute | solution.py:42
  224.6 38.5 %collective-permute-start.27 = (bf16[192,1152]{1,0:T(8,128)(2,1)S(1)}, bf16[192,1152]{1,0:T(8,128)(2,1)S(1)}, u32[]{:S(2)}, u32[]{:S(2)}) collective-permute-start(bf16[192,1152]{1,0:T(8,128)(2,1)S(1)} %pad_maximum_fusion.15), channel_id=1, source_target_pairs={{0,24},{4,28},{8,16},{12,20},{16,8},{20,12},{24,0},{28,4},{1,25},{... | collective-permute-start | bytes 1327112 | tf_op jit(solution)/shard_map/ppermute | solution.py:42
  224.9 42.8 %collective-permute-start.31 = (bf16[192,384]{1,0:T(8,128)(2,1)S(1)}, bf16[192,384]{1,0:T(8,128)(2,1)S(1)}, u32[]{:S(2)}, u32[]{:S(2)}) collective-permute-start(bf16[192,384]{1,0:T(8,128)(2,1)S(1)} %get-tuple-element.45), channel_id=1, source_target_pairs={{0,24},{4,28},{8,16},{12,20},{16,8},{20,12},{24,0},{28,4},{1,25},{... | collective-permute-start | bytes 442376 | tf_op jit(solution)/shard_map/ppermute | solution.py:42
  264.2 8.7 %collective-permute-start.28 = (bf16[256,384]{1,0:T(8,128)(2,1)S(1)}, bf16[256,384]{1,0:T(8,128)(2,1)S(1)}, u32[]{:S(2)}, u32[]{:S(2)}) collective-permute-start(bf16[256,384]{1,0:T(8,128)(2,1)S(1)} %get-tuple-element.51), channel_id=1, source_target_pairs={{0,3},{1,2},{2,1},{3,0},{4,7},{5,6},{6,5},{7,4},{8,11},{9,10},{10,... | collective-permute-start | bytes 589832 | tf_op jit(solution)/shard_map/ppermute | solution.py:82
  265.3 9.9 %collective-permute-start.29 = (bf16[256,384]{1,0:T(8,128)(2,1)S(1)}, bf16[256,384]{1,0:T(8,128)(2,1)S(1)}, u32[]{:S(2)}, u32[]{:S(2)}) collective-permute-start(bf16[256,384]{1,0:T(8,128)(2,1)S(1)} %get-tuple-element.50), channel_id=1, source_target_pairs={{0,2},{1,3},{2,0},{3,1},{4,6},{5,7},{6,4},{7,5},{8,10},{9,11},{10,... | collective-permute-start | bytes 589832 | tf_op jit(solution)/shard_map/ppermute | solution.py:82
  267.2 8.1 %collective-permute-start.30 = (bf16[256,384]{1,0:T(8,128)(2,1)S(1)}, bf16[256,384]{1,0:T(8,128)(2,1)S(1)}, u32[]{:S(2)}, u32[]{:S(2)}) collective-permute-start(bf16[256,384]{1,0:T(8,128)(2,1)S(1)} %get-tuple-element.49), channel_id=1, source_target_pairs={{0,1},{1,0},{2,3},{3,2},{4,5},{5,4},{6,7},{7,6},{8,9},{9,8},{10,11... | collective-permute-start | bytes 589832 | tf_op jit(solution)/shard_map/ppermute | solution.py:82
  (29 other events, 117.3 us)

commit v5 on v4

--- a/solution.py
+++ b/solution.py
@@ -20,6 +20,22 @@
     return 0.5 * (1.0 + tangent) + 0.5 * value * (1.0 - tangent * tangent) * gelu_coef * (
         1.0 + 3.0 * cubic_coef * value * value
     )
+
+
+LINE_CHIPS = 4
+
+
+def chip_pairs(pairs):
+    return [(2 * a + core, 2 * b + core) for a, b in pairs for core in (0, 1)]
+
+
+MIDDLE = chip_pairs([(1, 2), (2, 1)])
+ENDS = chip_pairs([(0, 3), (3, 0)])
+FOLD = chip_pairs([(2, 0), (1, 3), (3, 2), (0, 1)])
+
+
+def move(rows, pairs):
+    return lax.ppermute(rows, "dp", pairs)
 
 
 def dot(a, b, dims):
@@ -120,6 +136,20 @@
         return jnp.concatenate(rows).astype(jnp.bfloat16) if len(rows) > 1 else rows[0].astype(jnp.bfloat16)
 
     placers = [placer_of(g) for g in groups]
+    split = can_split(model_width)
+    line = split and chips == LINE_CHIPS
+    if line:
+        inner = jnp.logical_or(me // 2 == 1, me // 2 == 2)
+        far_target = move(target.T, MIDDLE)
+        slot = lax.broadcasted_iota(jnp.int32, (2 * depth, row_count), 0)
+        place_far = []
+        for k in (3, 2):
+            at = slot + 2 * k * depth
+            place_far.append(jnp.logical_or(far_target[0][None, :] == at, far_target[1][None, :] == at))
+        place_far = jnp.concatenate(place_far).astype(jnp.bfloat16)
+        home = [jnp.where(inner, jnp.zeros_like(placers[0]), placers[0])] + placers[1:]
+    else:
+        home = placers
     my_column = lax.broadcasted_iota(jnp.int32, (1, experts), 1) == me
     router_mine = jnp.sum(jnp.where(my_column, router_row.astype(jnp.float32), 0.0), axis=1)
 
@@ -144,7 +174,15 @@
             arrived.append(jnp.concatenate([mine, swap_cores(others)]))
         return arrived
 
+    def paired(rows):
+        return jnp.concatenate([rows[:depth], swap_cores(rows[depth:])])
+
+    def far_sum(pair, passed):
+        return dot(place_far, jnp.concatenate([pair, passed]), ((0,), (0,))).astype(jnp.bfloat16)
+
     def give_back(group, rows):
+        if line and group == groups[0]:
+            return move(paired(rows), FOLD)
         half = len(group) * depth
         others = swap_cores(rows[half:])
         parts = []
@@ -154,7 +192,7 @@
         return jnp.concatenate(parts)
 
     def partial_sum(start, parts):
-        for place, rows in zip(placers[:-1], parts[:-1]):
+        for place, rows in zip(home[:-1], parts[:-1]):
             start = start + dot(place, rows, ((0,), (0,)))
         return lax.optimization_barrier(start)
 
@@ -163,7 +201,6 @@
         return start + dot(placers[-1], parts[-1], ((0,), (0,)))
 
     own_rows = tokens.reshape(row_count, model_width)
-    split = can_split(model_width)
     if split:
         pieces = swap_heads(blocks_of(own_rows, model_width))
         mixed = in_order(pieces)
@@ -172,7 +209,7 @@
     cot_f = cotangent.reshape(row_count, model_width).astype(jnp.float32)
     mean_grad = lax.optimization_barrier(jnp.mean(cot_f * gain_row[None, :], axis=1, keepdims=True))
     kept, parts = [], []
-    for group, rows in zip(groups, dispatch(mixed, pieces)):
+    for g, (group, rows) in enumerate(zip(groups, dispatch(mixed, pieces))):
         if parts:
             rows = after(rows, gated)
         logits = lax.optimization_barrier(dot(rows, router_row, ((1,), (0,))))
@@ -182,8 +219,15 @@
         out = dot(act, weight_out, ((1,), (0,)))
         kept.append((rows, gate, lax.optimization_barrier(pre_act), act, out.astype(jnp.bfloat16)))
         gated = (gate * out).astype(jnp.bfloat16)
-        parts.append(give_back(group, gated))
+        if line and g == len(groups) - 1:
+            pair = paired(gated)
+            parts.append(move(pair, ENDS))
+            crossed = move(far_sum(pair, parts[0]), MIDDLE)
+        else:
+            parts.append(give_back(group, gated))
     residual = collect(mixed.astype(jnp.float32), parts)
+    if line:
+        residual = residual + crossed.astype(jnp.float32)
     row_mean = jnp.mean(residual, axis=1, keepdims=True)
     centered = residual - row_mean
     row_var = jnp.mean(centered * centered, axis=1, keepdims=True)
@@ -217,10 +261,18 @@
         grad_input = dot(grad_pre, weight_in, ((1,), (1,))) + grad_logit * router_mine[None, :]
         back = grad_input.astype(jnp.bfloat16)
         if split and g == len(groups) - 1:
-            pair = jnp.concatenate([back[:depth], swap_cores(back[depth:])])
+            pair = paired(back)
             own_block, *others = blocks_of(pair, model_width)
-            parts.append(to_chip(jnp.concatenate(others, axis=1), group[0]))
-            last_block = to_chip(own_block, group[0])
+            others = jnp.concatenate(others, axis=1)
+            if line:
+                parts.append(move(others, ENDS))
+                own_sum, *other_sums = blocks_of(far_sum(pair, parts[0]), model_width)
+                crossed = move(jnp.concatenate(other_sums, axis=1), MIDDLE)
+                last_block = move(own_block, ENDS)
+                last_crossed = move(own_sum, MIDDLE)
+            else:
+                parts.append(to_chip(others, group[0]))
+                last_block = to_chip(own_block, group[0])
         else:
             parts.append(give_back(group, back))
         part = jnp.sum(rows.astype(jnp.float32) * grad_logit, axis=0)
@@ -230,8 +282,10 @@
     if split:
         start, *others = blocks_of(partial_sum(grad_resid, parts), model_width)
         main = jnp.concatenate(others, axis=1) + dot(placers[-1], parts[-1], ((0,), (0,)))
-        main = main.astype(jnp.bfloat16)
-        start = (start + dot(placers[-1], last_block, ((0,), (0,)))).astype(jnp.bfloat16)
+        main = (main + crossed.astype(jnp.float32) if line else main).astype(jnp.bfloat16)
+        last_block = after(last_block, main)
+        start = start + dot(placers[-1], last_block, ((0,), (0,)))
+        start = (start + last_crossed.astype(jnp.float32) if line else start).astype(jnp.bfloat16)
         grad_tokens = in_order(swap_heads([start] + cut(main, model_width)))
     else:
         grad_tokens = mix_heads(collect(grad_resid, parts).astype(jnp.bfloat16))

time: 279 us -> 267 us (0.957)
  the two profiles are of different devices: /device:TPU:0 before, /device:TPU:8 now
where the time goes in v5:
time: 267 us; the launch traced here: 266 us
  waiting for transfers between devices  152 us (57%)
  starting transfers between devices  45.3 us (17%)
  matrix products  32.7 us (12%)
  local copies, waits for them, and re-layouts  17.1 us (6%)
  other arithmetic  17 us (6%)
    ppermute x9, waiting for transfers between devices, to_chip(): lax.ppermute(rows, 'dp', xor_pairs(lax.axis_size('dp'), 2 * k))  110 us
    dot_general x33, matrix products, dot(): lax.dot_general(a, b, (dims, ((), ())), preferred_element_type=jnp.float32)  32.7 us
    ppermute x9, waiting for transfers between devices, move(): return lax.ppermute(rows, 'dp', pairs)  32.7 us
    ppermute x9, starting transfers between devices, to_chip(): lax.ppermute(rows, 'dp', xor_pairs(lax.axis_size('dp'), 2 * k))  14.7 us
    ppermute x9, starting transfers between devices, move(): return lax.ppermute(rows, 'dp', pairs)  14.7 us
    ppermute x6, starting transfers between devices, swap_heads(): moved.append(lax.ppermute(piece, 'expert', pairs) if k else piece)  7.04 us
    ppermute x6, waiting for transfers between devices, swap_heads(): moved.append(lax.ppermute(piece, 'expert', pairs) if k else piece)  6.8 us
    all_to_all x1, starting transfers between devices, exchange(): return lax.all_to_all(blocks, 'dp', split_axis=0, concat_axis=0, tiled=True)  6.11 us
  transfers between devices with their start and end apart: 37, of which 19 were waited for; matrix products, arithmetic and copies ran while one was open for 20% of the time, Pallas kernels for 0%

profile of v5, /device:TPU:8, one launch (start us, length us, event | category | flops | bytes accessed | tf_op | source)
XLA Modules:
  0.0 265.8 jit_solution(4120865100865169222)
XLA Ops:
  2.0 1.1 reduce-window.6
  4.4 1.8 convolution_convert_fusion.10
  6.3 2.6 collective-permute-start.4
  9.7 2.4 collective-permute-start
  13.1 1.9 collective-permute-start.16
  16.5 2.2 collective-permute-done.16
  19.7 1.8 collective-permute-done.1
  21.5 1.5 convolution_convert_fusion.9
  23.4 1.4 fusion.144
  25.8 1.6 collective-permute-start.12
  27.4 2.5 collective-permute-start.8
  29.9 25.2 %collective-permute-done.3 = bf16[192,1152]{1,0:T(8,128)(2,1)S(1)} collective-permute-done((bf16[192,1152]{1,0:T(8,128)(2,1)S(1)}, bf16[192,1152]{1,0:T(8,128)(2,1)S(1)}, u32[]{:S(2)}, u32[]{:S(2)}) %collective-permute-start.3) | collective-permute-done | bytes 442400 | tf_op jit(solution)/shard_map/ppermute | solution.py:58
  55.4 14.4 %collective-permute-done.12 = bf16[192,1536]{1,0:T(8,128)(2,1)S(1)} collective-permute-done((bf16[192,1536]{1,0:T(8,128)(2,1)S(1)}, bf16[192,1536]{1,0:T(8,128)(2,1)S(1)}, u32[]{:S(2)}, u32[]{:S(2)}) %collective-permute-start.12) | collective-permute-done | bytes 589856 | tf_op jit(solution)/shard_map/ppermute | solution.py:58
  73.5 1.1 collective-permute-done.6
  75.8 1.3 fusion.76
  77.2 1.1 multiply_convert_fusion
  82.7 3.9 %collective-permute-start.11 = (bf16[192,1536]{1,0:T(8,128)(2,1)S(1)}, bf16[192,1536]{1,0:T(8,128)(2,1)S(1)}, u32[]{:S(2)}, u32[]{:S(2)}) collective-permute-start(bf16[192,1536]{1,0:T(8,128)(2,1)S(1)} %pad_maximum_fusion.7), channel_id=1, source_target_pairs={{0,8},{4,12},{8,0},{12,4},{16,24},{20,28},{24,16},{28,20},{1,9},{5... | collective-permute-start | bytes 1769480 | tf_op jit(solution)/shard_map/ppermute | solution.py:58
  86.6 4.3 %collective-permute-done.7 = bf16[192,1536]{1,0:T(8,128)(2,1)S(1)} collective-permute-done((bf16[192,1536]{1,0:T(8,128)(2,1)S(1)}, bf16[192,1536]{1,0:T(8,128)(2,1)S(1)}, u32[]{:S(2)}, u32[]{:S(2)}) %collective-permute-start.7) | collective-permute-done | bytes 589856 | tf_op jit(solution)/shard_map/ppermute | solution.py:38
  91.6 2.4 collective-permute-start.17
  94.9 20.5 %collective-permute-done.11 = bf16[192,1536]{1,0:T(8,128)(2,1)S(1)} collective-permute-done((bf16[192,1536]{1,0:T(8,128)(2,1)S(1)}, bf16[192,1536]{1,0:T(8,128)(2,1)S(1)}, u32[]{:S(2)}, u32[]{:S(2)}) %collective-permute-start.11) | collective-permute-done | bytes 589856 | tf_op jit(solution)/shard_map/ppermute | solution.py:58
  116.0 3.3 %collective-permute-done.17 = bf16[256,1536]{1,0:T(8,128)(2,1)S(1)} collective-permute-done((bf16[256,1536]{1,0:T(8,128)(2,1)S(1)}, bf16[256,1536]{1,0:T(8,128)(2,1)S(1)}, u32[]{:S(2)}, u32[]{:S(2)}) %collective-permute-start.17) | collective-permute-done | bytes 786464 | tf_op jit(solution)/shard_map/ppermute | solution.py:38
  121.4 1.5 fusion.47
  123.8 1.8 collective-permute-start.26
  126.1 1.8 collective-permute-start.22
  127.9 33.6 %collective-permute-done.26 = bf16[192,1536]{1,0:T(8,128)(2,1)S(1)} collective-permute-done((bf16[192,1536]{1,0:T(8,128)(2,1)S(1)}, bf16[192,1536]{1,0:T(8,128)(2,1)S(1)}, u32[]{:S(2)}, u32[]{:S(2)}) %collective-permute-start.26) | collective-permute-done | bytes 589856 | tf_op jit(solution)/shard_map/ppermute | solution.py:58
  161.6 11.7 %collective-permute-done.18 = bf16[192,1536]{1,0:T(8,128)(2,1)S(1)} collective-permute-done((bf16[192,1536]{1,0:T(8,128)(2,1)S(1)}, bf16[192,1536]{1,0:T(8,128)(2,1)S(1)}, u32[]{:S(2)}, u32[]{:S(2)}) %collective-permute-start.18) | collective-permute-done | bytes 589856 | tf_op jit(solution)/shard_map/ppermute | solution.py:58
  179.3 1.1 fusion.53
  180.4 1.1 fusion.3
  188.0 1.3 broadcast_in_dim.70
  189.3 1.3 broadcast_in_dim.71
  190.7 6.1 %all-to-all-start = ((f32[8,24,128]{2,1,0:T(8,128)}), f32[8,24,128]{2,1,0:T(8,128)}, u32[]{:S(2)}, u32[]{:S(2)}) async-start(f32[8,24,128]{2,1,0:T(8,128)} %broadcast_in_dim.71), calls=%async_computation | async-start | bytes 196608 | tf_op jit(solution)/shard_map/all_to_all | solution.py:62
  196.8 5.2 %fusion = bf16[1,1,1536,768]{3,2,1,0:T(8,128)(2,1)} fusion(bf16[192,1536]{1,0:T(8,128)(2,1)} %copy-done.3, bf16[384,1536]{1,0:T(8,128)(2,1)S(1)} %pad_maximum_fusion, bf16[96,1536]{1,0:T(8,128)(2,1)} %copy-done.20, bf16[96,1536]{1,0:T(8,128)(2,1)} %copy-done.9, bf16[192,768]{1,0:T(8,128)(2,1)} %copy-done.23, bf16[384,768]{1,0:T(8,128)(2,1)} %copy-done.45, ...), kind=kOutput, calls=%fused_computation.3 | convolution fusion | flops 1826095104 | bytes 5898240 | tf_op jit(solution)/shard_map/dot_general | solution.py:42
  202.1 3.4 %fusion.1 = bf16[1,1,768,1536]{3,2,1,0:T(8,128)(2,1)} fusion(bf16[192,1536]{1,0:T(8,128)(2,1)S(1)} %copy-done.8, bf16[384,1536]{1,0:T(8,128)(2,1)S(1)} %copy-done.11, bf16[192,1536]{1,0:T(8,128)(2,1)S(1)} %copy-done.6, bf16[192,768]{1,0:T(8,128)(2,1)S(1)} %copy-done.19, bf16[384,768]{1,0:T(8,128)(2,1)S(1)} %copy-done.47, bf16[192,768]{1,0:T(8,128)(2,1)S(1)} %copy-done.17), kind=kOutput, calls=%fused_computation.4 | convolution fusion | flops 1823735808 | bytes 5898240 | tf_op jit(solution)/shard_map/dot_general | solution.py:42
  206.6 2.4 collective-permute-start.21
  209.0 1.6 reshape.168
  210.6 1.1 slice_reduce_fusion
  213.9 1.1 fusion.197
  216.6 6.3 %collective-permute-done.21 = bf16[192,1536]{1,0:T(8,128)(2,1)} collective-permute-done((bf16[192,1536]{1,0:T(8,128)(2,1)S(1)}, bf16[192,1536]{1,0:T(8,128)(2,1)}, u32[]{:S(2)}, u32[]{:S(2)}) %collective-permute-start.21) | collective-permute-done | bytes 589856 | tf_op jit(solution)/shard_map/ppermute | solution.py:38
  222.9 1.8 convolution_convert_fusion.4
  224.9 3.4 %collective-permute-start.30 = (bf16[256,1152]{1,0:T(8,128)(2,1)S(1)}, bf16[256,1152]{1,0:T(8,128)(2,1)S(1)}, u32[]{:S(2)}, u32[]{:S(2)}) collective-permute-start(bf16[256,1152]{1,0:T(8,128)(2,1)S(1)} %pad_maximum_fusion.15), channel_id=1, source_target_pairs={{8,16},{12,20},{16,8},{20,12},{9,17},{13,21},{17,9},{21,13},{10,18... | collective-permute-start | bytes 1769480 | tf_op jit(solution)/shard_map/ppermute | solution.py:38
  228.3 2.5 collective-permute-start.35
  230.7 4.7 %collective-permute-done.25 = bf16[192,1536]{1,0:T(8,128)(2,1)S(1)} collective-permute-done((bf16[192,1536]{1,0:T(8,128)(2,1)S(1)}, bf16[192,1536]{1,0:T(8,128)(2,1)S(1)}, u32[]{:S(2)}, u32[]{:S(2)}) %collective-permute-start.25) | collective-permute-done | bytes 589856 | tf_op jit(solution)/shard_map/ppermute | solution.py:58
  236.9 1.5 fusion.4
  238.6 16.6 %collective-permute-done.30 = bf16[256,1152]{1,0:T(8,128)(2,1)S(1)} collective-permute-done((bf16[256,1152]{1,0:T(8,128)(2,1)S(1)}, bf16[256,1152]{1,0:T(8,128)(2,1)S(1)}, u32[]{:S(2)}, u32[]{:S(2)}) %collective-permute-start.30) | collective-permute-done | bytes 589856 | tf_op jit(solution)/shard_map/ppermute | solution.py:38
  255.7 1.1 collective-permute-start.31
  256.8 1.9 collective-permute-start.32
  259.6 2.8 %collective-permute-done.31 = bf16[256,384]{1,0:T(8,128)(2,1)S(1)} collective-permute-done((bf16[256,384]{1,0:T(8,128)(2,1)S(1)}, bf16[256,384]{1,0:T(8,128)(2,1)S(1)}, u32[]{:S(2)}, u32[]{:S(2)}) %collective-permute-start.31) | collective-permute-done | bytes 196640 | tf_op jit(solution)/shard_map/ppermute | solution.py:98
  262.5 2.0 collective-permute-done.32
  (257 shorter events, 44.9 us)
Async XLA Ops:
  0.6 71.6 %copy-start = (bf16[1,1,768,1536]{3,2,1,0:T(8,128)(2,1)S(1)}, bf16[1,1,768,1536]{3,2,1,0:T(8,128)(2,1)}, u32[]{:S(2)}) copy-start(bf16[1,1,768,1536]{3,2,1,0:T(8,128)(2,1)} %param.12) | copy-start | bytes 7077892
  0.7 15.1 %copy-start.24 = (bf16[1,1536,8]{1,2,0:T(8,128)(2,1)S(1)}, bf16[1,1536,8]{1,2,0:T(8,128)(2,1)}, u32[]{:S(2)}) copy-start(bf16[1,1536,8]{1,2,0:T(8,128)(2,1)} %param.9) | copy-start | bytes 73732
  0.7 15.8 %copy-start.43 = (f32[1,1536]{1,0:T(1,128)S(1)}, f32[1,1536]{1,0:T(1,128)}, u32[]{:S(2)}) copy-start(f32[1,1536]{1,0:T(1,128)} %param.10) | copy-start | bytes 18436
  2.0 21.1 %copy-start.37 = (s32[192]{0:T(256)}, s32[192]{0:T(256)S(1)}, u32[]{:S(2)}) copy-start(s32[192]{0:T(256)S(1)} %iota_add_fusion.2) | copy-start | bytes 2308
  6.3 23.6 %collective-permute-start.4 = (bf16[192,384]{1,0:T(8,128)(2,1)}, bf16[192,384]{1,0:T(8,128)(2,1)S(1)}, u32[]{:S(2)}, u32[]{:S(2)}) collective-permute-start(bf16[192,384]{1,0:T(8,128)(2,1)} %convolution_convert_fusion.10), channel_id=1, source_target_pairs={{0,16},{4,20},{8,24},{12,28},{16,0},{20,4},{24,8},{28,12},{1,17},{... | collective-permute-start | bytes 442376 | tf_op jit(solution)/shard_map/ppermute | solution.py:58
  9.7 10.0 %collective-permute-start = (bf16[256,384]{1,0:T(8,128)(2,1)}, bf16[256,384]{1,0:T(8,128)(2,1)}, u32[]{:S(2)}, u32[]{:S(2)}) collective-permute-start(bf16[256,384]{1,0:T(8,128)(2,1)} %get-tuple-element.51), channel_id=1, source_target_pairs={{0,3},{1,2},{2,1},{3,0},{4,7},{5,6},{6,5},{7,4},{8,11},{9,10},{10,... | collective-permute-start | bytes 589832 | tf_op jit(solution)/shard_map/ppermute | solution.py:98
  12.1 9.3 %collective-permute-start.1 = (bf16[256,384]{1,0:T(8,128)(2,1)}, bf16[256,384]{1,0:T(8,128)(2,1)}, u32[]{:S(2)}, u32[]{:S(2)}) collective-permute-start(bf16[256,384]{1,0:T(8,128)(2,1)} %get-tuple-element.50), channel_id=1, source_target_pairs={{0,2},{1,3},{2,0},{3,1},{4,6},{5,7},{6,4},{7,5},{8,10},{9,11},{10,... | collective-permute-start | bytes 589832 | tf_op jit(solution)/shard_map/ppermute | solution.py:98
  12.6 8.9 %collective-permute-start.2 = (bf16[256,384]{1,0:T(8,128)(2,1)S(1)}, bf16[256,384]{1,0:T(8,128)(2,1)}, u32[]{:S(2)}, u32[]{:S(2)}) collective-permute-start(bf16[256,384]{1,0:T(8,128)(2,1)S(1)} %get-tuple-element.49), channel_id=1, source_target_pairs={{0,1},{1,0},{2,3},{3,2},{4,5},{5,4},{6,7},{7,6},{8,9},{9,8},{10,11... | collective-permute-start | bytes 589832 | tf_op jit(solution)/shard_map/ppermute | solution.py:98
  13.1 5.6 %collective-permute-start.16 = (s32[2,256]{1,0:T(2,128)S(1)}, s32[2,256]{1,0:T(2,128)}, u32[]{:S(2)}, u32[]{:S(2)}) collective-permute-start(s32[2,256]{1,0:T(2,128)S(1)} %bitcast.166), channel_id=1, source_target_pairs={{8,16},{12,20},{16,8},{20,12},{9,17},{13,21},{17,9},{21,13},{10,18... | collective-permute-start | bytes 6152 | tf_op jit(solution)/shard_map/ppermute | solution.py:38
  15.1 55.7 %copy-start.40 = (pred[8]{0:T(512)(128)(4,1)}, pred[8]{0:T(512)(128)(4,1)S(1)}, u32[]{:S(2)}) copy-start(pred[8]{0:T(512)(128)(4,1)S(1)} %iota_compare_fusion.4) | copy-start | bytes 28
  19.6 71.3 %copy-start.30 = (pred[192,256]{1,0:T(32,128)(4,1)}, pred[192,256]{1,0:T(32,128)(4,1)S(1)}, u32[]{:S(2)}) copy-start(pred[192,256]{1,0:T(32,128)(4,1)S(1)} %get-tuple-element.92) | copy-start | bytes 147460
  19.6 71.3 %copy-start.32 = (pred[192,256]{1,0:T(32,128)(4,1)}, pred[192,256]{1,0:T(32,128)(4,1)S(1)}, u32[]{:S(2)}) copy-start(pred[192,256]{1,0:T(32,128)(4,1)S(1)} %get-tuple-element.93) | copy-start | bytes 147460
  23.0 32.0 %collective-permute-start.3 = (bf16[192,1152]{1,0:T(8,128)(2,1)S(1)}, bf16[192,1152]{1,0:T(8,128)(2,1)S(1)}, u32[]{:S(2)}, u32[]{:S(2)}) collective-permute-start(bf16[192,1152]{1,0:T(8,128)(2,1)S(1)} %convolution_convert_fusion.9), channel_id=1, source_target_pairs={{0,16},{4,20},{8,24},{12,28},{16,0},{20,4},{24,8},{28,12},{1,17},{... | collective-permute-start | bytes 1327112 | tf_op jit(solution)/shard_map/ppermute | solution.py:58
  25.8 44.0 %collective-permute-start.12 = (bf16[192,1536]{1,0:T(8,128)(2,1)S(1)}, bf16[192,1536]{1,0:T(8,128)(2,1)S(1)}, u32[]{:S(2)}, u32[]{:S(2)}) collective-permute-start(bf16[192,1536]{1,0:T(8,128)(2,1)S(1)} %convolution_convert_fusion.8), channel_id=1, source_target_pairs={{0,24},{4,28},{8,16},{12,20},{16,8},{20,12},{24,0},{28,4},{1,25},{... | collective-permute-start | bytes 1769480 | tf_op jit(solution)/shard_map/ppermute | solution.py:58
  27.4 42.5 %collective-permute-start.8 = (bf16[192,1536]{1,0:T(8,128)(2,1)S(1)}, bf16[192,1536]{1,0:T(8,128)(2,1)S(1)}, u32[]{:S(2)}, u32[]{:S(2)}) collective-permute-start(bf16[192,1536]{1,0:T(8,128)(2,1)S(1)} %slice.225), channel_id=1, source_target_pairs={{0,8},{4,12},{8,0},{12,4},{16,24},{20,28},{24,16},{28,20},{1,9},{5... | collective-permute-start | bytes 1769480 | tf_op jit(solution)/shard_map/ppermute | solution.py:58
  55.3 123.1 %copy-start.9 = (bf16[96,1536]{1,0:T(8,128)(2,1)}, bf16[96,1536]{1,0:T(8,128)(2,1)S(1)}, u32[]{:S(2)}) copy-start(bf16[96,1536]{1,0:T(8,128)(2,1)S(1)} %get-tuple-element.85) | copy-start | bytes 884740
  55.3 15.3 %collective-permute-start.5 = (bf16[96,1536]{1,0:T(8,128)(2,1)S(1)}, bf16[96,1536]{1,0:T(8,128)(2,1)S(1)}, u32[]{:S(2)}, u32[]{:S(2)}) collective-permute-start(bf16[96,1536]{1,0:T(8,128)(2,1)S(1)} %get-tuple-element.86), channel_id=1, source_target_pairs={{0,4},{4,0},{8,12},{12,8},{16,20},{20,16},{24,28},{28,24},{1,5},{5... | collective-permute-start | bytes 884744 | tf_op jit(solution)/shard_map/ppermute | solution.py:54
  69.8 3.6 %collective-permute-start.13 = (bf16[96,1536]{1,0:T(8,128)(2,1)S(1)}, bf16[96,1536]{1,0:T(8,128)(2,1)S(1)}, u32[]{:S(2)}, u32[]{:S(2)}) collective-permute-start(bf16[96,1536]{1,0:T(8,128)(2,1)S(1)} %get-tuple-element.82), channel_id=1, source_target_pairs={{0,4},{4,0},{8,12},{12,8},{16,20},{20,16},{24,28},{28,24},{1,5},{5... | collective-permute-start | bytes 884744 | tf_op jit(solution)/shard_map/ppermute | solution.py:54
  70.0 4.7 %collective-permute-start.9 = (bf16[192,1536]{1,0:T(8,128)(2,1)S(1)}, bf16[192,1536]{1,0:T(8,128)(2,1)S(1)}, u32[]{:S(2)}, u32[]{:S(2)}) collective-permute-start(bf16[192,1536]{1,0:T(8,128)(2,1)S(1)} %pad_maximum_fusion.6), channel_id=1, source_target_pairs={{0,4},{4,0},{8,12},{12,8},{16,20},{20,16},{24,28},{28,24},{1,5},{5... | collective-permute-start | bytes 1769480 | tf_op jit(solution)/shard_map/ppermute | solution.py:54
  70.6 107.8 %copy-start.20 = (bf16[96,1536]{1,0:T(8,128)(2,1)}, bf16[96,1536]{1,0:T(8,128)(2,1)S(1)}, u32[]{:S(2)}) copy-start(bf16[96,1536]{1,0:T(8,128)(2,1)S(1)} %collective-permute-done.5) | copy-start | bytes 884740
  73.0 1.6 collective-permute-start.6
  73.5 110.5 %copy-start.3 = (bf16[192,1536]{1,0:T(8,128)(2,1)}, bf16[192,1536]{1,0:T(8,128)(2,1)S(1)}, u32[]{:S(2)}) copy-start(bf16[192,1536]{1,0:T(8,128)(2,1)S(1)} %pad_maximum_fusion.8) | copy-start | bytes 1769476
  74.7 16.3 %collective-permute-start.7 = (bf16[192,1536]{1,0:T(8,128)(2,1)S(1)}, bf16[192,1536]{1,0:T(8,128)(2,1)S(1)}, u32[]{:S(2)}, u32[]{:S(2)}) collective-permute-start(bf16[192,1536]{1,0:T(8,128)(2,1)S(1)} %pad_maximum_fusion.5), channel_id=1, source_target_pairs={{16,0},{20,4},{8,24},{12,28},{24,16},{28,20},{0,8},{4,12},{17,1},{... | collective-permute-start | bytes 1769480 | tf_op jit(solution)/shard_map/ppermute | solution.py:38
  80.1 1.7 collective-permute-start.14
  80.3 2.3 collective-permute-start.10
  81.9 12.6 %collective-permute-start.15 = (bf16[192,1536]{1,0:T(8,128)(2,1)S(1)}, bf16[192,1536]{1,0:T(8,128)(2,1)S(1)}, u32[]{:S(2)}, u32[]{:S(2)}) collective-permute-start(bf16[192,1536]{1,0:T(8,128)(2,1)S(1)} %pad_maximum_fusion.9), channel_id=1, source_target_pairs={{0,24},{4,28},{24,0},{28,4},{1,25},{5,29},{25,1},{29,5},{2,26},{6,... | collective-permute-start | bytes 1769480 | tf_op jit(solution)/shard_map/ppermute | solution.py:38
  82.7 32.7 %collective-permute-start.11 = (bf16[192,1536]{1,0:T(8,128)(2,1)S(1)}, bf16[192,1536]{1,0:T(8,128)(2,1)S(1)}, u32[]{:S(2)}, u32[]{:S(2)}) collective-permute-start(bf16[192,1536]{1,0:T(8,128)(2,1)S(1)} %pad_maximum_fusion.7), channel_id=1, source_target_pairs={{0,8},{4,12},{8,0},{12,4},{16,24},{20,28},{24,16},{28,20},{1,9},{5... | collective-permute-start | bytes 1769480 | tf_op jit(solution)/shard_map/ppermute | solution.py:58
  91.6 27.7 %collective-permute-start.17 = (bf16[256,1536]{1,0:T(8,128)(2,1)S(1)}, bf16[256,1536]{1,0:T(8,128)(2,1)S(1)}, u32[]{:S(2)}, u32[]{:S(2)}) collective-permute-start(bf16[256,1536]{1,0:T(8,128)(2,1)S(1)} %convolution_convert_fusion.5), channel_id=1, source_target_pairs={{8,16},{12,20},{16,8},{20,12},{9,17},{13,21},{17,9},{21,13},{10,18... | collective-permute-start | bytes 2359304 | tf_op jit(solution)/shard_map/ppermute | solution.py:38
  123.8 37.7 %collective-permute-start.26 = (bf16[192,1536]{1,0:T(8,128)(2,1)S(1)}, bf16[192,1536]{1,0:T(8,128)(2,1)S(1)}, u32[]{:S(2)}, u32[]{:S(2)}) collective-permute-start(bf16[192,1536]{1,0:T(8,128)(2,1)S(1)} %convolution_convert_fusion.6), channel_id=1, source_target_pairs={{0,24},{4,28},{8,16},{12,20},{16,8},{20,12},{24,0},{28,4},{1,25},{... | collective-permute-start | bytes 1769480 | tf_op jit(solution)/shard_map/ppermute | solution.py:58
  125.9 47.4 %collective-permute-start.18 = (bf16[192,1536]{1,0:T(8,128)(2,1)S(1)}, bf16[192,1536]{1,0:T(8,128)(2,1)S(1)}, u32[]{:S(2)}, u32[]{:S(2)}) collective-permute-start(bf16[192,1536]{1,0:T(8,128)(2,1)S(1)} %convolution_convert_fusion.7), channel_id=1, source_target_pairs={{0,16},{4,20},{8,24},{12,28},{16,0},{20,4},{24,8},{28,12},{1,17},{... | collective-permute-start | bytes 1769480 | tf_op jit(solution)/shard_map/ppermute | solution.py:58
  126.1 47.3 %collective-permute-start.22 = (bf16[192,1536]{1,0:T(8,128)(2,1)S(1)}, bf16[192,1536]{1,0:T(8,128)(2,1)S(1)}, u32[]{:S(2)}, u32[]{:S(2)}) collective-permute-start(bf16[192,1536]{1,0:T(8,128)(2,1)S(1)} %slice.245), channel_id=1, source_target_pairs={{0,8},{4,12},{8,0},{12,4},{16,24},{20,28},{24,16},{28,20},{1,9},{5... | collective-permute-start | bytes 1769480 | tf_op jit(solution)/shard_map/ppermute | solution.py:58
  161.5 17.0 %collective-permute-start.27 = (bf16[96,1536]{1,0:T(8,128)(2,1)S(1)}, bf16[96,1536]{1,0:T(8,128)(2,1)S(1)}, u32[]{:S(2)}, u32[]{:S(2)}) collective-permute-start(bf16[96,1536]{1,0:T(8,128)(2,1)S(1)} %get-tuple-element.74), channel_id=1, source_target_pairs={{0,4},{4,0},{8,12},{12,8},{16,20},{20,16},{24,28},{28,24},{1,5},{5... | collective-permute-start | bytes 884744 | tf_op jit(solution)/shard_map/ppermute | solution.py:54
  173.3 1.6 collective-permute-start.19
  173.5 5.1 %collective-permute-start.23 = (bf16[192,1536]{1,0:T(8,128)(2,1)S(1)}, bf16[192,1536]{1,0:T(8,128)(2,1)S(1)}, u32[]{:S(2)}, u32[]{:S(2)}) collective-permute-start(bf16[192,1536]{1,0:T(8,128)(2,1)S(1)} %pad_maximum_fusion.12), channel_id=1, source_target_pairs={{0,4},{4,0},{8,12},{12,8},{16,20},{20,16},{24,28},{28,24},{1,5},{5... | collective-permute-start | bytes 1769480 | tf_op jit(solution)/shard_map/ppermute | solution.py:54
  178.2 27.3 %collective-permute-start.20 = (bf16[96,1536]{1,0:T(8,128)(2,1)}, bf16[96,1536]{1,0:T(8,128)(2,1)}, u32[]{:S(2)}, u32[]{:S(2)}) collective-permute-start(bf16[96,1536]{1,0:T(8,128)(2,1)} %get-tuple-element.60), channel_id=1, source_target_pairs={{0,4},{4,0},{8,12},{12,8},{16,20},{20,16},{24,28},{28,24},{1,5},{5... | collective-permute-start | bytes 884744 | tf_op jit(solution)/shard_map/ppermute | solution.py:54
  186.9 26.0 %collective-permute-start.28 = (bf16[96,1536]{1,0:T(8,128)(2,1)}, bf16[96,1536]{1,0:T(8,128)(2,1)}, u32[]{:S(2)}, u32[]{:S(2)}) collective-permute-start(bf16[96,1536]{1,0:T(8,128)(2,1)} %get-tuple-element.63), channel_id=1, source_target_pairs={{0,4},{4,0},{8,12},{12,8},{16,20},{20,16},{24,28},{28,24},{1,5},{5... | collective-permute-start | bytes 884744 | tf_op jit(solution)/shard_map/ppermute | solution.py:54
  187.2 26.7 %collective-permute-start.24 = (bf16[192,1536]{1,0:T(8,128)(2,1)}, bf16[192,1536]{1,0:T(8,128)(2,1)}, u32[]{:S(2)}, u32[]{:S(2)}) collective-permute-start(bf16[192,1536]{1,0:T(8,128)(2,1)} %slice.250), channel_id=1, source_target_pairs={{0,4},{4,0},{8,12},{12,8},{16,20},{20,16},{24,28},{28,24},{1,5},{5... | collective-permute-start | bytes 1769480 | tf_op jit(solution)/shard_map/ppermute | solution.py:54
  190.7 18.3 %all-to-all-start = ((f32[8,24,128]{2,1,0:T(8,128)}), f32[8,24,128]{2,1,0:T(8,128)}, u32[]{:S(2)}, u32[]{:S(2)}) async-start(f32[8,24,128]{2,1,0:T(8,128)} %broadcast_in_dim.71), calls=%async_computation | async-start | bytes 196608 | tf_op jit(solution)/shard_map/all_to_all | solution.py:62
  206.6 16.4 %collective-permute-start.21 = (bf16[192,1536]{1,0:T(8,128)(2,1)S(1)}, bf16[192,1536]{1,0:T(8,128)(2,1)}, u32[]{:S(2)}, u32[]{:S(2)}) collective-permute-start(bf16[192,1536]{1,0:T(8,128)(2,1)S(1)} %pad_maximum_fusion.11), channel_id=1, source_target_pairs={{16,0},{20,4},{8,24},{12,28},{24,16},{28,20},{0,8},{4,12},{17,1},{... | collective-permute-start | bytes 1769480 | tf_op jit(solution)/shard_map/ppermute | solution.py:38
  215.1 20.3 %collective-permute-start.25 = (bf16[192,1536]{1,0:T(8,128)(2,1)S(1)}, bf16[192,1536]{1,0:T(8,128)(2,1)S(1)}, u32[]{:S(2)}, u32[]{:S(2)}) collective-permute-start(bf16[192,1536]{1,0:T(8,128)(2,1)S(1)} %pad_maximum_fusion.13), channel_id=1, source_target_pairs={{0,8},{4,12},{8,0},{12,4},{16,24},{20,28},{24,16},{28,20},{1,9},{5... | collective-permute-start | bytes 1769480 | tf_op jit(solution)/shard_map/ppermute | solution.py:58
  215.2 23.3 %collective-permute-start.29 = (bf16[192,1152]{1,0:T(8,128)(2,1)S(1)}, bf16[192,1152]{1,0:T(8,128)(2,1)S(1)}, u32[]{:S(2)}, u32[]{:S(2)}) collective-permute-start(bf16[192,1152]{1,0:T(8,128)(2,1)S(1)} %pad_maximum_fusion.16), channel_id=1, source_target_pairs={{0,24},{4,28},{24,0},{28,4},{1,25},{5,29},{25,1},{29,5},{2,26},{6,... | collective-permute-start | bytes 1327112 | tf_op jit(solution)/shard_map/ppermute | solution.py:38
  215.9 43.4 %collective-permute-start.34 = (bf16[192,384]{1,0:T(8,128)(2,1)S(1)}, bf16[192,384]{1,0:T(8,128)(2,1)S(1)}, u32[]{:S(2)}, u32[]{:S(2)}) collective-permute-start(bf16[192,384]{1,0:T(8,128)(2,1)S(1)} %get-tuple-element.52), channel_id=1, source_target_pairs={{0,24},{4,28},{24,0},{28,4},{1,25},{5,29},{25,1},{29,5},{2,26},{6,... | collective-permute-start | bytes 442376 | tf_op jit(solution)/shard_map/ppermute | solution.py:38
  224.9 30.3 %collective-permute-start.30 = (bf16[256,1152]{1,0:T(8,128)(2,1)S(1)}, bf16[256,1152]{1,0:T(8,128)(2,1)S(1)}, u32[]{:S(2)}, u32[]{:S(2)}) collective-permute-start(bf16[256,1152]{1,0:T(8,128)(2,1)S(1)} %pad_maximum_fusion.15), channel_id=1, source_target_pairs={{8,16},{12,20},{16,8},{20,12},{9,17},{13,21},{17,9},{21,13},{10,18... | collective-permute-start | bytes 1769480 | tf_op jit(solution)/shard_map/ppermute | solution.py:38
  228.3 31.4 %collective-permute-start.35 = (bf16[256,384]{1,0:T(8,128)(2,1)S(1)}, bf16[256,384]{1,0:T(8,128)(2,1)S(1)}, u32[]{:S(2)}, u32[]{:S(2)}) collective-permute-start(bf16[256,384]{1,0:T(8,128)(2,1)S(1)} %get-tuple-element.45), channel_id=1, source_target_pairs={{8,16},{12,20},{16,8},{20,12},{9,17},{13,21},{17,9},{21,13},{10,18... | collective-permute-start | bytes 589832 | tf_op jit(solution)/shard_map/ppermute | solution.py:38
  238.4 16.7 %copy-start.36 = (s32[192]{0:T(256)S(1)}, s32[192]{0:T(256)}, u32[]{:S(2)}) copy-start(s32[192]{0:T(256)} %copy-done.34) | copy-start | bytes 2308
  255.7 6.7 %collective-permute-start.31 = (bf16[256,384]{1,0:T(8,128)(2,1)S(1)}, bf16[256,384]{1,0:T(8,128)(2,1)S(1)}, u32[]{:S(2)}, u32[]{:S(2)}) collective-permute-start(bf16[256,384]{1,0:T(8,128)(2,1)S(1)} %get-tuple-element.58), channel_id=1, source_target_pairs={{0,3},{1,2},{2,1},{3,0},{4,7},{5,6},{6,5},{7,4},{8,11},{9,10},{10,... | collective-permute-start | bytes 589832 | tf_op jit(solution)/shard_map/ppermute | solution.py:98
  256.8 7.7 %collective-permute-start.32 = (bf16[256,384]{1,0:T(8,128)(2,1)S(1)}, bf16[256,384]{1,0:T(8,128)(2,1)S(1)}, u32[]{:S(2)}, u32[]{:S(2)}) collective-permute-start(bf16[256,384]{1,0:T(8,128)(2,1)S(1)} %get-tuple-element.57), channel_id=1, source_target_pairs={{0,2},{1,3},{2,0},{3,1},{4,6},{5,7},{6,4},{7,5},{8,10},{9,11},{10,... | collective-permute-start | bytes 589832 | tf_op jit(solution)/shard_map/ppermute | solution.py:98
  258.8 5.8 %collective-permute-start.33 = (bf16[256,384]{1,0:T(8,128)(2,1)S(1)}, bf16[256,384]{1,0:T(8,128)(2,1)S(1)}, u32[]{:S(2)}, u32[]{:S(2)}) collective-permute-start(bf16[256,384]{1,0:T(8,128)(2,1)S(1)} %get-tuple-element.56), channel_id=1, source_target_pairs={{0,1},{1,0},{2,3},{3,2},{4,5},{5,4},{6,7},{7,6},{8,9},{9,8},{10,11... | collective-permute-start | bytes 589832 | tf_op jit(solution)/shard_map/ppermute | solution.py:98
  (37 other events, 154.5 us)

commit v6 on v5

--- a/solution.py
+++ b/solution.py
@@ -1,6 +1,8 @@
 import jax
 import jax.numpy as jnp
 from jax import lax
+from jax.experimental import pallas as pl
+from jax.experimental.pallas import tpu as pltpu
 from jax.sharding import PartitionSpec as P
 
 
@@ -84,6 +86,30 @@
             block = jnp.where(mine ^ t == k, pieces[k], block)
         blocks.append(block)
     return jnp.concatenate(blocks, axis=1)
+
+
+def place_kernel(mine_ref, *refs):
+    pieces, out = refs[:-1], refs[-1]
+    head = pieces[0].shape[1]
+    for own in range(len(pieces)):
+
+        @pl.when(mine_ref[0] == own)
+        def _():
+            for t in range(len(pieces)):
+                out[:, t * head : (t + 1) * head] = pieces[own ^ t][...]
+
+
+def placed(pieces):
+    rows, head = pieces[0].shape
+    mine = lax.axis_index("expert").astype(jnp.int32).reshape(1)
+    return pl.pallas_call(
+        place_kernel,
+        out_shape=jax.ShapeDtypeStruct((rows, head * len(pieces)), pieces[0].dtype),
+        in_specs=[pl.BlockSpec(memory_space=pltpu.SMEM)]
+        + [pl.BlockSpec(memory_space=pltpu.VMEM)] * len(pieces),
+        out_specs=pl.BlockSpec(memory_space=pltpu.VMEM),
+        compiler_params=pltpu.CompilerParams(vmem_limit_bytes=4 * 1024 * 1024),
+    )(mine, *pieces)
 
 
 def cut(rows, width):
@@ -178,7 +204,8 @@
         return jnp.concatenate([rows[:depth], swap_cores(rows[depth:])])
 
     def far_sum(pair, passed):
-        return dot(place_far, jnp.concatenate([pair, passed]), ((0,), (0,))).astype(jnp.bfloat16)
+        both = jnp.concatenate([pair, passed])
+        return dot(place_far, both, ((0,), (0,))).astype(jnp.bfloat16)
 
     def give_back(group, rows):
         if line and group == groups[0]:
@@ -286,7 +313,7 @@
         last_block = after(last_block, main)
         start = start + dot(placers[-1], last_block, ((0,), (0,)))
         start = (start + last_crossed.astype(jnp.float32) if line else start).astype(jnp.bfloat16)
-        grad_tokens = in_order(swap_heads([start] + cut(main, model_width)))
+        grad_tokens = placed(swap_heads([start] + cut(main, model_width)))
     else:
         grad_tokens = mix_heads(collect(grad_resid, parts).astype(jnp.bfloat16))
 

time: 267 us -> 268 us (level)
  waiting for transfers between devices: 152 us -> 156 us
    ppermute x9, waiting for transfers between devices: 110 us -> 116 us  [to_chip(): lax.ppermute(rows, 'dp', xor_pairs(lax.axis_size('dp'), 2 * k))]
  transfers between devices with their start and end apart: 37 -> 37, of which waited for: 19 -> 17; matrix products, arithmetic and copies ran while one was open for 20% -> 21% of each run, Pallas kernels for 0% -> 0%
where the time goes in v6:
time: 268 us; the launch traced here: 267 us
  waiting for transfers between devices  156 us (58%)
  starting transfers between devices  43.4 us (16%)
  matrix products  31.4 us (12%)
  local copies, waits for them, and re-layouts  17.6 us (7%)
  other arithmetic  16 us (6%)
    ppermute x9, waiting for transfers between devices, to_chip(): lax.ppermute(rows, 'dp', xor_pairs(lax.axis_size('dp'), 2 * k))  116 us
    ppermute x9, waiting for transfers between devices, move(): return lax.ppermute(rows, 'dp', pairs)  33.3 us
    dot_general x33, matrix products, dot(): lax.dot_general(a, b, (dims, ((), ())), preferred_element_type=jnp.float32)  31.4 us
    ppermute x9, starting transfers between devices, to_chip(): lax.ppermute(rows, 'dp', xor_pairs(lax.axis_size('dp'), 2 * k))  14.4 us
    ppermute x9, starting transfers between devices, move(): return lax.ppermute(rows, 'dp', pairs)  14.4 us
    ppermute x6, starting transfers between devices, swap_heads(): moved.append(lax.ppermute(piece, 'expert', pairs) if k else piece)  7.04 us
    ppermute x6, waiting for transfers between devices, swap_heads(): moved.append(lax.ppermute(piece, 'expert', pairs) if k else piece)  5.65 us
  transfers between devices with their start and end apart: 37, of which 17 were waited for; matrix products, arithmetic and copies ran while one was open for 21% of the time, Pallas kernels for 0%

profile of v6, /device:TPU:8, one launch (start us, length us, event | category | flops | bytes accessed | tf_op | source)
XLA Modules:
  0.0 267.3 jit_solution(6942247510016977660)
XLA Ops:
  0.7 2.1 dynamic-slice_bitcast_fusion
  2.8 2.4 collective-permute-start
  6.8 1.1 reduce-window.6
  9.4 2.6 collective-permute-start.4
  12.0 1.9 collective-permute-start.16
  15.4 2.3 collective-permute-done.16
  18.6 1.4 convolution_convert_fusion.9
  20.2 1.4 fusion.144
  22.1 4.0 %collective-permute-start.8 = (bf16[192,1536]{1,0:T(8,128)(2,1)S(1)}, bf16[192,1536]{1,0:T(8,128)(2,1)S(1)}, u32[]{:S(2)}, u32[]{:S(2)}) collective-permute-start(bf16[192,1536]{1,0:T(8,128)(2,1)S(1)} %slice.225), channel_id=1, source_target_pairs={{0,8},{4,12},{8,0},{12,4},{16,24},{20,28},{24,16},{28,20},{1,9},{5... | collective-permute-start | bytes 1769480 | tf_op jit(solution)/shard_map/ppermute | solution.py:60
  26.6 13.6 %collective-permute-done.3 = bf16[192,1152]{1,0:T(8,128)(2,1)S(1)} collective-permute-done((bf16[192,1152]{1,0:T(8,128)(2,1)S(1)}, bf16[192,1152]{1,0:T(8,128)(2,1)S(1)}, u32[]{:S(2)}, u32[]{:S(2)}) %collective-permute-start.3) | collective-permute-done | bytes 442400 | tf_op jit(solution)/shard_map/ppermute | solution.py:60
  40.6 19.1 %collective-permute-done.8 = bf16[192,1536]{1,0:T(8,128)(2,1)S(1)} collective-permute-done((bf16[192,1536]{1,0:T(8,128)(2,1)S(1)}, bf16[192,1536]{1,0:T(8,128)(2,1)S(1)}, u32[]{:S(2)}, u32[]{:S(2)}) %collective-permute-start.8) | collective-permute-done | bytes 589856 | tf_op jit(solution)/shard_map/ppermute | solution.py:60
  59.8 7.4 %collective-permute-done.12 = bf16[192,1536]{1,0:T(8,128)(2,1)S(1)} collective-permute-done((bf16[192,1536]{1,0:T(8,128)(2,1)S(1)}, bf16[192,1536]{1,0:T(8,128)(2,1)S(1)}, u32[]{:S(2)}, u32[]{:S(2)}) %collective-permute-start.12) | collective-permute-done | bytes 589856 | tf_op jit(solution)/shard_map/ppermute | solution.py:60
  71.2 1.2 fusion.76
  77.5 1.2 fusion.136
  79.5 4.0 %collective-permute-start.11 = (bf16[192,1536]{1,0:T(8,128)(2,1)S(1)}, bf16[192,1536]{1,0:T(8,128)(2,1)S(1)}, u32[]{:S(2)}, u32[]{:S(2)}) collective-permute-start(bf16[192,1536]{1,0:T(8,128)(2,1)S(1)} %pad_maximum_fusion.7), channel_id=1, source_target_pairs={{0,8},{4,12},{8,0},{12,4},{16,24},{20,28},{24,16},{28,20},{1,9},{5... | collective-permute-start | bytes 1769480 | tf_op jit(solution)/shard_map/ppermute | solution.py:60
  83.5 3.8 %collective-permute-done.7 = bf16[192,1536]{1,0:T(8,128)(2,1)S(1)} collective-permute-done((bf16[192,1536]{1,0:T(8,128)(2,1)S(1)}, bf16[192,1536]{1,0:T(8,128)(2,1)S(1)}, u32[]{:S(2)}, u32[]{:S(2)}) %collective-permute-start.7) | collective-permute-done | bytes 589856 | tf_op jit(solution)/shard_map/ppermute | solution.py:40
  87.9 2.1 collective-permute-start.17
  91.0 21.0 %collective-permute-done.11 = bf16[192,1536]{1,0:T(8,128)(2,1)S(1)} collective-permute-done((bf16[192,1536]{1,0:T(8,128)(2,1)S(1)}, bf16[192,1536]{1,0:T(8,128)(2,1)S(1)}, u32[]{:S(2)}, u32[]{:S(2)}) %collective-permute-start.11) | collective-permute-done | bytes 589856 | tf_op jit(solution)/shard_map/ppermute | solution.py:60
  112.7 2.8 %collective-permute-done.17 = bf16[256,1536]{1,0:T(8,128)(2,1)S(1)} collective-permute-done((bf16[256,1536]{1,0:T(8,128)(2,1)S(1)}, bf16[256,1536]{1,0:T(8,128)(2,1)S(1)}, u32[]{:S(2)}, u32[]{:S(2)}) %collective-permute-start.17) | collective-permute-done | bytes 786464 | tf_op jit(solution)/shard_map/ppermute | solution.py:40
  117.6 1.4 fusion.47
  120.6 3.5 %collective-permute-start.18 = (bf16[192,1536]{1,0:T(8,128)(2,1)S(1)}, bf16[192,1536]{1,0:T(8,128)(2,1)S(1)}, u32[]{:S(2)}, u32[]{:S(2)}) collective-permute-start(bf16[192,1536]{1,0:T(8,128)(2,1)S(1)} %convolution_convert_fusion.7), channel_id=1, source_target_pairs={{0,16},{4,20},{8,24},{12,28},{16,0},{20,4},{24,8},{28,12},{1,17},{... | collective-permute-start | bytes 1769480 | tf_op jit(solution)/shard_map/ppermute | solution.py:60
  124.2 20.9 %collective-permute-done.22 = bf16[192,1536]{1,0:T(8,128)(2,1)S(1)} collective-permute-done((bf16[192,1536]{1,0:T(8,128)(2,1)S(1)}, bf16[192,1536]{1,0:T(8,128)(2,1)S(1)}, u32[]{:S(2)}, u32[]{:S(2)}) %collective-permute-start.22) | collective-permute-done | bytes 589856 | tf_op jit(solution)/shard_map/ppermute | solution.py:60
  145.3 17.8 %collective-permute-done.18 = bf16[192,1536]{1,0:T(8,128)(2,1)S(1)} collective-permute-done((bf16[192,1536]{1,0:T(8,128)(2,1)S(1)}, bf16[192,1536]{1,0:T(8,128)(2,1)S(1)}, u32[]{:S(2)}, u32[]{:S(2)}) %collective-permute-start.18) | collective-permute-done | bytes 589856 | tf_op jit(solution)/shard_map/ppermute | solution.py:60
  163.2 11.6 %collective-permute-done.26 = bf16[192,1536]{1,0:T(8,128)(2,1)S(1)} collective-permute-done((bf16[192,1536]{1,0:T(8,128)(2,1)S(1)}, bf16[192,1536]{1,0:T(8,128)(2,1)S(1)}, u32[]{:S(2)}, u32[]{:S(2)}) %collective-permute-start.26) | collective-permute-done | bytes 589856 | tf_op jit(solution)/shard_map/ppermute | solution.py:60
  180.5 1.1 fusion.53
  181.6 1.1 fusion.3
  184.5 1.2 fusion.71
  187.1 1.3 broadcast_in_dim.70
  188.4 1.3 broadcast_in_dim.71
  189.7 5.0 %all-to-all-start = ((f32[8,24,128]{2,1,0:T(8,128)}), f32[8,24,128]{2,1,0:T(8,128)}, u32[]{:S(2)}, u32[]{:S(2)}) async-start(f32[8,24,128]{2,1,0:T(8,128)} %broadcast_in_dim.71), calls=%async_computation | async-start | bytes 196608 | tf_op jit(solution)/shard_map/all_to_all | solution.py:64
  194.7 2.3 fusion.62
  199.5 3.5 %fusion = bf16[1,1,1536,768]{3,2,1,0:T(8,128)(2,1)} fusion(bf16[192,1536]{1,0:T(8,128)(2,1)S(1)} %copy-done.4, bf16[384,1536]{1,0:T(8,128)(2,1)S(1)} %pad_maximum_fusion, bf16[96,1536]{1,0:T(8,128)(2,1)S(1)} %copy-done.22, bf16[96,1536]{1,0:T(8,128)(2,1)S(1)} %copy-done.10, bf16[192,768]{1,0:T(8,128)(2,1)S(1)} %fusion.62, ...), kind=kOutput, calls=%fused_computation.3 | convolution fusion | flops 1826095104 | bytes 5898240 | tf_op jit(solution)/shard_map/dot_general | solution.py:44
  203.0 3.4 %fusion.1 = bf16[1,1,768,1536]{3,2,1,0:T(8,128)(2,1)} fusion(bf16[192,1536]{1,0:T(8,128)(2,1)S(1)} %copy-done.8, bf16[384,1536]{1,0:T(8,128)(2,1)S(1)} %copy-done.12, bf16[192,1536]{1,0:T(8,128)(2,1)S(1)} %copy-done.7, bf16[192,768]{1,0:T(8,128)(2,1)S(1)} %copy-done.20, bf16[384,768]{1,0:T(8,128)(2,1)S(1)} %copy-done.54, bf16[192,768]{1,0:T(8,128)(2,1)S(1)} %copy-done.18), kind=kOutput, calls=%fused_computation.4 | convolution fusion | flops 1823735808 | bytes 5898240 | tf_op jit(solution)/shard_map/dot_general | solution.py:44
  207.5 2.4 collective-permute-start.21
  212.2 1.1 fusion.155
  213.3 1.1 fusion.196
  216.0 7.9 %collective-permute-done.21 = bf16[192,1536]{1,0:T(8,128)(2,1)} collective-permute-done((bf16[192,1536]{1,0:T(8,128)(2,1)S(1)}, bf16[192,1536]{1,0:T(8,128)(2,1)}, u32[]{:S(2)}, u32[]{:S(2)}) %collective-permute-start.21) | collective-permute-done | bytes 589856 | tf_op jit(solution)/shard_map/ppermute | solution.py:40
  223.9 1.8 convolution_convert_fusion.4
  225.9 3.4 %collective-permute-start.31 = (bf16[256,1152]{1,0:T(8,128)(2,1)S(1)}, bf16[256,1152]{1,0:T(8,128)(2,1)S(1)}, u32[]{:S(2)}, u32[]{:S(2)}) collective-permute-start(bf16[256,1152]{1,0:T(8,128)(2,1)S(1)} %pad_maximum_fusion.15), channel_id=1, source_target_pairs={{8,16},{12,20},{16,8},{20,12},{9,17},{13,21},{17,9},{21,13},{10,18... | collective-permute-start | bytes 1769480 | tf_op jit(solution)/shard_map/ppermute | solution.py:40
  229.2 2.5 collective-permute-start.32
  231.7 4.7 %collective-permute-done.25 = bf16[192,1536]{1,0:T(8,128)(2,1)S(1)} collective-permute-done((bf16[192,1536]{1,0:T(8,128)(2,1)S(1)}, bf16[192,1536]{1,0:T(8,128)(2,1)S(1)}, u32[]{:S(2)}, u32[]{:S(2)}) %collective-permute-start.25) | collective-permute-done | bytes 589856 | tf_op jit(solution)/shard_map/ppermute | solution.py:60
  237.8 1.5 fusion.4
  239.5 16.6 %collective-permute-done.31 = bf16[256,1152]{1,0:T(8,128)(2,1)S(1)} collective-permute-done((bf16[256,1152]{1,0:T(8,128)(2,1)S(1)}, bf16[256,1152]{1,0:T(8,128)(2,1)S(1)}, u32[]{:S(2)}, u32[]{:S(2)}) %collective-permute-start.31) | collective-permute-done | bytes 589856 | tf_op jit(solution)/shard_map/ppermute | solution.py:40
  256.7 1.6 collective-permute-start.33
  258.3 1.5 collective-permute-start.34
  260.7 1.7 collective-permute-done.33.refs_1_
  262.4 2.7 %collective-permute-done.34.refs_2_ = bf16[256,384]{1,0:T(8,128)(2,1)S(1)} collective-permute-done((bf16[256,384]{1,0:T(8,128)(2,1)S(1)}, bf16[256,384]{1,0:T(8,128)(2,1)S(1)}, u32[]{:S(2)}, u32[]{:S(2)}) %collective-permute-start.34) | collective-permute-done | bytes 196640 | tf_op jit(solution)/shard_map/ppermute | solution.py:124
  265.1 1.2 collective-permute-done.35.refs_3_
  (270 shorter events, 42.7 us)
Async XLA Ops:
  0.6 67.9 %copy-start = (bf16[1,1,768,1536]{3,2,1,0:T(8,128)(2,1)S(1)}, bf16[1,1,768,1536]{3,2,1,0:T(8,128)(2,1)}, u32[]{:S(2)}) copy-start(bf16[1,1,768,1536]{3,2,1,0:T(8,128)(2,1)} %param.12) | copy-start | bytes 7077892
  0.7 14.0 %copy-start.26 = (bf16[1,1536,8]{1,2,0:T(8,128)(2,1)S(1)}, bf16[1,1536,8]{1,2,0:T(8,128)(2,1)}, u32[]{:S(2)}) copy-start(bf16[1,1536,8]{1,2,0:T(8,128)(2,1)} %param.9) | copy-start | bytes 73732
  0.7 14.7 %copy-start.46 = (f32[1,1536]{1,0:T(1,128)S(1)}, f32[1,1536]{1,0:T(1,128)}, u32[]{:S(2)}) copy-start(f32[1,1536]{1,0:T(1,128)} %param.10) | copy-start | bytes 18436
  2.8 15.8 %collective-permute-start = (bf16[256,384]{1,0:T(8,128)(2,1)}, bf16[256,384]{1,0:T(8,128)(2,1)}, u32[]{:S(2)}, u32[]{:S(2)}) collective-permute-start(bf16[256,384]{1,0:T(8,128)(2,1)} %get-tuple-element.46), channel_id=1, source_target_pairs={{0,3},{1,2},{2,1},{3,0},{4,7},{5,6},{6,5},{7,4},{8,11},{9,10},{10,... | collective-permute-start | bytes 589832 | tf_op jit(solution)/shard_map/ppermute | solution.py:124
  5.2 13.3 %collective-permute-start.1 = (bf16[256,384]{1,0:T(8,128)(2,1)}, bf16[256,384]{1,0:T(8,128)(2,1)}, u32[]{:S(2)}, u32[]{:S(2)}) collective-permute-start(bf16[256,384]{1,0:T(8,128)(2,1)} %get-tuple-element.45), channel_id=1, source_target_pairs={{0,2},{1,3},{2,0},{3,1},{4,6},{5,7},{6,4},{7,5},{8,10},{9,11},{10,... | collective-permute-start | bytes 589832 | tf_op jit(solution)/shard_map/ppermute | solution.py:124
  5.8 12.9 %collective-permute-start.2 = (bf16[256,384]{1,0:T(8,128)(2,1)S(1)}, bf16[256,384]{1,0:T(8,128)(2,1)}, u32[]{:S(2)}, u32[]{:S(2)}) collective-permute-start(bf16[256,384]{1,0:T(8,128)(2,1)S(1)} %get-tuple-element.44), channel_id=1, source_target_pairs={{0,1},{1,0},{2,3},{3,2},{4,5},{5,4},{6,7},{7,6},{8,9},{9,8},{10,11... | collective-permute-start | bytes 589832 | tf_op jit(solution)/shard_map/ppermute | solution.py:124
  6.7 13.3 %copy-start.39 = (s32[192]{0:T(256)}, s32[192]{0:T(256)S(1)}, u32[]{:S(2)}) copy-start(s32[192]{0:T(256)S(1)} %iota_add_fusion.2) | copy-start | bytes 2308
  9.4 17.2 %collective-permute-start.4 = (bf16[192,384]{1,0:T(8,128)(2,1)}, bf16[192,384]{1,0:T(8,128)(2,1)S(1)}, u32[]{:S(2)}, u32[]{:S(2)}) collective-permute-start(bf16[192,384]{1,0:T(8,128)(2,1)} %convolution_convert_fusion.10), channel_id=1, source_target_pairs={{0,16},{4,20},{8,24},{12,28},{16,0},{20,4},{24,8},{28,12},{1,17},{... | collective-permute-start | bytes 442376 | tf_op jit(solution)/shard_map/ppermute | solution.py:60
  12.0 5.7 %collective-permute-start.16 = (s32[2,256]{1,0:T(2,128)S(1)}, s32[2,256]{1,0:T(2,128)}, u32[]{:S(2)}, u32[]{:S(2)}) collective-permute-start(s32[2,256]{1,0:T(2,128)S(1)} %bitcast.167), channel_id=1, source_target_pairs={{8,16},{12,20},{16,8},{20,12},{9,17},{13,21},{17,9},{21,13},{10,18... | collective-permute-start | bytes 6152 | tf_op jit(solution)/shard_map/ppermute | solution.py:40
  14.0 53.6 %copy-start.43 = (pred[8]{0:T(512)(128)(4,1)}, pred[8]{0:T(512)(128)(4,1)S(1)}, u32[]{:S(2)}) copy-start(pred[8]{0:T(512)(128)(4,1)S(1)} %iota_compare_fusion.4) | copy-start | bytes 28
  18.6 68.7 %copy-start.32 = (pred[192,256]{1,0:T(32,128)(4,1)}, pred[192,256]{1,0:T(32,128)(4,1)S(1)}, u32[]{:S(2)}) copy-start(pred[192,256]{1,0:T(32,128)(4,1)S(1)} %get-tuple-element.87) | copy-start | bytes 147460
  18.6 68.7 %copy-start.34 = (pred[192,256]{1,0:T(32,128)(4,1)}, pred[192,256]{1,0:T(32,128)(4,1)S(1)}, u32[]{:S(2)}) copy-start(pred[192,256]{1,0:T(32,128)(4,1)S(1)} %get-tuple-element.88) | copy-start | bytes 147460
  20.1 20.2 %collective-permute-start.3 = (bf16[192,1152]{1,0:T(8,128)(2,1)S(1)}, bf16[192,1152]{1,0:T(8,128)(2,1)S(1)}, u32[]{:S(2)}, u32[]{:S(2)}) collective-permute-start(bf16[192,1152]{1,0:T(8,128)(2,1)S(1)} %convolution_convert_fusion.9), channel_id=1, source_target_pairs={{0,16},{4,20},{8,24},{12,28},{16,0},{20,4},{24,8},{28,12},{1,17},{... | collective-permute-start | bytes 1327112 | tf_op jit(solution)/shard_map/ppermute | solution.py:60
  22.1 37.5 %collective-permute-start.8 = (bf16[192,1536]{1,0:T(8,128)(2,1)S(1)}, bf16[192,1536]{1,0:T(8,128)(2,1)S(1)}, u32[]{:S(2)}, u32[]{:S(2)}) collective-permute-start(bf16[192,1536]{1,0:T(8,128)(2,1)S(1)} %slice.225), channel_id=1, source_target_pairs={{0,8},{4,12},{8,0},{12,4},{16,24},{20,28},{24,16},{28,20},{1,9},{5... | collective-permute-start | bytes 1769480 | tf_op jit(solution)/shard_map/ppermute | solution.py:60
  26.5 40.7 %collective-permute-start.12 = (bf16[192,1536]{1,0:T(8,128)(2,1)S(1)}, bf16[192,1536]{1,0:T(8,128)(2,1)S(1)}, u32[]{:S(2)}, u32[]{:S(2)}) collective-permute-start(bf16[192,1536]{1,0:T(8,128)(2,1)S(1)} %convolution_convert_fusion.8), channel_id=1, source_target_pairs={{0,24},{4,28},{8,16},{12,20},{16,8},{20,12},{24,0},{28,4},{1,25},{... | collective-permute-start | bytes 1769480 | tf_op jit(solution)/shard_map/ppermute | solution.py:60
  40.5 134.8 %copy-start.9 = (bf16[96,1536]{1,0:T(8,128)(2,1)}, bf16[96,1536]{1,0:T(8,128)(2,1)S(1)}, u32[]{:S(2)}) copy-start(bf16[96,1536]{1,0:T(8,128)(2,1)S(1)} %get-tuple-element.80) | copy-start | bytes 884740
  40.5 26.8 %collective-permute-start.5 = (bf16[96,1536]{1,0:T(8,128)(2,1)S(1)}, bf16[96,1536]{1,0:T(8,128)(2,1)S(1)}, u32[]{:S(2)}, u32[]{:S(2)}) collective-permute-start(bf16[96,1536]{1,0:T(8,128)(2,1)S(1)} %get-tuple-element.81), channel_id=1, source_target_pairs={{0,4},{4,0},{8,12},{12,8},{16,20},{20,16},{24,28},{28,24},{1,5},{5... | collective-permute-start | bytes 884744 | tf_op jit(solution)/shard_map/ppermute | solution.py:56
  59.8 11.3 %collective-permute-start.9 = (bf16[192,1536]{1,0:T(8,128)(2,1)S(1)}, bf16[192,1536]{1,0:T(8,128)(2,1)S(1)}, u32[]{:S(2)}, u32[]{:S(2)}) collective-permute-start(bf16[192,1536]{1,0:T(8,128)(2,1)S(1)} %pad_maximum_fusion.6), channel_id=1, source_target_pairs={{0,4},{4,0},{8,12},{12,8},{16,20},{20,16},{24,28},{28,24},{1,5},{5... | collective-permute-start | bytes 1769480 | tf_op jit(solution)/shard_map/ppermute | solution.py:56
  67.3 2.9 %collective-permute-start.13 = (bf16[96,1536]{1,0:T(8,128)(2,1)S(1)}, bf16[96,1536]{1,0:T(8,128)(2,1)S(1)}, u32[]{:S(2)}, u32[]{:S(2)}) collective-permute-start(bf16[96,1536]{1,0:T(8,128)(2,1)S(1)} %get-tuple-element.77), channel_id=1, source_target_pairs={{0,4},{4,0},{8,12},{12,8},{16,20},{20,16},{24,28},{28,24},{1,5},{5... | collective-permute-start | bytes 884744 | tf_op jit(solution)/shard_map/ppermute | solution.py:56
  67.4 108.0 %copy-start.21 = (bf16[96,1536]{1,0:T(8,128)(2,1)}, bf16[96,1536]{1,0:T(8,128)(2,1)S(1)}, u32[]{:S(2)}) copy-start(bf16[96,1536]{1,0:T(8,128)(2,1)S(1)} %collective-permute-done.5) | copy-start | bytes 884740
  69.2 1.8 collective-permute-start.6
  70.2 115.5 %copy-start.3 = (bf16[192,1536]{1,0:T(8,128)(2,1)}, bf16[192,1536]{1,0:T(8,128)(2,1)S(1)}, u32[]{:S(2)}) copy-start(bf16[192,1536]{1,0:T(8,128)(2,1)S(1)} %pad_maximum_fusion.8) | copy-start | bytes 1769476
  71.0 16.3 %collective-permute-start.7 = (bf16[192,1536]{1,0:T(8,128)(2,1)S(1)}, bf16[192,1536]{1,0:T(8,128)(2,1)S(1)}, u32[]{:S(2)}, u32[]{:S(2)}) collective-permute-start(bf16[192,1536]{1,0:T(8,128)(2,1)S(1)} %pad_maximum_fusion.5), channel_id=1, source_target_pairs={{16,0},{20,4},{8,24},{12,28},{24,16},{28,20},{0,8},{4,12},{17,1},{... | collective-permute-start | bytes 1769480 | tf_op jit(solution)/shard_map/ppermute | solution.py:40
  76.2 2.5 collective-permute-start.14
  76.6 2.8 %collective-permute-start.10 = (bf16[192,1536]{1,0:T(8,128)(2,1)S(1)}, bf16[192,1536]{1,0:T(8,128)(2,1)S(1)}, u32[]{:S(2)}, u32[]{:S(2)}) collective-permute-start(bf16[192,1536]{1,0:T(8,128)(2,1)S(1)} %slice.230), channel_id=1, source_target_pairs={{0,4},{4,0},{8,12},{12,8},{16,20},{20,16},{24,28},{28,24},{1,5},{5... | collective-permute-start | bytes 1769480 | tf_op jit(solution)/shard_map/ppermute | solution.py:56
  78.7 11.8 %collective-permute-start.15 = (bf16[192,1536]{1,0:T(8,128)(2,1)S(1)}, bf16[192,1536]{1,0:T(8,128)(2,1)S(1)}, u32[]{:S(2)}, u32[]{:S(2)}) collective-permute-start(bf16[192,1536]{1,0:T(8,128)(2,1)S(1)} %pad_maximum_fusion.9), channel_id=1, source_target_pairs={{0,24},{4,28},{24,0},{28,4},{1,25},{5,29},{25,1},{29,5},{2,26},{6,... | collective-permute-start | bytes 1769480 | tf_op jit(solution)/shard_map/ppermute | solution.py:40
  79.5 32.5 %collective-permute-start.11 = (bf16[192,1536]{1,0:T(8,128)(2,1)S(1)}, bf16[192,1536]{1,0:T(8,128)(2,1)S(1)}, u32[]{:S(2)}, u32[]{:S(2)}) collective-permute-start(bf16[192,1536]{1,0:T(8,128)(2,1)S(1)} %pad_maximum_fusion.7), channel_id=1, source_target_pairs={{0,8},{4,12},{8,0},{12,4},{16,24},{20,28},{24,16},{28,20},{1,9},{5... | collective-permute-start | bytes 1769480 | tf_op jit(solution)/shard_map/ppermute | solution.py:60
  87.9 27.5 %collective-permute-start.17 = (bf16[256,1536]{1,0:T(8,128)(2,1)S(1)}, bf16[256,1536]{1,0:T(8,128)(2,1)S(1)}, u32[]{:S(2)}, u32[]{:S(2)}) collective-permute-start(bf16[256,1536]{1,0:T(8,128)(2,1)S(1)} %convolution_convert_fusion.5), channel_id=1, source_target_pairs={{8,16},{12,20},{16,8},{20,12},{9,17},{13,21},{17,9},{21,13},{10,18... | collective-permute-start | bytes 2359304 | tf_op jit(solution)/shard_map/ppermute | solution.py:40
  119.9 25.2 %collective-permute-start.22 = (bf16[192,1536]{1,0:T(8,128)(2,1)S(1)}, bf16[192,1536]{1,0:T(8,128)(2,1)S(1)}, u32[]{:S(2)}, u32[]{:S(2)}) collective-permute-start(bf16[192,1536]{1,0:T(8,128)(2,1)S(1)} %slice.245), channel_id=1, source_target_pairs={{0,8},{4,12},{8,0},{12,4},{16,24},{20,28},{24,16},{28,20},{1,9},{5... | collective-permute-start | bytes 1769480 | tf_op jit(solution)/shard_map/ppermute | solution.py:60
  120.6 42.5 %collective-permute-start.18 = (bf16[192,1536]{1,0:T(8,128)(2,1)S(1)}, bf16[192,1536]{1,0:T(8,128)(2,1)S(1)}, u32[]{:S(2)}, u32[]{:S(2)}) collective-permute-start(bf16[192,1536]{1,0:T(8,128)(2,1)S(1)} %convolution_convert_fusion.7), channel_id=1, source_target_pairs={{0,16},{4,20},{8,24},{12,28},{16,0},{20,4},{24,8},{28,12},{1,17},{... | collective-permute-start | bytes 1769480 | tf_op jit(solution)/shard_map/ppermute | solution.py:60
  124.1 50.7 %collective-permute-start.26 = (bf16[192,1536]{1,0:T(8,128)(2,1)S(1)}, bf16[192,1536]{1,0:T(8,128)(2,1)S(1)}, u32[]{:S(2)}, u32[]{:S(2)}) collective-permute-start(bf16[192,1536]{1,0:T(8,128)(2,1)S(1)} %convolution_convert_fusion.6), channel_id=1, source_target_pairs={{0,24},{4,28},{8,16},{12,20},{16,8},{20,12},{24,0},{28,4},{1,25},{... | collective-permute-start | bytes 1769480 | tf_op jit(solution)/shard_map/ppermute | solution.py:60
  145.2 33.7 %collective-permute-start.23 = (bf16[192,1536]{1,0:T(8,128)(2,1)S(1)}, bf16[192,1536]{1,0:T(8,128)(2,1)S(1)}, u32[]{:S(2)}, u32[]{:S(2)}) collective-permute-start(bf16[192,1536]{1,0:T(8,128)(2,1)S(1)} %pad_maximum_fusion.12), channel_id=1, source_target_pairs={{0,4},{4,0},{8,12},{12,8},{16,20},{20,16},{24,28},{28,24},{1,5},{5... | collective-permute-start | bytes 1769480 | tf_op jit(solution)/shard_map/ppermute | solution.py:56
  163.2 11.8 %collective-permute-start.19 = (bf16[96,1536]{1,0:T(8,128)(2,1)S(1)}, bf16[96,1536]{1,0:T(8,128)(2,1)S(1)}, u32[]{:S(2)}, u32[]{:S(2)}) collective-permute-start(bf16[96,1536]{1,0:T(8,128)(2,1)S(1)} %get-tuple-element.69), channel_id=1, source_target_pairs={{0,4},{4,0},{8,12},{12,8},{16,20},{20,16},{24,28},{28,24},{1,5},{5... | collective-permute-start | bytes 884744 | tf_op jit(solution)/shard_map/ppermute | solution.py:56
  174.9 4.0 %collective-permute-start.27 = (bf16[96,1536]{1,0:T(8,128)(2,1)S(1)}, bf16[96,1536]{1,0:T(8,128)(2,1)S(1)}, u32[]{:S(2)}, u32[]{:S(2)}) collective-permute-start(bf16[96,1536]{1,0:T(8,128)(2,1)S(1)} %get-tuple-element.63), channel_id=1, source_target_pairs={{0,4},{4,0},{8,12},{12,8},{16,20},{20,16},{24,28},{28,24},{1,5},{5... | collective-permute-start | bytes 884744 | tf_op jit(solution)/shard_map/ppermute | solution.py:56
  178.3 28.1 %collective-permute-start.20 = (bf16[96,1536]{1,0:T(8,128)(2,1)}, bf16[96,1536]{1,0:T(8,128)(2,1)}, u32[]{:S(2)}, u32[]{:S(2)}) collective-permute-start(bf16[96,1536]{1,0:T(8,128)(2,1)} %get-tuple-element.65), channel_id=1, source_target_pairs={{0,4},{4,0},{8,12},{12,8},{16,20},{20,16},{24,28},{28,24},{1,5},{5... | collective-permute-start | bytes 884744 | tf_op jit(solution)/shard_map/ppermute | solution.py:56
  189.7 20.2 %all-to-all-start = ((f32[8,24,128]{2,1,0:T(8,128)}), f32[8,24,128]{2,1,0:T(8,128)}, u32[]{:S(2)}, u32[]{:S(2)}) async-start(f32[8,24,128]{2,1,0:T(8,128)} %broadcast_in_dim.71), calls=%async_computation | async-start | bytes 196608 | tf_op jit(solution)/shard_map/all_to_all | solution.py:64
  198.9 13.3 %collective-permute-start.28 = (bf16[96,1536]{1,0:T(8,128)(2,1)}, bf16[96,1536]{1,0:T(8,128)(2,1)}, u32[]{:S(2)}, u32[]{:S(2)}) collective-permute-start(bf16[96,1536]{1,0:T(8,128)(2,1)} %get-tuple-element.57), channel_id=1, source_target_pairs={{0,4},{4,0},{8,12},{12,8},{16,20},{20,16},{24,28},{28,24},{1,5},{5... | collective-permute-start | bytes 884744 | tf_op jit(solution)/shard_map/ppermute | solution.py:56
  199.1 14.2 %collective-permute-start.24 = (bf16[192,1536]{1,0:T(8,128)(2,1)}, bf16[192,1536]{1,0:T(8,128)(2,1)}, u32[]{:S(2)}, u32[]{:S(2)}) collective-permute-start(bf16[192,1536]{1,0:T(8,128)(2,1)} %slice.250), channel_id=1, source_target_pairs={{0,4},{4,0},{8,12},{12,8},{16,20},{20,16},{24,28},{28,24},{1,5},{5... | collective-permute-start | bytes 1769480 | tf_op jit(solution)/shard_map/ppermute | solution.py:56
  207.5 16.4 %collective-permute-start.21 = (bf16[192,1536]{1,0:T(8,128)(2,1)S(1)}, bf16[192,1536]{1,0:T(8,128)(2,1)}, u32[]{:S(2)}, u32[]{:S(2)}) collective-permute-start(bf16[192,1536]{1,0:T(8,128)(2,1)S(1)} %pad_maximum_fusion.11), channel_id=1, source_target_pairs={{16,0},{20,4},{8,24},{12,28},{24,16},{28,20},{0,8},{4,12},{17,1},{... | collective-permute-start | bytes 1769480 | tf_op jit(solution)/shard_map/ppermute | solution.py:40
  214.5 21.9 %collective-permute-start.25 = (bf16[192,1536]{1,0:T(8,128)(2,1)S(1)}, bf16[192,1536]{1,0:T(8,128)(2,1)S(1)}, u32[]{:S(2)}, u32[]{:S(2)}) collective-permute-start(bf16[192,1536]{1,0:T(8,128)(2,1)S(1)} %pad_maximum_fusion.13), channel_id=1, source_target_pairs={{0,8},{4,12},{8,0},{12,4},{16,24},{20,28},{24,16},{28,20},{1,9},{5... | collective-permute-start | bytes 1769480 | tf_op jit(solution)/shard_map/ppermute | solution.py:60
  214.6 24.9 %collective-permute-start.30 = (bf16[192,1152]{1,0:T(8,128)(2,1)S(1)}, bf16[192,1152]{1,0:T(8,128)(2,1)S(1)}, u32[]{:S(2)}, u32[]{:S(2)}) collective-permute-start(bf16[192,1152]{1,0:T(8,128)(2,1)S(1)} %pad_maximum_fusion.16), channel_id=1, source_target_pairs={{0,24},{4,28},{24,0},{28,4},{1,25},{5,29},{25,1},{29,5},{2,26},{6,... | collective-permute-start | bytes 1327112 | tf_op jit(solution)/shard_map/ppermute | solution.py:40
  215.3 44.9 %collective-permute-start.29 = (bf16[192,384]{1,0:T(8,128)(2,1)S(1)}, bf16[192,384]{1,0:T(8,128)(2,1)S(1)}, u32[]{:S(2)}, u32[]{:S(2)}) collective-permute-start(bf16[192,384]{1,0:T(8,128)(2,1)S(1)} %get-tuple-element.53), channel_id=1, source_target_pairs={{0,24},{4,28},{24,0},{28,4},{1,25},{5,29},{25,1},{29,5},{2,26},{6,... | collective-permute-start | bytes 442376 | tf_op jit(solution)/shard_map/ppermute | solution.py:40
  225.9 30.3 %collective-permute-start.31 = (bf16[256,1152]{1,0:T(8,128)(2,1)S(1)}, bf16[256,1152]{1,0:T(8,128)(2,1)S(1)}, u32[]{:S(2)}, u32[]{:S(2)}) collective-permute-start(bf16[256,1152]{1,0:T(8,128)(2,1)S(1)} %pad_maximum_fusion.15), channel_id=1, source_target_pairs={{8,16},{12,20},{16,8},{20,12},{9,17},{13,21},{17,9},{21,13},{10,18... | collective-permute-start | bytes 1769480 | tf_op jit(solution)/shard_map/ppermute | solution.py:40
  229.2 31.4 %collective-permute-start.32 = (bf16[256,384]{1,0:T(8,128)(2,1)S(1)}, bf16[256,384]{1,0:T(8,128)(2,1)S(1)}, u32[]{:S(2)}, u32[]{:S(2)}) collective-permute-start(bf16[256,384]{1,0:T(8,128)(2,1)S(1)} %get-tuple-element.41), channel_id=1, source_target_pairs={{8,16},{12,20},{16,8},{20,12},{9,17},{13,21},{17,9},{21,13},{10,18... | collective-permute-start | bytes 589832 | tf_op jit(solution)/shard_map/ppermute | solution.py:40
  239.4 16.7 %copy-start.38 = (s32[192]{0:T(256)S(1)}, s32[192]{0:T(256)}, u32[]{:S(2)}) copy-start(s32[192]{0:T(256)} %copy-done.36) | copy-start | bytes 2308
  256.7 5.7 %collective-permute-start.33 = (bf16[256,384]{1,0:T(8,128)(2,1)S(1)}, bf16[256,384]{1,0:T(8,128)(2,1)S(1)}, u32[]{:S(2)}, u32[]{:S(2)}) collective-permute-start(bf16[256,384]{1,0:T(8,128)(2,1)S(1)} %get-tuple-element.49), channel_id=1, source_target_pairs={{0,1},{1,0},{2,3},{3,2},{4,5},{5,4},{6,7},{7,6},{8,9},{9,8},{10,11... | collective-permute-start | bytes 589832 | tf_op jit(solution)/shard_map/ppermute | solution.py:124
  258.3 6.9 %collective-permute-start.34 = (bf16[256,384]{1,0:T(8,128)(2,1)S(1)}, bf16[256,384]{1,0:T(8,128)(2,1)S(1)}, u32[]{:S(2)}, u32[]{:S(2)}) collective-permute-start(bf16[256,384]{1,0:T(8,128)(2,1)S(1)} %get-tuple-element.48), channel_id=1, source_target_pairs={{0,2},{1,3},{2,0},{3,1},{4,6},{5,7},{6,4},{7,5},{8,10},{9,11},{10,... | collective-permute-start | bytes 589832 | tf_op jit(solution)/shard_map/ppermute | solution.py:124
  259.8 6.6 %collective-permute-start.35 = (bf16[256,384]{1,0:T(8,128)(2,1)S(1)}, bf16[256,384]{1,0:T(8,128)(2,1)S(1)}, u32[]{:S(2)}, u32[]{:S(2)}) collective-permute-start(bf16[256,384]{1,0:T(8,128)(2,1)S(1)} %get-tuple-element.47), channel_id=1, source_target_pairs={{0,3},{1,2},{2,1},{3,0},{4,7},{5,6},{6,5},{7,4},{8,11},{9,10},{10,... | collective-permute-start | bytes 589832 | tf_op jit(solution)/shard_map/ppermute | solution.py:124
  (44 other events, 158.4 us)
